TPU v7x, 512 devices: a whole 4x8x8 slice. The times are simulated.
512 devices in a mesh: node: 16 (over z, core), dp: 32 (over x, y).
Axes of the slice: x: 4, y: 8, z: 8, core: 2. Of those that a mesh axis runs over, the one named last changes fastest.
Arguments:
- out_grad: bfloat16 [65536, 2560], P(('node', 'dp')), may hold values from -3 to 3
- gate_prob: bfloat16 [65536, 6], P(('node', 'dp')), may hold values from 0.019897461 to 0.5
- presel_nodes: int32 [65536, 3], P(('node', 'dp')), may hold values from 0 to 15, as said below
- route_expert: int32 [65536, 6], P(('node', 'dp')), may hold values from 0 to 29, as said below
- route_slot: int32 [65536, 6], P(('node', 'dp')), may hold values from -1 to 79, as said below
- gate_pre: bfloat16 [40960, 768], P(('node', 'dp')), may hold values from -6 to 6
- up_pre: bfloat16 [40960, 768], P(('node', 'dp')), may hold values from -6 to 6
- down_weight: bfloat16 [16, 768, 2560], P('node'), may hold values from -0.21875 to 0.21875
Outputs:
- grad_gate: bfloat16 [40960, 768], P(('node', 'dp'))
- grad_up: bfloat16 [40960, 768], P(('node', 'dp'))
- grad_down: bfloat16 [16, 768, 2560], P('node', 'dp')
- grad_prob: float32 [65536, 6], P(('node', 'dp'))
Inputs may be any that keep to these rules, and one draw needn't show every extreme that they name: `presel_nodes`: three different nodes for each token. `route_expert`: each token names 6 different numbers; number c stands for expert c % 10 of the node in column c // 10 of presel_nodes. `route_slot`: -1 wherever route_expert % 10 != 0. Call a route with route_expert % 10 == 0 and route_slot >= 0 active: active routes of the tokens of one data index to one node have distinct slots, and in every draw some such block uses all 80 slots; the tokens of one device have at most 16 active routes to one node, and in every draw some device has exactly 16.
All inputs are finite; a program needn't handle non-finite values.
Results may differ from a plain program's by a relative error of at most 0.015.
Values may be sent and summed in bfloat16 or wider, within the bound.
No kernel may reach another device: no remote copies, remote signals or barrier semaphores. Data moves between devices by JAX's collectives and lax.ppermute only.
A program may use at most 64 MiB of HBM per device.

v0:
```python
import jax
import jax.numpy as jnp
from jax import lax
from jax.sharding import Mesh
from jax.sharding import PartitionSpec as P

EXP_NODE = 10
TOPK = 6
SRC_CAP = 16
DP = ("dp_0", "dp_1")
NODE_DP = ("node", "dp_0", "dp_1")


def laid_out(tiles, dim):
    shape = list(tiles.shape[1:])
    shape[dim] *= tiles.shape[0]
    return jnp.moveaxis(tiles, 0, dim).reshape(shape)


def copy_for_each(value, axis):
    copies = jnp.broadcast_to(value, (lax.axis_size(axis), *value.shape))
    return lax.all_to_all(copies, axis, split_axis=0, concat_axis=0, tiled=True)


def gather_directly(value, axis, dim):
    return laid_out(copy_for_each(value, axis), dim)


def summed_rows(terms, axes):
    running = terms.astype(jnp.bfloat16)
    for axis in axes:
        running = lax.psum_scatter(running, axis, scatter_dimension=0, tiled=True)
    return running.astype(jnp.float32)


def shards(
    out_grad, gate_prob, presel_nodes, route_expert, route_slot, gate_pre, up_pre, down_weight
):
    tokens_here, features = out_grad.shape
    capacity = gate_pre.shape[0]
    n_node = lax.axis_size("node")
    active = (route_expert % EXP_NODE == 0) & (route_slot >= 0)
    target_node = jnp.take_along_axis(presel_nodes, route_expert // EXP_NODE, axis=1)
    slot_ids = jnp.arange(capacity, dtype=jnp.int32)
    flat_active = active.reshape(-1)
    flat_node = target_node.reshape(-1)
    node_numbering = jnp.arange(n_node, dtype=jnp.int32)
    onehot = (flat_node[:, None] == node_numbering[None, :]) & flat_active[:, None]
    running_rank = jnp.cumsum(onehot.astype(jnp.int32), axis=0) - 1
    sorted_position = jnp.sum(jnp.where(onehot, running_rank, 0), axis=1)
    position = jnp.where(flat_active, flat_node * SRC_CAP + sorted_position, -1)
    positions = jnp.arange(n_node * SRC_CAP, dtype=jnp.int32)
    matched = position[None, :] == positions[:, None]
    token_pick = jnp.any(matched.reshape(n_node * SRC_CAP, tokens_here, TOPK), axis=2).astype(
        jnp.bfloat16
    )
    send_rows = jnp.dot(token_pick, out_grad, preferred_element_type=jnp.float32).astype(
        jnp.bfloat16
    )
    send_slot = jnp.sum(jnp.where(matched, route_slot.reshape(-1)[None, :] + 1, 0), axis=1) - 1
    send_prob = jnp.sum(
        jnp.where(matched, gate_prob.reshape(-1).astype(jnp.float32)[None, :], 0.0), axis=1
    ).astype(jnp.bfloat16)
    recv_rows, recv_slot, recv_prob = (
        lax.all_to_all(send_rows, "node", split_axis=0, concat_axis=0, tiled=True),
        lax.all_to_all(send_slot, "node", split_axis=0, concat_axis=0, tiled=True),
        lax.all_to_all(send_prob, "node", split_axis=0, concat_axis=0, tiled=True),
    )
    landing = recv_slot[None, :] == slot_ids[:, None]
    slot_dy = jnp.dot(landing.astype(jnp.bfloat16), recv_rows, preferred_element_type=jnp.float32)
    slot_p = jnp.sum(jnp.where(landing, recv_prob.astype(jnp.float32)[None, :], 0.0), axis=1)
    weight = down_weight[0]
    gate_rows = gate_pre.astype(jnp.float32)
    up_rows = up_pre.astype(jnp.float32)
    sigmoid_gate = jax.nn.sigmoid(gate_rows)
    activated = gate_rows * sigmoid_gate
    hidden = (activated * up_rows).astype(jnp.bfloat16)
    scaled_scores = (slot_p[:, None] * slot_dy).astype(jnp.bfloat16)
    d_hidden = lax.dot_general(
        scaled_scores, weight, (((1,), (1,)), ((), ())), preferred_element_type=jnp.float32
    )
    grad_gate = (
        d_hidden * up_rows * sigmoid_gate * (1.0 + gate_rows * (1.0 - sigmoid_gate))
    ).astype(jnp.bfloat16)
    grad_up = (d_hidden * activated).astype(jnp.bfloat16)
    slot_out = jnp.dot(hidden, weight, preferred_element_type=jnp.float32)
    slot_grad_p = jnp.sum(slot_dy * slot_out, axis=1)
    all_grad_p = gather_directly(slot_grad_p, "node", 0)
    lookup = jnp.clip(target_node * capacity + route_slot, 0, n_node * capacity - 1)
    grad_prob = jnp.where(active, all_grad_p[lookup], jnp.float32(0.0))
    grad_down = summed_rows(
        lax.dot_general(
            hidden, scaled_scores, (((0,), (0,)), ((), ())), preferred_element_type=jnp.float32
        ),
        DP,
    ).astype(jnp.bfloat16)[None]
    return (grad_gate, grad_up, grad_down, grad_prob)


def solution(mesh):
    finer = Mesh(mesh.devices.reshape(mesh.shape["node"], 4, 8), ("node", "dp_0", "dp_1"))
    in_specs = (
        P(NODE_DP, None),
        P(NODE_DP, None),
        P(NODE_DP, None),
        P(NODE_DP, None),
        P(NODE_DP, None),
        P(NODE_DP, None),
        P(NODE_DP, None),
        P("node", None, None),
    )
    out_specs = (P(NODE_DP, None), P(NODE_DP, None), P("node", DP, None), P(NODE_DP, None))
    return jax.shard_map(
        shards, mesh=finer, in_specs=in_specs, out_specs=out_specs, check_vma=False
    )
```

profile of v0, /device:TPU:2, one launch (start us, length us, event | category | flops | bytes accessed | tf_op | source)
XLA Modules:
  0.0 188.3 jit_solution(6632216446034441256)
XLA Ops:
  7.2 0.8 bitcast_or_fusion
  8.0 0.7 fusion.28
  9.4 6.3 %gather_fusion.1 = s32[768]{0:T(1024)S(1)} fusion(s32[128,3]{0,1:T(4,128)S(1)} %copy-done.1, s32[768]{0:T(1024)S(1)} %reshape.170), kind=kCustom, calls=%fused_computation.1 | custom fusion | bytes 12288 | tf_op jit(solution)/shard_map/jit(take_along_axis)/gather | solution.py:43
  16.5 1.7 reduce-window.6
  19.0 0.7 convert_element_type.83
  19.7 10.4 %all-to-all-start.1 = ((bf16[16,16,1]{1,2,0:T(2,128)(2,1)}), bf16[16,16,1]{1,2,0:T(2,128)(2,1)S(1)}, u32[]{:S(2)}, u32[]{:S(2)}) async-start(bf16[16,16,1]{1,2,0:T(2,128)(2,1)} %convert_element_type.83), calls=%async_computation.1 | async-start | bytes 16384 | tf_op jit(solution)/shard_map/all_to_all | solution.py:67
  30.9 0.7 sub.28
  31.6 6.1 %all-to-all-done.1 = bf16[16,16,1]{1,2,0:T(2,128)(2,1)S(1)} async-done(((bf16[16,16,1]{1,2,0:T(2,128)(2,1)}), bf16[16,16,1]{1,2,0:T(2,128)(2,1)S(1)}, u32[]{:S(2)}, u32[]{:S(2)}) %all-to-all-start.1) | async-done | bytes 544 | tf_op jit(solution)/shard_map/all_to_all | solution.py:67
  37.7 3.5 %all-to-all-start = ((s32[16,16,1]{1,2,0:T(1,128)}), s32[16,16,1]{1,2,0:T(1,128)S(1)}, u32[]{:S(2)}, u32[]{:S(2)}) async-start(s32[16,16,1]{1,2,0:T(1,128)} %bitcast.2), calls=%async_computation | async-start | bytes 16384 | tf_op jit(solution)/shard_map/all_to_all | solution.py:66
  41.1 1.6 convolution_convert_fusion.1
  42.7 5.9 %all-to-all-done = s32[16,16,1]{1,2,0:T(1,128)S(1)} async-done(((s32[16,16,1]{1,2,0:T(1,128)}), s32[16,16,1]{1,2,0:T(1,128)S(1)}, u32[]{:S(2)}, u32[]{:S(2)}) %all-to-all-start) | async-done | bytes 1056 | tf_op jit(solution)/shard_map/all_to_all | solution.py:66
  48.6 3.7 %all-to-all-start.2 = ((bf16[16,16,2560]{2,1,0:T(8,128)(2,1)}), bf16[16,16,2560]{2,1,0:T(8,128)(2,1)S(1)}, u32[]{:S(2)}, u32[]{:S(2)}) async-start(bf16[16,16,2560]{2,1,0:T(8,128)(2,1)} %bitcast.3), calls=%async_computation.2 | async-start | bytes 2621440 | tf_op jit(solution)/shard_map/all_to_all | solution.py:65
  53.0 0.7 reduce.12
  53.9 30.5 %all-to-all-done.2 = bf16[16,16,2560]{2,1,0:T(8,128)(2,1)S(1)} async-done(((bf16[16,16,2560]{2,1,0:T(8,128)(2,1)}), bf16[16,16,2560]{2,1,0:T(8,128)(2,1)S(1)}, u32[]{:S(2)}, u32[]{:S(2)}) %all-to-all-start.2) | async-done | bytes 1310752 | tf_op jit(solution)/shard_map/all_to_all | solution.py:65
  84.8 3.1 %convolution_convert_fusion = bf16[768,2560]{1,0:T(8,128)(2,1)} fusion(f32[80,2560]{1,0:T(8,128)S(1)} %fusion.19, f32[80]{0:T(128)S(1)} %select_reduce_fusion.2, bf16[80,768]{1,0:T(8,128)(2,1)S(1)} %copy-done.3, bf16[80,768]{1,0:T(8,128)(2,1)S(1)} %copy-done.2), kind=kOutput, calls=%fused_computation.2 | convolution fusion | flops 317440000 | bytes 4997440 | tf_op jit(solution)/shard_map/dot_general | solution.py:92
  88.0 48.0 %reduce-scatter.3.cloned.1.call-done = bf16[192,2560]{1,0:T(8,128)(2,1)} async-done(((bf16[768,2560]{1,0:T(8,128)(2,1)}), bf16[192,2560]{1,0:T(8,128)(2,1)}) %reduce-scatter.3.cloned.1.call-update) | async-done | bytes 983056 | tf_op jit(solution)/shard_map/reduce_scatter | solution.py:32
  136.2 3.0 %fusion.7 = f32[80]{0:T(128)S(1)} fusion(f32[80,2560]{1,0:T(8,128)S(1)} %fusion.19, bf16[1,768,2560]{2,1,0:T(8,128)(2,1)} %param.15, bf16[80,768]{1,0:T(8,128)(2,1)S(1)} %copy-done.3, bf16[80,768]{1,0:T(8,128)(2,1)S(1)} %copy-done.2), kind=kOutput, calls=%fused_computation.9 | convolution fusion | flops 315473856 | bytes 4997440 | tf_op jit(solution)/shard_map/dot_general | solution.py:86
  139.9 7.5 %all-to-all-start.3 = ((f32[16,1,80]{2,1,0:T(1,128)}), f32[16,1,80]{2,1,0:T(1,128)S(1)}, u32[]{:S(2)}, u32[]{:S(2)}) async-start(f32[16,1,80]{2,1,0:T(1,128)} %broadcast_in_dim.79), calls=%async_computation.5 | async-start | bytes 16384 | tf_op jit(solution)/shard_map/all_to_all | solution.py:22
  147.4 4.1 %multiply_convert_fusion.1 = (bf16[80,768]{1,0:T(8,128)(2,1)}, bf16[80,768]{1,0:T(8,128)(2,1)}) fusion(bf16[80,768]{1,0:T(8,128)(2,1)S(1)} %copy-done.2, bf16[80,768]{1,0:T(8,128)(2,1)S(1)} %copy-done.3, bf16[1,768,2560]{2,1,0:T(8,128)(2,1)} %param.15, f32[80,2560]{1,0:T(8,128)S(1)} %fusion.19, f32[80]{0:T(128)S(1)} %select_reduce_fusion.2), kind=kOutput, calls=%fused_computation.29 | convolution fusion | flops 315904000 | bytes 5243200 | tf_op jit(solution)/shard_map/dot_general | solution.py:79
  151.5 3.4 %all-to-all-done.3 = f32[16,1,80]{2,1,0:T(1,128)S(1)} async-done(((f32[16,1,80]{2,1,0:T(1,128)}), f32[16,1,80]{2,1,0:T(1,128)S(1)}, u32[]{:S(2)}, u32[]{:S(2)}) %all-to-all-start.3) | async-done | bytes 5152 | tf_op jit(solution)/shard_map/all_to_all | solution.py:22
  155.5 0.7 reduce.13
  156.2 4.5 %gather_fusion = f32[768]{0:T(1024)S(1)} fusion(f32[1280]{0:T(1024)S(1)} %reshape.159, s32[1024]{0:T(1024)S(1)} %pad_clamp_fusion), kind=kCustom, calls=%fused_computation | custom fusion | bytes 9216 | tf_op jit(solution)/shard_map/gather | solution.py:90
  160.9 0.6 broadcast_select_fusion
  161.5 20.0 %reduce-scatter.5.cloned.1.call-done = bf16[24,2560]{1,0:T(8,128)(2,1)} async-done(((bf16[192,2560]{1,0:T(8,128)(2,1)}), bf16[24,2560]{1,0:T(8,128)(2,1)}) %reduce-scatter.5.cloned.1.call-update) | async-done | bytes 122896 | tf_op jit(solution)/shard_map/reduce_scatter | solution.py:32
  (59 shorter events, 5.8 us)
Async XLA Ops:
  7.2 34.0 %copy-start = (bf16[128,2560]{1,0:T(8,128)(2,1)S(1)}, bf16[128,2560]{1,0:T(8,128)(2,1)}, u32[]{:S(2)}) copy-start(bf16[128,2560]{1,0:T(8,128)(2,1)} %param.8) | copy-start | bytes 1966084
  7.2 2.2 %copy-start.1 = (s32[128,3]{0,1:T(4,128)S(1)}, s32[128,3]{0,1:T(4,128)}, u32[]{:S(2)}) copy-start(s32[128,3]{0,1:T(4,128)} %param.10) | copy-start | bytes 4612
  9.4 6.6 %copy-start.4 = (s32[128,6]{0,1:T(8,128)S(1)}, s32[128,6]{0,1:T(8,128)}, u32[]{:S(2)}) copy-start(s32[128,6]{0,1:T(8,128)} %param.11) | copy-start | bytes 9220
  9.4 6.6 %copy-start.5 = (s32[128,6]{0,1:T(8,128)S(1)}, s32[128,6]{0,1:T(8,128)}, u32[]{:S(2)}) copy-start(s32[128,6]{0,1:T(8,128)} %param.12) | copy-start | bytes 9220
  9.4 9.2 %copy-start.6 = (bf16[128,6]{0,1:T(8,128)(2,1)S(1)}, bf16[128,6]{0,1:T(8,128)(2,1)}, u32[]{:S(2)}) copy-start(bf16[128,6]{0,1:T(8,128)(2,1)} %param.9) | copy-start | bytes 4612
  16.0 68.7 %copy-start.2 = (bf16[80,768]{1,0:T(8,128)(2,1)S(1)}, bf16[80,768]{1,0:T(8,128)(2,1)}, u32[]{:S(2)}) copy-start(bf16[80,768]{1,0:T(8,128)(2,1)} %param.13) | copy-start | bytes 368644
  16.0 68.7 %copy-start.3 = (bf16[80,768]{1,0:T(8,128)(2,1)S(1)}, bf16[80,768]{1,0:T(8,128)(2,1)}, u32[]{:S(2)}) copy-start(bf16[80,768]{1,0:T(8,128)(2,1)} %param.14) | copy-start | bytes 368644
  19.7 18.0 %all-to-all-start.1 = ((bf16[16,16,1]{1,2,0:T(2,128)(2,1)}), bf16[16,16,1]{1,2,0:T(2,128)(2,1)S(1)}, u32[]{:S(2)}, u32[]{:S(2)}) async-start(bf16[16,16,1]{1,2,0:T(2,128)(2,1)} %convert_element_type.83), calls=%async_computation.1 | async-start | bytes 16384 | tf_op jit(solution)/shard_map/all_to_all | solution.py:67
  37.7 10.9 %all-to-all-start = ((s32[16,16,1]{1,2,0:T(1,128)}), s32[16,16,1]{1,2,0:T(1,128)S(1)}, u32[]{:S(2)}, u32[]{:S(2)}) async-start(s32[16,16,1]{1,2,0:T(1,128)} %bitcast.2), calls=%async_computation | async-start | bytes 16384 | tf_op jit(solution)/shard_map/all_to_all | solution.py:66
  48.6 35.8 %all-to-all-start.2 = ((bf16[16,16,2560]{2,1,0:T(8,128)(2,1)}), bf16[16,16,2560]{2,1,0:T(8,128)(2,1)S(1)}, u32[]{:S(2)}, u32[]{:S(2)}) async-start(bf16[16,16,2560]{2,1,0:T(8,128)(2,1)} %bitcast.3), calls=%async_computation.2 | async-start | bytes 2621440 | tf_op jit(solution)/shard_map/all_to_all | solution.py:65
  52.3 83.7 %reduce-scatter.3.cloned.1.call-start = ((), (), s32[]{:S(2)}) async-start(), calls=%async_computation.6 | async-start | bytes 4915200 | tf_op jit(solution)/shard_map/reduce_scatter | solution.py:32
  87.9 93.6 %reduce-scatter.5.cloned.1.call-start = ((), (), s32[]{:S(2)}) async-start(), calls=%async_computation.7 | async-start | bytes 1105920 | tf_op jit(solution)/shard_map/reduce_scatter | solution.py:32
  139.9 15.1 %all-to-all-start.3 = ((f32[16,1,80]{2,1,0:T(1,128)}), f32[16,1,80]{2,1,0:T(1,128)S(1)}, u32[]{:S(2)}, u32[]{:S(2)}) async-start(f32[16,1,80]{2,1,0:T(1,128)} %broadcast_in_dim.79), calls=%async_computation.5 | async-start | bytes 16384 | tf_op jit(solution)/shard_map/all_to_all | solution.py:22
Sparse Core Ops, SparseCore 0:
  88.0 47.8 reduce-scatter.2
  139.4 42.0 reduce-scatter.4
where the time goes:
time: 189 us; the launch traced here: 188 us
  waiting for transfers between devices  114 us (60%)
  starting transfers between devices  25.1 us (13%)
  local copies, waits for them, and re-layouts  16.7 us (9%)
  between operations  14.3 us (8%)
  matrix products  12.2 us (6%)
  other arithmetic  5.93 us (3%)
    reduce_scatter x2, waiting for transfers between devices, summed_rows(): running = lax.psum_scatter(running, axis, scatter_dimension=0, tiled=True)  68 us
    all_to_all x1, waiting for transfers between devices, shards(): lax.all_to_all(send_rows, 'node', split_axis=0, concat_axis=0, tiled=True)  30.5 us
    all_to_all x1, starting transfers between devices, shards(): lax.all_to_all(send_prob, 'node', split_axis=0, concat_axis=0, tiled=True)  10.4 us
    all_to_all x1, starting transfers between devices, copy_for_each(): return lax.all_to_all(copies, axis, split_axis=0, concat_axis=0, tiled=True)  7.47 us
    gather x5, local copies, waits for them, and re-layouts, shards(): jnp.take_along_axis(presel_nodes, route_expert // EXP_NODE, axis=1)  6.78 us
    all_to_all x1, waiting for transfers between devices, shards(): lax.all_to_all(send_prob, 'node', split_axis=0, concat_axis=0, tiled=True)  6.08 us
    all_to_all x1, waiting for transfers between devices, shards(): lax.all_to_all(send_slot, 'node', split_axis=0, concat_axis=0, tiled=True)  5.9 us
    gather x3, local copies, waits for them, and re-layouts, shards(): grad_prob = jnp.where(active, all_grad_p[lookup], jnp.float32(0.0))  4.64 us
  transfers between devices with their start and end apart: 6, of which 6 were waited for; matrix products, arithmetic and copies ran while one was open for 10% of the time, Pallas kernels for 0%

commit v1 on v0

v1 whole, which is shorter than its diff:
```python
import jax
import jax.numpy as jnp
from jax import lax
from jax.experimental import pallas as pl
from jax.experimental.pallas import tpu as pltpu
from jax.sharding import Mesh
from jax.sharding import PartitionSpec as P

EXP_NODE = 10
PRESEL = 3
SRC_CAP = 16
LANES = 128
NODE_DP = ("node", "dp_0", "dp_1")
F32 = jnp.float32
BF16 = jnp.bfloat16


def columns_of_routes(expert, slot, value):
    rows = []
    for c in range(PRESEL):
        named = (expert == c * EXP_NODE) & (slot >= 0)
        rows.append(jnp.sum(jnp.where(named, value, 0), axis=0, keepdims=True))
    return rows


def route_kernel(og_ref, prob_ref, presel_ref, expert_ref, slot_ref, send_ref):
    tokens, features = og_ref.shape
    n_node = send_ref.shape[0] // SRC_CAP
    expert, slot, presel = expert_ref[...], slot_ref[...], presel_ref[...]
    slots = columns_of_routes(expert, slot, slot + 1)
    probs = columns_of_routes(expert, slot, prob_ref[...].astype(F32))
    node_ids = lax.broadcasted_iota(jnp.int32, (n_node, tokens), 0)
    slot_to = jnp.zeros((n_node, tokens), F32)
    prob_to = jnp.zeros((n_node, tokens), F32)
    for c in range(PRESEL):
        here = presel[c : c + 1] == node_ids
        slot_to += jnp.where(here, slots[c].astype(F32), 0.0)
        prob_to += jnp.where(here, probs[c], 0.0)
    sent = slot_to > 0.0
    before = lax.broadcasted_iota(jnp.int32, (tokens, tokens), 0) < lax.broadcasted_iota(
        jnp.int32, (tokens, tokens), 1
    )
    rank = jnp.dot(
        jnp.where(sent, 1.0, 0.0).astype(BF16),
        jnp.where(before, 1.0, 0.0).astype(BF16),
        preferred_element_type=F32,
    )
    rank = jnp.where(sent, rank, -1.0)
    place = lax.broadcasted_iota(jnp.int32, (n_node, SRC_CAP, tokens), 1).astype(F32)
    picked = rank[:, None, :] == place
    rows = n_node * SRC_CAP
    slot_rows = jnp.sum(jnp.where(picked, slot_to[:, None, :], 0.0), axis=2, keepdims=True)
    prob_rows = jnp.sum(jnp.where(picked, prob_to[:, None, :], 0.0), axis=2, keepdims=True)
    lane = lax.broadcasted_iota(jnp.int32, (n_node, SRC_CAP, LANES), 2)
    info = jnp.where(lane == 0, slot_rows, jnp.where(lane == 1, prob_rows, 0.0))
    send_ref[:, features:] = info.reshape(rows, LANES).astype(BF16)
    pick = jnp.where(picked, 1.0, 0.0).reshape(rows, tokens).astype(BF16)
    send_ref[:, :features] = jnp.dot(pick, og_ref[...], preferred_element_type=F32).astype(BF16)


def land_kernel(recv_ref, out_ref, scaled_ref, parts_ref, grad_p_ref):
    capacity, features = scaled_ref.shape
    n_parts, _, width = parts_ref.shape
    recv = recv_ref[...]
    slot = recv_ref[:, features : features + 1].astype(F32)
    lane = lax.broadcasted_iota(jnp.int32, (recv.shape[0], LANES), 1).astype(F32)
    landing = jnp.where(slot == lane + 1.0, 1.0, 0.0).astype(BF16)
    landed = lax.dot_general(
        landing, recv, (((0,), (0,)), ((), ())), preferred_element_type=F32
    )[:capacity]
    dy = landed[:, :features]
    p = landed[:, features + 1 : features + 2]
    scaled = (p * dy).astype(BF16)
    scaled_ref[...] = scaled
    for k in range(n_parts):
        parts_ref[k] = scaled[:, k * width : (k + 1) * width]
    grad_p = jnp.sum(dy * out_ref[...], axis=1, keepdims=True)
    row = lax.broadcasted_iota(jnp.int32, (capacity, LANES), 0)
    column = lax.broadcasted_iota(jnp.int32, (capacity, LANES), 1)
    grad_p_ref[...] = jnp.sum(jnp.where(row == column, grad_p, 0.0), axis=0, keepdims=True)


def partial_kernel(me_ref, scaled_ref, *refs):
    *hidden_refs, out_ref = refs
    n = len(hidden_refs)
    total = None
    for k, hidden_ref in enumerate(hidden_refs):
        block = lax.rem(me_ref[0] - k + n, n)
        term = lax.dot_general(
            hidden_ref[...],
            scaled_ref[block],
            (((0,), (0,)), ((), ())),
            preferred_element_type=F32,
        )
        total = term if total is None else total + term
    out_ref[...] = total.astype(BF16).reshape(out_ref.shape)


def sum_kernel(terms_ref, out_ref):
    n, _, width = terms_ref.shape
    n_parts = out_ref.shape[1] // width
    each = n // n_parts
    for k in range(n_parts):
        total = terms_ref[k * each].astype(F32)
        for j in range(1, each):
            total += terms_ref[k * each + j].astype(F32)
        out_ref[:, k * width : (k + 1) * width] = total.astype(BF16)


def return_kernel(me_ref, grad_p_ref, presel_ref, expert_ref, slot_ref, out_ref):
    n_node = grad_p_ref.shape[0]
    tokens = presel_ref.shape[1]
    expert, slot, presel = expert_ref[...], slot_ref[...], presel_ref[...]
    slots = columns_of_routes(expert, slot, slot + 1)
    node_ids = lax.broadcasted_iota(jnp.int32, (n_node, tokens), 0)
    slot_ids = lax.broadcasted_iota(jnp.int32, (LANES, tokens), 0)
    result = jnp.zeros(out_ref.shape, F32)
    for c in range(PRESEL):
        here = (presel[c : c + 1] ^ me_ref[0]) == node_ids
        by_slot = lax.dot_general(
            grad_p_ref[...],
            jnp.where(here, 1.0, 0.0),
            (((0,), (0,)), ((), ())),
            preferred_element_type=F32,
            precision=lax.Precision.HIGHEST,
        )
        value = jnp.sum(jnp.where(slot_ids + 1 == slots[c], by_slot, 0.0), axis=0, keepdims=True)
        result += jnp.where((expert == c * EXP_NODE) & (slot >= 0), value, 0.0)
    out_ref[...] = result


VMEM = pl.BlockSpec(memory_space=pltpu.VMEM)
SMEM = pl.BlockSpec(memory_space=pltpu.SMEM)


def call(kernel, out_shape, in_specs):
    many = isinstance(out_shape, (tuple, list))
    return pl.pallas_call(
        kernel,
        out_shape=out_shape,
        in_specs=in_specs,
        out_specs=[VMEM] * len(out_shape) if many else VMEM,
        compiler_params=pltpu.CompilerParams(vmem_limit_bytes=12 * 1024 * 1024),
    )


def exchange(value, axes):
    return lax.all_to_all(value, axes, split_axis=0, concat_axis=0, tiled=True)


def step_of(
    out_grad, gate_prob, presel_nodes, route_expert, route_slot, gate_pre, up_pre, down_weight
):
    _, features = out_grad.shape
    capacity, units = gate_pre.shape
    n_node, n_0, n_1 = (lax.axis_size(a) for a in NODE_DP)
    width = features // n_0
    share = units // (n_0 * n_1)
    shape = jax.ShapeDtypeStruct
    presel, expert, slot = presel_nodes.T, route_expert.T, route_slot.T

    send = call(
        route_kernel, shape((n_node * SRC_CAP, features + LANES), BF16), [VMEM] * 5
    )(out_grad, gate_prob.T, presel, expert, slot)
    recv = exchange(send.reshape(n_node, SRC_CAP, features + LANES), "node")
    recv = recv.reshape(n_node * SRC_CAP, features + LANES)

    weight = down_weight[0]
    gate_rows = gate_pre.astype(F32)
    up_rows = up_pre.astype(F32)
    sigmoid_gate = jax.nn.sigmoid(gate_rows)
    activated = gate_rows * sigmoid_gate
    hidden = (activated * up_rows).astype(BF16)
    hiddens = [hidden]
    for k in range(1, n_0):
        hiddens.append(
            lax.ppermute(hidden, "dp_0", [(i, (i + k) % n_0) for i in range(n_0)])
        )
    slot_out = jnp.dot(hidden, weight, preferred_element_type=F32)

    scaled, parts, grad_p = call(
        land_kernel,
        [
            shape((capacity, features), BF16),
            shape((n_0, capacity, width), BF16),
            shape((1, LANES), F32),
        ],
        [VMEM] * 2,
    )(recv, slot_out)
    parts = exchange(parts, "dp_0")

    d_hidden = lax.dot_general(
        scaled, weight, (((1,), (1,)), ((), ())), preferred_element_type=F32
    )
    grad_gate = (
        d_hidden * up_rows * sigmoid_gate * (1.0 + gate_rows * (1.0 - sigmoid_gate))
    ).astype(BF16)
    grad_up = (d_hidden * activated).astype(BF16)

    partial = call(
        partial_kernel, shape((n_0 * n_1, share, width), BF16), [SMEM] + [VMEM] * (1 + n_0)
    )(lax.axis_index("dp_0")[None], parts, *hiddens)
    terms = exchange(partial, ("dp_0", "dp_1"))
    grad_down = call(sum_kernel, shape((share, features), BF16), [VMEM])(terms)[None]

    step = 1
    while step < n_node:
        other = lax.ppermute(grad_p, "node", [(i, i ^ step) for i in range(n_node)])
        grad_p = jnp.concatenate([grad_p, other])
        step *= 2
    grad_prob = call(
        return_kernel, shape(route_expert.shape[::-1], F32), [SMEM] + [VMEM] * 4
    )(lax.axis_index("node")[None], grad_p, presel, expert, slot).T
    return (grad_gate, grad_up, grad_down, grad_prob)


def solution(mesh):
    finer = Mesh(mesh.devices.reshape(mesh.shape["node"], 4, 8), NODE_DP)
    in_specs = (P(NODE_DP, None),) * 7 + (P("node", None, None),)
    out_specs = (
        P(NODE_DP, None),
        P(NODE_DP, None),
        P("node", ("dp_0", "dp_1"), None),
        P(NODE_DP, None),
    )
    return jax.shard_map(
        step_of, mesh=finer, in_specs=in_specs, out_specs=out_specs, check_vma=False
    )
```

time: 189 us -> 112 us (0.59)
  the two profiles are of different devices: /device:TPU:2 before, /device:TPU:8 now
where the time goes in v1:
time: 112 us; the launch traced here: 111 us
  starting transfers between devices  48.2 us (43%)
  waiting for transfers between devices  44.4 us (40%)
  matrix products  7.05 us (6%)
  Pallas kernels  6.99 us (6%)
  local copies, waits for them, and re-layouts  3.86 us (3%)
    all_to_all x3, waiting for transfers between devices, exchange(): return lax.all_to_all(value, axes, split_axis=0, concat_axis=0, tiled=True)  32 us
    all_to_all x3, starting transfers between devices, exchange(): return lax.all_to_all(value, axes, split_axis=0, concat_axis=0, tiled=True)  24.5 us
    ppermute x3, starting transfers between devices, step_of(): lax.ppermute(hidden, 'dp_0', [(i, (i + k) % n_0) for i in range(n_0)])  11.9 us
    ppermute x4, starting transfers between devices, step_of(): other = lax.ppermute(grad_p, 'node', [(i, i ^ step) for i in range(n_node)])  11.8 us
    ppermute x4, waiting for transfers between devices, step_of(): other = lax.ppermute(grad_p, 'node', [(i, i ^ step) for i in range(n_node)])  8.35 us
    dot_general x1, matrix products, step_of(): lax.dot_general(scaled, weight, (((1,), (1,)), ((), ())), preferred_eleme...  4.14 us
    ppermute x3, waiting for transfers between devices, step_of(): lax.ppermute(hidden, 'dp_0', [(i, (i + k) % n_0) for i in range(n_0)])  4.04 us
    unnamed x20, local copies, waits for them, and re-layouts  3.83 us
  transfers between devices with their start and end apart: 10, of which 8 were waited for; matrix products, arithmetic and copies ran while one was open for 6% of the time, Pallas kernels for 1%

profile of v1, /device:TPU:8, one launch (start us, length us, event | category | flops | bytes accessed | tf_op | source)
XLA Modules:
  0.0 111.3 jit_solution(11113224462872006657)
XLA Ops:
  0.6 1.1 copy-done
  4.5 1.7 %shard_map.111 = bf16[256,2688]{1,0:T(8,128)(2,1)} custom-call(bf16[128,2560]{1,0:T(8,128)(2,1)S(1)} %copy-done, bf16[6,128]{1,0:T(8,128)(2,1)S(1)} %bitcast.26, s32[3,128]{1,0:T(4,128)S(1)} %bitcast.24, s32[6,128]{1,0:T(8,128)S(1)} %bitcast.20, s32[6,128]{1,0:T(8,128)S(1)} %bitcast.22), custom_call_target="tpu_custom_call" | custom-call | tf_op jit(solution)/shard_map/pallas_call | solution.py:162
  6.2 10.4 %all-to-all-start = ((bf16[16,16,2688]{2,1,0:T(8,128)(2,1)}), bf16[16,16,2688]{2,1,0:T(8,128)(2,1)S(1)}, u32[]{:S(2)}, u32[]{:S(2)}) async-start(bf16[16,16,2688]{2,1,0:T(8,128)(2,1)} %bitcast.4), calls=%async_computation | async-start | bytes 2752512 | tf_op jit(solution)/shard_map/all_to_all | solution.py:148
  16.7 2.9 %fusion.2.out_ref = f32[80,2560]{1,0:T(8,128)S(1)} fusion(bf16[80,768]{1,0:T(8,128)(2,1)S(1)} %fusion.4.refs_0_, bf16[1,768,2560]{2,1,0:T(8,128)(2,1)} %param.15), kind=kOutput, calls=%fused_computation.2 | convolution fusion | flops 314572800 | bytes 4874240 | tf_op jit(solution)/shard_map/dot_general | solution.py:179
  19.6 30.5 %all-to-all-done = bf16[16,16,2688]{2,1,0:T(8,128)(2,1)S(1)} async-done(((bf16[16,16,2688]{2,1,0:T(8,128)(2,1)}), bf16[16,16,2688]{2,1,0:T(8,128)(2,1)S(1)}, u32[]{:S(2)}, u32[]{:S(2)}) %all-to-all-start) | async-done | bytes 1376288 | tf_op jit(solution)/shard_map/all_to_all | solution.py:148
  50.2 1.3 %shard_map.112 = (bf16[80,2560]{1,0:T(8,128)(2,1)S(1)}, bf16[4,80,640]{2,1,0:T(8,128)(2,1)}, f32[1,128]{1,0:T(1,128)S(1)}) custom-call(bf16[256,2688]{1,0:T(8,128)(2,1)S(1)} %bitcast.19, f32[80,2560]{1,0:T(8,128)S(1)} %fusion.2.out_ref), custom_call_target="tpu_custom_call" | custom-call | tf_op jit(solution)/shard_map/pallas_call | solution.py:181
  51.5 4.3 %all-to-all-start.1 = ((bf16[4,80,640]{2,1,0:T(8,128)(2,1)}), bf16[4,80,640]{2,1,0:T(8,128)(2,1)S(1)}, u32[]{:S(2)}, u32[]{:S(2)}) async-start(bf16[4,80,640]{2,1,0:T(8,128)(2,1)} %get-tuple-element.8), calls=%async_computation.1 | async-start | bytes 819200 | tf_op jit(solution)/shard_map/all_to_all | solution.py:148
  55.8 3.9 %collective-permute-start = (bf16[80,768]{1,0:T(8,128)(2,1)S(1)}, bf16[80,768]{1,0:T(8,128)(2,1)S(1)}, u32[]{:S(2)}, u32[]{:S(2)}) collective-permute-start(bf16[80,768]{1,0:T(8,128)(2,1)S(1)} %fusion.4.refs_0_), channel_id=1, source_target_pairs={{0,8},{8,16},{16,24},{24,0},{1,9},{9,17},{17,25},{25,1},{2,10},{10... | collective-permute-start | bytes 368648 | tf_op jit(solution)/shard_map/ppermute | solution.py:177
  59.7 4.6 %collective-permute-start.1 = (bf16[80,768]{1,0:T(8,128)(2,1)S(1)}, bf16[80,768]{1,0:T(8,128)(2,1)S(1)}, u32[]{:S(2)}, u32[]{:S(2)}) collective-permute-start(bf16[80,768]{1,0:T(8,128)(2,1)S(1)} %fusion.4.refs_0_), channel_id=1, source_target_pairs={{0,16},{8,24},{16,0},{24,8},{1,17},{9,25},{17,1},{25,9},{2,18},{10... | collective-permute-start | bytes 368648 | tf_op jit(solution)/shard_map/ppermute | solution.py:177
  64.3 3.4 %collective-permute-start.2 = (bf16[80,768]{1,0:T(8,128)(2,1)S(1)}, bf16[80,768]{1,0:T(8,128)(2,1)S(1)}, u32[]{:S(2)}, u32[]{:S(2)}) collective-permute-start(bf16[80,768]{1,0:T(8,128)(2,1)S(1)} %fusion.4.refs_0_), channel_id=1, source_target_pairs={{0,24},{8,0},{16,8},{24,16},{1,25},{9,1},{17,9},{25,17},{2,26},{10... | collective-permute-start | bytes 368648 | tf_op jit(solution)/shard_map/ppermute | solution.py:177
  67.7 2.9 %collective-permute-done.1.refs_2_ = bf16[80,768]{1,0:T(8,128)(2,1)S(1)} collective-permute-done((bf16[80,768]{1,0:T(8,128)(2,1)S(1)}, bf16[80,768]{1,0:T(8,128)(2,1)S(1)}, u32[]{:S(2)}, u32[]{:S(2)}) %collective-permute-start.1) | collective-permute-done | bytes 122912 | tf_op jit(solution)/shard_map/ppermute | solution.py:177
  70.6 1.1 %collective-permute-done.2.refs_3_ = bf16[80,768]{1,0:T(8,128)(2,1)S(1)} collective-permute-done((bf16[80,768]{1,0:T(8,128)(2,1)S(1)}, bf16[80,768]{1,0:T(8,128)(2,1)S(1)}, u32[]{:S(2)}, u32[]{:S(2)}) %collective-permute-start.2) | collective-permute-done | bytes 122912 | tf_op jit(solution)/shard_map/ppermute | solution.py:177
  71.8 2.2 %shard_map.113 = bf16[32,24,640]{2,1,0:T(8,128)(2,1)} custom-call(s32[1]{0:T(128)} %bitcast.7.me_ref, bf16[4,80,640]{2,1,0:T(8,128)(2,1)S(1)} %all-to-all-done.1.scaled_ref, bf16[80,768]{1,0:T(8,128)(2,1)S(1)} %fusion.4.refs_0_, bf16[80,768]{1,0:T(8,128)(2,1)S(1)} %collective-permute-done.refs_1_, bf16[80,768]{1,0:T(8,128)(2,1)S(1)} %collective-permute-done.1.refs_2_, ...), custom_call_target="tpu_custom_call" | custom-call | tf_op jit(solution)/shard_map/pallas_call | solution.py:200
  74.0 9.8 %all-to-all-start.2 = ((bf16[32,24,640]{2,1,0:T(8,128)(2,1)}), bf16[32,24,640]{2,1,0:T(8,128)(2,1)S(1)}, u32[]{:S(2)}, u32[]{:S(2)}) async-start(bf16[32,24,640]{2,1,0:T(8,128)(2,1)} %shard_map.113), calls=%async_computation.2 | async-start | bytes 1966080 | tf_op jit(solution)/shard_map/all_to_all | solution.py:148
  83.8 1.9 %collective-permute-start.3 = (f32[1,128]{1,0:T(1,128)S(1)}, f32[1,128]{1,0:T(1,128)S(1)}, u32[]{:S(2)}, u32[]{:S(2)}) collective-permute-start(f32[1,128]{1,0:T(1,128)S(1)} %get-tuple-element.9), channel_id=1, source_target_pairs={{0,32},{32,0},{64,96},{96,64},{128,160},{160,128},{192,224},{224,1... | collective-permute-start | bytes 1544 | tf_op jit(solution)/shard_map/ppermute | solution.py:208
  85.7 1.1 %collective-permute-done.3 = f32[1,128]{1,0:T(1,128)S(1)} collective-permute-done((f32[1,128]{1,0:T(1,128)S(1)}, f32[1,128]{1,0:T(1,128)S(1)}, u32[]{:S(2)}, u32[]{:S(2)}) %collective-permute-start.3) | collective-permute-done | bytes 544 | tf_op jit(solution)/shard_map/ppermute | solution.py:208
  86.8 1.9 %collective-permute-start.4 = (f32[2,128]{1,0:T(2,128)S(1)}, f32[2,128]{1,0:T(2,128)S(1)}, u32[]{:S(2)}, u32[]{:S(2)}) collective-permute-start(f32[2,128]{1,0:T(2,128)S(1)} %pad_maximum_fusion.2), channel_id=1, source_target_pairs={{0,64},{32,96},{64,0},{96,32},{128,192},{160,224},{192,128},{224,1... | collective-permute-start | bytes 3080 | tf_op jit(solution)/shard_map/ppermute | solution.py:208
  88.8 3.5 %collective-permute-done.4 = f32[2,128]{1,0:T(2,128)S(1)} collective-permute-done((f32[2,128]{1,0:T(2,128)S(1)}, f32[2,128]{1,0:T(2,128)S(1)}, u32[]{:S(2)}, u32[]{:S(2)}) %collective-permute-start.4) | collective-permute-done | bytes 1056 | tf_op jit(solution)/shard_map/ppermute | solution.py:208
  92.3 3.2 %collective-permute-start.5 = (f32[4,128]{1,0:T(4,128)S(1)}, f32[4,128]{1,0:T(4,128)S(1)}, u32[]{:S(2)}, u32[]{:S(2)}) collective-permute-start(f32[4,128]{1,0:T(4,128)S(1)} %pad_maximum_fusion.1), channel_id=1, source_target_pairs={{0,128},{32,160},{64,192},{96,224},{128,0},{160,32},{192,64},{224,... | collective-permute-start | bytes 6152 | tf_op jit(solution)/shard_map/ppermute | solution.py:208
  95.5 3.2 %collective-permute-done.5 = f32[4,128]{1,0:T(4,128)S(1)} collective-permute-done((f32[4,128]{1,0:T(4,128)S(1)}, f32[4,128]{1,0:T(4,128)S(1)}, u32[]{:S(2)}, u32[]{:S(2)}) %collective-permute-start.5) | collective-permute-done | bytes 2080 | tf_op jit(solution)/shard_map/ppermute | solution.py:208
  98.7 4.7 %collective-permute-start.6 = (f32[8,128]{1,0:T(8,128)S(1)}, f32[8,128]{1,0:T(8,128)S(1)}, u32[]{:S(2)}, u32[]{:S(2)}) collective-permute-start(f32[8,128]{1,0:T(8,128)S(1)} %pad_maximum_fusion), channel_id=1, source_target_pairs={{0,256},{32,288},{64,320},{96,352},{128,384},{160,416},{192,448},{... | collective-permute-start | bytes 12296 | tf_op jit(solution)/shard_map/ppermute | solution.py:208
  103.5 4.1 %multiply_convert_fusion = (bf16[80,768]{1,0:T(8,128)(2,1)}, bf16[80,768]{1,0:T(8,128)(2,1)}) fusion(bf16[80,768]{1,0:T(8,128)(2,1)S(1)} %copy-done.8, bf16[80,768]{1,0:T(8,128)(2,1)S(1)} %copy-done.9, bf16[80,2560]{1,0:T(8,128)(2,1)S(1)} %get-tuple-element.7, bf16[1,768,2560]{2,1,0:T(8,128)(2,1)} %param.15), kind=kOutput, calls=%fused_computation.17 | convolution fusion | flops 315494400 | bytes 4833280 | tf_op jit(solution)/shard_map/dot_general | solution.py:192
  108.2 1.0 shard_map.115
  109.1 1.4 %all-to-all-done.2.terms_ref = bf16[32,24,640]{2,1,0:T(8,128)(2,1)S(1)} async-done(((bf16[32,24,640]{2,1,0:T(8,128)(2,1)}), bf16[32,24,640]{2,1,0:T(8,128)(2,1)S(1)}, u32[]{:S(2)}, u32[]{:S(2)}) %all-to-all-start.2) | async-done | bytes 983072 | tf_op jit(solution)/shard_map/all_to_all | solution.py:148
  (28 shorter events, 4.2 us)
Async XLA Ops:
  0.6 1.1 copy-start
  1.7 0.7 copy-start.1
  2.4 0.7 copy-start.3
  3.1 0.7 copy-start.5
  3.8 0.7 copy-start.7
  4.5 12.2 %copy-start.8 = (bf16[80,768]{1,0:T(8,128)(2,1)S(1)}, bf16[80,768]{1,0:T(8,128)(2,1)}, u32[]{:S(2)}) copy-start(bf16[80,768]{1,0:T(8,128)(2,1)} %param.13) | copy-start | bytes 368644
  4.5 12.2 %copy-start.9 = (bf16[80,768]{1,0:T(8,128)(2,1)S(1)}, bf16[80,768]{1,0:T(8,128)(2,1)}, u32[]{:S(2)}) copy-start(bf16[80,768]{1,0:T(8,128)(2,1)} %param.14) | copy-start | bytes 368644
  6.2 44.0 %all-to-all-start = ((bf16[16,16,2688]{2,1,0:T(8,128)(2,1)}), bf16[16,16,2688]{2,1,0:T(8,128)(2,1)S(1)}, u32[]{:S(2)}, u32[]{:S(2)}) async-start(bf16[16,16,2688]{2,1,0:T(8,128)(2,1)} %bitcast.4), calls=%async_computation | async-start | bytes 2752512 | tf_op jit(solution)/shard_map/all_to_all | solution.py:148
  51.5 20.2 %all-to-all-start.1 = ((bf16[4,80,640]{2,1,0:T(8,128)(2,1)}), bf16[4,80,640]{2,1,0:T(8,128)(2,1)S(1)}, u32[]{:S(2)}, u32[]{:S(2)}) async-start(bf16[4,80,640]{2,1,0:T(8,128)(2,1)} %get-tuple-element.8), calls=%async_computation.1 | async-start | bytes 819200 | tf_op jit(solution)/shard_map/all_to_all | solution.py:148
  55.8 11.9 %collective-permute-start = (bf16[80,768]{1,0:T(8,128)(2,1)S(1)}, bf16[80,768]{1,0:T(8,128)(2,1)S(1)}, u32[]{:S(2)}, u32[]{:S(2)}) collective-permute-start(bf16[80,768]{1,0:T(8,128)(2,1)S(1)} %fusion.4.refs_0_), channel_id=1, source_target_pairs={{0,8},{8,16},{16,24},{24,0},{1,9},{9,17},{17,25},{25,1},{2,10},{10... | collective-permute-start | bytes 368648 | tf_op jit(solution)/shard_map/ppermute | solution.py:177
  59.7 10.9 %collective-permute-start.1 = (bf16[80,768]{1,0:T(8,128)(2,1)S(1)}, bf16[80,768]{1,0:T(8,128)(2,1)S(1)}, u32[]{:S(2)}, u32[]{:S(2)}) collective-permute-start(bf16[80,768]{1,0:T(8,128)(2,1)S(1)} %fusion.4.refs_0_), channel_id=1, source_target_pairs={{0,16},{8,24},{16,0},{24,8},{1,17},{9,25},{17,1},{25,9},{2,18},{10... | collective-permute-start | bytes 368648 | tf_op jit(solution)/shard_map/ppermute | solution.py:177
  64.3 7.4 %collective-permute-start.2 = (bf16[80,768]{1,0:T(8,128)(2,1)S(1)}, bf16[80,768]{1,0:T(8,128)(2,1)S(1)}, u32[]{:S(2)}, u32[]{:S(2)}) collective-permute-start(bf16[80,768]{1,0:T(8,128)(2,1)S(1)} %fusion.4.refs_0_), channel_id=1, source_target_pairs={{0,24},{8,0},{16,8},{24,16},{1,25},{9,1},{17,9},{25,17},{2,26},{10... | collective-permute-start | bytes 368648 | tf_op jit(solution)/shard_map/ppermute | solution.py:177
  71.7 36.4 %copy-start.2 = (s32[128,6]{0,1:T(8,128)S(1)}, s32[128,6]{0,1:T(8,128)}, u32[]{:S(2)}) copy-start(s32[128,6]{0,1:T(8,128)} %param.11) | copy-start | bytes 9220
  71.7 36.4 %copy-start.4 = (s32[128,6]{0,1:T(8,128)S(1)}, s32[128,6]{0,1:T(8,128)}, u32[]{:S(2)}) copy-start(s32[128,6]{0,1:T(8,128)} %param.12) | copy-start | bytes 9220
  71.8 36.4 %copy-start.6 = (s32[128,3]{0,1:T(4,128)S(1)}, s32[128,3]{0,1:T(4,128)}, u32[]{:S(2)}) copy-start(s32[128,3]{0,1:T(4,128)} %param.10) | copy-start | bytes 4612
  74.0 36.6 %all-to-all-start.2 = ((bf16[32,24,640]{2,1,0:T(8,128)(2,1)}), bf16[32,24,640]{2,1,0:T(8,128)(2,1)S(1)}, u32[]{:S(2)}, u32[]{:S(2)}) async-start(bf16[32,24,640]{2,1,0:T(8,128)(2,1)} %shard_map.113), calls=%async_computation.2 | async-start | bytes 1966080 | tf_op jit(solution)/shard_map/all_to_all | solution.py:148
  83.8 3.1 %collective-permute-start.3 = (f32[1,128]{1,0:T(1,128)S(1)}, f32[1,128]{1,0:T(1,128)S(1)}, u32[]{:S(2)}, u32[]{:S(2)}) collective-permute-start(f32[1,128]{1,0:T(1,128)S(1)} %get-tuple-element.9), channel_id=1, source_target_pairs={{0,32},{32,0},{64,96},{96,64},{128,160},{160,128},{192,224},{224,1... | collective-permute-start | bytes 1544 | tf_op jit(solution)/shard_map/ppermute | solution.py:208
  86.8 5.5 %collective-permute-start.4 = (f32[2,128]{1,0:T(2,128)S(1)}, f32[2,128]{1,0:T(2,128)S(1)}, u32[]{:S(2)}, u32[]{:S(2)}) collective-permute-start(f32[2,128]{1,0:T(2,128)S(1)} %pad_maximum_fusion.2), channel_id=1, source_target_pairs={{0,64},{32,96},{64,0},{96,32},{128,192},{160,224},{192,128},{224,1... | collective-permute-start | bytes 3080 | tf_op jit(solution)/shard_map/ppermute | solution.py:208
  92.3 6.4 %collective-permute-start.5 = (f32[4,128]{1,0:T(4,128)S(1)}, f32[4,128]{1,0:T(4,128)S(1)}, u32[]{:S(2)}, u32[]{:S(2)}) collective-permute-start(f32[4,128]{1,0:T(4,128)S(1)} %pad_maximum_fusion.1), channel_id=1, source_target_pairs={{0,128},{32,160},{64,192},{96,224},{128,0},{160,32},{192,64},{224,... | collective-permute-start | bytes 6152 | tf_op jit(solution)/shard_map/ppermute | solution.py:208
  98.7 9.4 %collective-permute-start.6 = (f32[8,128]{1,0:T(8,128)S(1)}, f32[8,128]{1,0:T(8,128)S(1)}, u32[]{:S(2)}, u32[]{:S(2)}) collective-permute-start(f32[8,128]{1,0:T(8,128)S(1)} %pad_maximum_fusion), channel_id=1, source_target_pairs={{0,256},{32,288},{64,320},{96,352},{128,384},{160,416},{192,448},{... | collective-permute-start | bytes 12296 | tf_op jit(solution)/shard_map/ppermute | solution.py:208

commit v2 on v1

--- a/solution.py
+++ b/solution.py
@@ -1,3 +1,5 @@
+import functools
+
 import jax
 import jax.numpy as jnp
 from jax import lax
@@ -10,7 +12,10 @@
 PRESEL = 3
 SRC_CAP = 16
 LANES = 128
-NODE_DP = ("node", "dp_0", "dp_1")
+DP = ("dp_0", "dp_1", "dp_2")
+NODE_DP = ("node", *DP)
+TEAM = ("dp_0", "dp_2")
+HALF = LANES // 2
 F32 = jnp.float32
 BF16 = jnp.bfloat16
 
@@ -23,7 +28,17 @@
     return rows
 
 
-def route_kernel(og_ref, prob_ref, presel_ref, expert_ref, slot_ref, send_ref):
+def route_kernel(*refs):
+    sources, send_ref, held, arrived = refs[:5], refs[5], refs[6:11], refs[11]
+    copies = [
+        pltpu.make_async_copy(source, place, arrived.at[i])
+        for i, (source, place) in enumerate(zip(sources, held))
+    ]
+    for copy in reversed(copies):
+        copy.start()
+    for copy in reversed(copies[1:]):
+        copy.wait()
+    og_ref, prob_ref, presel_ref, expert_ref, slot_ref = held
     tokens, features = og_ref.shape
     n_node = send_ref.shape[0] // SRC_CAP
     expert, slot, presel = expert_ref[...], slot_ref[...], presel_ref[...]
@@ -55,12 +70,12 @@
     info = jnp.where(lane == 0, slot_rows, jnp.where(lane == 1, prob_rows, 0.0))
     send_ref[:, features:] = info.reshape(rows, LANES).astype(BF16)
     pick = jnp.where(picked, 1.0, 0.0).reshape(rows, tokens).astype(BF16)
+    copies[0].wait()
     send_ref[:, :features] = jnp.dot(pick, og_ref[...], preferred_element_type=F32).astype(BF16)
 
 
 def land_kernel(recv_ref, out_ref, scaled_ref, parts_ref, grad_p_ref):
     capacity, features = scaled_ref.shape
-    n_parts, _, width = parts_ref.shape
     recv = recv_ref[...]
     slot = recv_ref[:, features : features + 1].astype(F32)
     lane = lax.broadcasted_iota(jnp.int32, (recv.shape[0], LANES), 1).astype(F32)
@@ -72,39 +87,84 @@
     p = landed[:, features + 1 : features + 2]
     scaled = (p * dy).astype(BF16)
     scaled_ref[...] = scaled
-    for k in range(n_parts):
-        parts_ref[k] = scaled[:, k * width : (k + 1) * width]
+    n = parts_ref.shape[0]
+    rows = capacity // 2
+    low = lax.broadcasted_iota(jnp.int32, (rows, LANES), 1) < HALF
+    for k in range(n):
+        for j in range(2):
+            tile = 2 * k + j
+            parts_ref[k, j * capacity : (j + 1) * capacity] = scaled[
+                :, tile * LANES : (tile + 1) * LANES
+            ]
+    for k in range(n):
+        tile = 2 * n + k // 2
+        own = (p * dy[:, tile * LANES : (tile + 1) * LANES])
+        swapped = pltpu.roll(own, HALF, 1)
+        top, bottom = (own, swapped) if k % 2 == 0 else (swapped, own)
+        parts_ref[k, 2 * capacity :] = jnp.where(low, top[:rows], bottom[rows:]).astype(BF16)
     grad_p = jnp.sum(dy * out_ref[...], axis=1, keepdims=True)
     row = lax.broadcasted_iota(jnp.int32, (capacity, LANES), 0)
     column = lax.broadcasted_iota(jnp.int32, (capacity, LANES), 1)
     grad_p_ref[...] = jnp.sum(jnp.where(row == column, grad_p, 0.0), axis=0, keepdims=True)
 
 
-def partial_kernel(me_ref, scaled_ref, *refs):
+def partial_kernel(me_ref, parts_ref, *refs):
     *hidden_refs, out_ref = refs
-    n = len(hidden_refs)
+    n_0 = len(hidden_refs)
+    capacity = hidden_refs[0].shape[1]
     total = None
     for k, hidden_ref in enumerate(hidden_refs):
-        block = lax.rem(me_ref[0] - k + n, n)
-        term = lax.dot_general(
-            hidden_ref[...],
-            scaled_ref[block],
-            (((0,), (0,)), ((), ())),
-            preferred_element_type=F32,
-        )
-        total = term if total is None else total + term
-    out_ref[...] = total.astype(BF16).reshape(out_ref.shape)
-
-
-def sum_kernel(terms_ref, out_ref):
-    n, _, width = terms_ref.shape
-    n_parts = out_ref.shape[1] // width
-    each = n // n_parts
-    for k in range(n_parts):
-        total = terms_ref[k * each].astype(F32)
-        for j in range(1, each):
-            total += terms_ref[k * each + j].astype(F32)
-        out_ref[:, k * width : (k + 1) * width] = total.astype(BF16)
+        for j in range(2):
+            block = lax.rem(me_ref[0] - k + n_0, n_0) * 2 + (me_ref[1] ^ j)
+            packed = parts_ref[block, 2 * capacity :].astype(F32)
+            halves = jnp.concatenate([packed, pltpu.roll(packed, HALF, 1)]).astype(BF16)
+            scaled = jnp.concatenate(
+                [parts_ref[block, :capacity], parts_ref[block, capacity : 2 * capacity], halves],
+                axis=1,
+            )
+            term = lax.dot_general(
+                hidden_ref[j], scaled, (((0,), (0,)), ((), ())), preferred_element_type=F32
+            )
+            total = term if total is None else total + term
+    n = out_ref.shape[0]
+    share = total.shape[0] // n
+    total = total.reshape(n, share, 3 * LANES)
+    out_ref[:, :share] = total[:, :, :LANES].astype(BF16)
+    out_ref[:, share : 2 * share] = total[:, :, LANES : 2 * LANES].astype(BF16)
+    third = share // 3
+    last = total[:, :, 2 * LANES :]
+    low = lax.broadcasted_iota(jnp.int32, (n, third, LANES), 2) < HALF
+    swapped = pltpu.roll(last[:, third : 2 * third], HALF, 2)
+    mixed = jnp.where(low, last[:, :third], swapped)
+    out_ref[:, 2 * share : 2 * share + third] = mixed.astype(BF16)
+    out_ref[:, 2 * share + third :] = last[:, 2 * third :].astype(BF16)
+
+
+def sum_kernel(n_0, n_1, terms_ref, out_ref):
+    share = out_ref.shape[0]
+    third = share // 3
+    n = 2 * n_0
+    low = lax.broadcasted_iota(jnp.int32, (third, LANES), 1) < HALF
+
+    def put(row, tile, value):
+        out_ref[row : row + value.shape[0], tile * LANES : (tile + 1) * LANES] = value.astype(BF16)
+
+    for k in range(n_0):
+        ends = []
+        for j in range(2):
+            total = None
+            for i in range(n_1):
+                term = terms_ref[(k * n_1 + i) * 2 + j].astype(F32)
+                total = term if total is None else total + term
+            tile = 2 * (2 * k + j)
+            put(0, tile, total[:share])
+            put(0, tile + 1, total[share : 2 * share])
+            ends.append((total[2 * share : 2 * share + third], total[2 * share + third :]))
+        (mixed_0, last_0), (mixed_1, last_1) = ends
+        tile = 2 * n + k
+        put(0, tile, jnp.where(low, mixed_0, pltpu.roll(mixed_1, HALF, 1)))
+        put(third, tile, jnp.where(low, pltpu.roll(mixed_0, HALF, 1), mixed_1))
+        put(2 * third, tile, jnp.where(low, last_0, pltpu.roll(last_1, HALF, 1)))
 
 
 def return_kernel(me_ref, grad_p_ref, presel_ref, expert_ref, slot_ref, out_ref):
@@ -129,18 +189,20 @@
     out_ref[...] = result
 
 
+HBM = pl.BlockSpec(memory_space=pltpu.HBM)
 VMEM = pl.BlockSpec(memory_space=pltpu.VMEM)
 SMEM = pl.BlockSpec(memory_space=pltpu.SMEM)
 
 
-def call(kernel, out_shape, in_specs):
+def call(kernel, out_shape, in_specs, scratch=(), vmem_mib=12):
     many = isinstance(out_shape, (tuple, list))
     return pl.pallas_call(
         kernel,
         out_shape=out_shape,
         in_specs=in_specs,
         out_specs=[VMEM] * len(out_shape) if many else VMEM,
-        compiler_params=pltpu.CompilerParams(vmem_limit_bytes=12 * 1024 * 1024),
+        scratch_shapes=scratch,
+        compiler_params=pltpu.CompilerParams(vmem_limit_bytes=vmem_mib << 20),
     )
 
 
@@ -153,15 +215,21 @@
 ):
     _, features = out_grad.shape
     capacity, units = gate_pre.shape
-    n_node, n_0, n_1 = (lax.axis_size(a) for a in NODE_DP)
-    width = features // n_0
-    share = units // (n_0 * n_1)
+    n_node, n_0, n_1, n_2 = (lax.axis_size(a) for a in NODE_DP)
+    team = n_0 * n_2
+    group = team * n_1
+    share = units // group
     shape = jax.ShapeDtypeStruct
     presel, expert, slot = presel_nodes.T, route_expert.T, route_slot.T
+    routed = (out_grad, gate_prob.T, presel, expert, slot)
 
     send = call(
-        route_kernel, shape((n_node * SRC_CAP, features + LANES), BF16), [VMEM] * 5
-    )(out_grad, gate_prob.T, presel, expert, slot)
+        route_kernel,
+        shape((n_node * SRC_CAP, features + LANES), BF16),
+        [HBM] * 5,
+        [pltpu.VMEM(a.shape, a.dtype) for a in routed] + [pltpu.SemaphoreType.DMA((5,))],
+        vmem_mib=60,
+    )(*routed)
     recv = exchange(send.reshape(n_node, SRC_CAP, features + LANES), "node")
     recv = recv.reshape(n_node * SRC_CAP, features + LANES)
 
@@ -171,37 +239,39 @@
     sigmoid_gate = jax.nn.sigmoid(gate_rows)
     activated = gate_rows * sigmoid_gate
     hidden = (activated * up_rows).astype(BF16)
-    hiddens = [hidden]
+    near = lax.ppermute(hidden, "dp_2", [(0, 1), (1, 0)])
+    hidden_pair = jnp.stack([hidden, near])
+    hiddens = [hidden_pair]
     for k in range(1, n_0):
-        hiddens.append(
-            lax.ppermute(hidden, "dp_0", [(i, (i + k) % n_0) for i in range(n_0)])
-        )
+        hiddens.append(lax.ppermute(hidden_pair, "dp_0", [(i, (i + k) % n_0) for i in range(n_0)]))
     slot_out = jnp.dot(hidden, weight, preferred_element_type=F32)
 
     scaled, parts, grad_p = call(
         land_kernel,
         [
             shape((capacity, features), BF16),
-            shape((n_0, capacity, width), BF16),
+            shape((team, features * capacity // (team * LANES), LANES), BF16),
             shape((1, LANES), F32),
         ],
         [VMEM] * 2,
     )(recv, slot_out)
-    parts = exchange(parts, "dp_0")
-
-    d_hidden = lax.dot_general(
-        scaled, weight, (((1,), (1,)), ((), ())), preferred_element_type=F32
-    )
+    parts = exchange(parts, TEAM)
+
+    d_hidden = lax.dot_general(scaled, weight, (((1,), (1,)), ((), ())), preferred_element_type=F32)
     grad_gate = (
         d_hidden * up_rows * sigmoid_gate * (1.0 + gate_rows * (1.0 - sigmoid_gate))
     ).astype(BF16)
     grad_up = (d_hidden * activated).astype(BF16)
 
     partial = call(
-        partial_kernel, shape((n_0 * n_1, share, width), BF16), [SMEM] + [VMEM] * (1 + n_0)
-    )(lax.axis_index("dp_0")[None], parts, *hiddens)
-    terms = exchange(partial, ("dp_0", "dp_1"))
-    grad_down = call(sum_kernel, shape((share, features), BF16), [VMEM])(terms)[None]
+        partial_kernel,
+        shape((group, 2 * share + 2 * share // 3, LANES), BF16),
+        [SMEM] + [VMEM] * (1 + n_0),
+    )(jnp.stack([lax.axis_index(a) for a in TEAM]), parts, *hiddens)
+    terms = exchange(partial, DP)
+    grad_down = call(
+        functools.partial(sum_kernel, n_0, n_1), shape((share, features), BF16), [VMEM]
+    )(terms)[None]
 
     step = 1
     while step < n_node:
@@ -215,12 +285,12 @@
 
 
 def solution(mesh):
-    finer = Mesh(mesh.devices.reshape(mesh.shape["node"], 4, 8), NODE_DP)
+    finer = Mesh(mesh.devices.reshape(mesh.shape["node"], 4, 4, 2), NODE_DP)
     in_specs = (P(NODE_DP, None),) * 7 + (P("node", None, None),)
     out_specs = (
         P(NODE_DP, None),
         P(NODE_DP, None),
-        P("node", ("dp_0", "dp_1"), None),
+        P("node", DP, None),
         P(NODE_DP, None),
     )
     return jax.shard_map(

time: 112 us -> 123 us (1.098)
  the two profiles are of different devices: /device:TPU:8 before, /device:TPU:2 now
where the time goes in v2:
time: 123 us; the launch traced here: 122 us
  waiting for transfers between devices  57.3 us (47%)
  starting transfers between devices  47.8 us (39%)
  Pallas kernels  8.76 us (7%)
  matrix products  7.05 us (6%)
    all_to_all x3, waiting for transfers between devices, exchange(): return lax.all_to_all(value, axes, split_axis=0, concat_axis=0, tiled=True)  30.5 us
    all_to_all x3, starting transfers between devices, exchange(): return lax.all_to_all(value, axes, split_axis=0, concat_axis=0, tiled=True)  24.7 us
    ppermute x4, waiting for transfers between devices, step_of(): other = lax.ppermute(grad_p, 'node', [(i, i ^ step) for i in range(n_node)])  10.9 us
    ppermute x3, starting transfers between devices, step_of(): lax.ppermute(hidden_pair, 'dp_0', [(i, (i + k) % n_0) for i in range(n_0)])  10.4 us
    ppermute x4, starting transfers between devices, step_of(): other = lax.ppermute(grad_p, 'node', [(i, i ^ step) for i in range(n_node)])  9.26 us
    ppermute x3, waiting for transfers between devices, step_of(): lax.ppermute(hidden_pair, 'dp_0', [(i, (i + k) % n_0) for i in range(n_0)])  9.16 us
    ppermute x1, waiting for transfers between devices, step_of(): near = lax.ppermute(hidden, 'dp_2', [(0, 1), (1, 0)])  6.73 us
    dot_general x1, matrix products, step_of(): lax.dot_general(scaled, weight, (((1,), (1,)), ((), ())), preferred_eleme...  4.13 us
  transfers between devices with their start and end apart: 11, of which 9 were waited for; matrix products, arithmetic and copies ran while one was open for 6% of the time, Pallas kernels for 1%

profile of v2, /device:TPU:2, one launch (start us, length us, event | category | flops | bytes accessed | tf_op | source)
XLA Modules:
  0.0 121.9 jit_solution(6655022936089830358)
XLA Ops:
  0.7 2.8 %shard_map.111 = bf16[256,2688]{1,0:T(8,128)(2,1)} custom-call(bf16[128,2560]{1,0:T(8,128)(2,1)} %refs_0_.1, bf16[6,128]{1,0:T(8,128)(2,1)} %bitcast.34, s32[3,128]{1,0:T(4,128)} %bitcast.27, s32[6,128]{1,0:T(8,128)} %bitcast.23, s32[6,128]{1,0:T(8,128)} %bitcast.25), custom_call_target="tpu_custom_call" | custom-call | tf_op jit(solution)/shard_map/pallas_call | solution.py:226
  3.5 10.4 %all-to-all-start = ((bf16[16,16,2688]{2,1,0:T(8,128)(2,1)}), bf16[16,16,2688]{2,1,0:T(8,128)(2,1)S(1)}, u32[]{:S(2)}, u32[]{:S(2)}) async-start(bf16[16,16,2688]{2,1,0:T(8,128)(2,1)} %bitcast.29), calls=%async_computation | async-start | bytes 2752512 | tf_op jit(solution)/shard_map/all_to_all | solution.py:210
  14.0 2.9 %fusion.2.out_ref = f32[80,2560]{1,0:T(8,128)S(1)} fusion(bf16[80,768]{1,0:T(8,128)(2,1)S(1)} %fusion.4, bf16[1,768,2560]{2,1,0:T(8,128)(2,1)} %param.15), kind=kOutput, calls=%fused_computation.2 | convolution fusion | flops 314572800 | bytes 4874240 | tf_op jit(solution)/shard_map/dot_general | solution.py:247
  16.9 30.5 %all-to-all-done = bf16[16,16,2688]{2,1,0:T(8,128)(2,1)S(1)} async-done(((bf16[16,16,2688]{2,1,0:T(8,128)(2,1)}), bf16[16,16,2688]{2,1,0:T(8,128)(2,1)S(1)}, u32[]{:S(2)}, u32[]{:S(2)}) %all-to-all-start) | async-done | bytes 1376288 | tf_op jit(solution)/shard_map/all_to_all | solution.py:210
  47.5 1.4 %shard_map.112 = (bf16[80,2560]{1,0:T(8,128)(2,1)S(1)}, bf16[8,200,128]{2,1,0:T(8,128)(2,1)}, f32[1,128]{1,0:T(1,128)S(1)}) custom-call(bf16[256,2688]{1,0:T(8,128)(2,1)S(1)} %bitcast.22, f32[80,2560]{1,0:T(8,128)S(1)} %fusion.2.out_ref), custom_call_target="tpu_custom_call" | custom-call | tf_op jit(solution)/shard_map/pallas_call | solution.py:249
  48.9 5.8 %all-to-all-start.1 = ((bf16[8,200,128]{2,1,0:T(8,128)(2,1)}), bf16[8,200,128]{2,1,0:T(8,128)(2,1)S(1)}, u32[]{:S(2)}, u32[]{:S(2)}) async-start(bf16[8,200,128]{2,1,0:T(8,128)(2,1)} %get-tuple-element.8), calls=%async_computation.1 | async-start | bytes 819200 | tf_op jit(solution)/shard_map/all_to_all | solution.py:210
  54.7 3.4 %collective-permute-start = (bf16[80,768]{1,0:T(8,128)(2,1)S(1)}, bf16[80,768]{1,0:T(8,128)(2,1)S(1)}, u32[]{:S(2)}, u32[]{:S(2)}) collective-permute-start(bf16[80,768]{1,0:T(8,128)(2,1)S(1)} %fusion.4), channel_id=1, source_target_pairs={{0,1},{1,0},{2,3},{3,2},{4,5},{5,4},{6,7},{7,6},{8,9},{9,8},{10,11... | collective-permute-start | bytes 368648 | tf_op jit(solution)/shard_map/ppermute | solution.py:242
  58.1 6.7 %collective-permute-done = bf16[80,768]{1,0:T(8,128)(2,1)S(1)} collective-permute-done((bf16[80,768]{1,0:T(8,128)(2,1)S(1)}, bf16[80,768]{1,0:T(8,128)(2,1)S(1)}, u32[]{:S(2)}, u32[]{:S(2)}) %collective-permute-start) | collective-permute-done | bytes 122912 | tf_op jit(solution)/shard_map/ppermute | solution.py:242
  64.9 3.3 %collective-permute-start.1 = (bf16[2,80,768]{2,1,0:T(8,128)(2,1)S(1)}, bf16[2,80,768]{2,1,0:T(8,128)(2,1)S(1)}, u32[]{:S(2)}, u32[]{:S(2)}) collective-permute-start(bf16[2,80,768]{2,1,0:T(8,128)(2,1)S(1)} %pad_maximum_fusion.refs_0_), channel_id=1, source_target_pairs={{0,8},{8,16},{16,24},{24,0},{1,9},{9,17},{17,25},{25,1},{2,10},{10... | collective-permute-start | bytes 737288 | tf_op jit(solution)/shard_map/ppermute | solution.py:246
  68.2 3.1 %collective-permute-start.2 = (bf16[2,80,768]{2,1,0:T(8,128)(2,1)S(1)}, bf16[2,80,768]{2,1,0:T(8,128)(2,1)S(1)}, u32[]{:S(2)}, u32[]{:S(2)}) collective-permute-start(bf16[2,80,768]{2,1,0:T(8,128)(2,1)S(1)} %pad_maximum_fusion.refs_0_), channel_id=1, source_target_pairs={{0,16},{8,24},{16,0},{24,8},{1,17},{9,25},{17,1},{25,9},{2,18},{10... | collective-permute-start | bytes 737288 | tf_op jit(solution)/shard_map/ppermute | solution.py:246
  71.3 4.0 %collective-permute-start.3 = (bf16[2,80,768]{2,1,0:T(8,128)(2,1)S(1)}, bf16[2,80,768]{2,1,0:T(8,128)(2,1)S(1)}, u32[]{:S(2)}, u32[]{:S(2)}) collective-permute-start(bf16[2,80,768]{2,1,0:T(8,128)(2,1)S(1)} %pad_maximum_fusion.refs_0_), channel_id=1, source_target_pairs={{0,24},{8,0},{16,8},{24,16},{1,25},{9,1},{17,9},{25,17},{2,26},{10... | collective-permute-start | bytes 737288 | tf_op jit(solution)/shard_map/ppermute | solution.py:246
  75.6 4.9 %collective-permute-done.2.refs_2_ = bf16[2,80,768]{2,1,0:T(8,128)(2,1)S(1)} collective-permute-done((bf16[2,80,768]{2,1,0:T(8,128)(2,1)S(1)}, bf16[2,80,768]{2,1,0:T(8,128)(2,1)S(1)}, u32[]{:S(2)}, u32[]{:S(2)}) %collective-permute-start.2) | collective-permute-done | bytes 245792 | tf_op jit(solution)/shard_map/ppermute | solution.py:246
  80.5 4.1 %collective-permute-done.3.refs_3_ = bf16[2,80,768]{2,1,0:T(8,128)(2,1)S(1)} collective-permute-done((bf16[2,80,768]{2,1,0:T(8,128)(2,1)S(1)}, bf16[2,80,768]{2,1,0:T(8,128)(2,1)S(1)}, u32[]{:S(2)}, u32[]{:S(2)}) %collective-permute-start.3) | collective-permute-done | bytes 245792 | tf_op jit(solution)/shard_map/ppermute | solution.py:246
  84.6 2.8 %shard_map.113 = bf16[32,64,128]{2,1,0:T(8,128)(2,1)} custom-call(s32[2]{0:T(128)S(1)} %pad_add_fusion.me_ref, bf16[8,200,128]{2,1,0:T(8,128)(2,1)S(1)} %all-to-all-done.1.parts_ref, bf16[2,80,768]{2,1,0:T(8,128)(2,1)S(1)} %pad_maximum_fusion.refs_0_, bf16[2,80,768]{2,1,0:T(8,128)(2,1)S(1)} %collective-permute-done.1.refs_1_, ...), custom_call_target="tpu_custom_call" | custom-call | tf_op jit(solution)/shard_map/pallas_call | solution.py:266
  87.4 8.5 %all-to-all-start.2 = ((bf16[32,64,128]{2,1,0:T(8,128)(2,1)}), bf16[32,64,128]{2,1,0:T(8,128)(2,1)S(1)}, u32[]{:S(2)}, u32[]{:S(2)}) async-start(bf16[32,64,128]{2,1,0:T(8,128)(2,1)} %shard_map.113), calls=%async_computation.2 | async-start | bytes 1048576 | tf_op jit(solution)/shard_map/all_to_all | solution.py:210
  95.8 1.9 %collective-permute-start.4 = (f32[1,128]{1,0:T(1,128)S(1)}, f32[1,128]{1,0:T(1,128)S(1)}, u32[]{:S(2)}, u32[]{:S(2)}) collective-permute-start(f32[1,128]{1,0:T(1,128)S(1)} %get-tuple-element.9), channel_id=1, source_target_pairs={{0,32},{32,0},{64,96},{96,64},{128,160},{160,128},{192,224},{224,1... | collective-permute-start | bytes 1544 | tf_op jit(solution)/shard_map/ppermute | solution.py:278
  97.8 1.1 collective-permute-done.4
  98.9 1.9 %collective-permute-start.5 = (f32[2,128]{1,0:T(2,128)S(1)}, f32[2,128]{1,0:T(2,128)S(1)}, u32[]{:S(2)}, u32[]{:S(2)}) collective-permute-start(f32[2,128]{1,0:T(2,128)S(1)} %pad_maximum_fusion.3), channel_id=1, source_target_pairs={{0,64},{32,96},{64,0},{96,32},{128,192},{160,224},{192,128},{224,1... | collective-permute-start | bytes 3080 | tf_op jit(solution)/shard_map/ppermute | solution.py:278
  100.8 3.5 %collective-permute-done.5 = f32[2,128]{1,0:T(2,128)S(1)} collective-permute-done((f32[2,128]{1,0:T(2,128)S(1)}, f32[2,128]{1,0:T(2,128)S(1)}, u32[]{:S(2)}, u32[]{:S(2)}) %collective-permute-start.5) | collective-permute-done | bytes 1056 | tf_op jit(solution)/shard_map/ppermute | solution.py:278
  104.4 2.1 %collective-permute-start.6 = (f32[4,128]{1,0:T(4,128)S(1)}, f32[4,128]{1,0:T(4,128)S(1)}, u32[]{:S(2)}, u32[]{:S(2)}) collective-permute-start(f32[4,128]{1,0:T(4,128)S(1)} %pad_maximum_fusion.2), channel_id=1, source_target_pairs={{0,128},{32,160},{64,192},{96,224},{128,0},{160,32},{192,64},{224,... | collective-permute-start | bytes 6152 | tf_op jit(solution)/shard_map/ppermute | solution.py:278
  106.5 4.2 %collective-permute-done.6 = f32[4,128]{1,0:T(4,128)S(1)} collective-permute-done((f32[4,128]{1,0:T(4,128)S(1)}, f32[4,128]{1,0:T(4,128)S(1)}, u32[]{:S(2)}, u32[]{:S(2)}) %collective-permute-start.6) | collective-permute-done | bytes 2080 | tf_op jit(solution)/shard_map/ppermute | solution.py:278
  110.8 3.3 %collective-permute-start.7 = (f32[8,128]{1,0:T(8,128)S(1)}, f32[8,128]{1,0:T(8,128)S(1)}, u32[]{:S(2)}, u32[]{:S(2)}) collective-permute-start(f32[8,128]{1,0:T(8,128)S(1)} %pad_maximum_fusion.1), channel_id=1, source_target_pairs={{0,256},{32,288},{64,320},{96,352},{128,384},{160,416},{192,448},{... | collective-permute-start | bytes 12296 | tf_op jit(solution)/shard_map/ppermute | solution.py:278
  114.1 4.1 %multiply_convert_fusion = (bf16[80,768]{1,0:T(8,128)(2,1)}, bf16[80,768]{1,0:T(8,128)(2,1)}) fusion(bf16[80,768]{1,0:T(8,128)(2,1)S(1)} %copy-done.3, bf16[80,768]{1,0:T(8,128)(2,1)S(1)} %copy-done.4, bf16[80,2560]{1,0:T(8,128)(2,1)S(1)} %get-tuple-element.7, bf16[1,768,2560]{2,1,0:T(8,128)(2,1)} %param.15), kind=kOutput, calls=%fused_computation.18 | convolution fusion | flops 315494400 | bytes 4833280 | tf_op jit(solution)/shard_map/dot_general | solution.py:260
  118.2 2.0 %collective-permute-done.7 = f32[8,128]{1,0:T(8,128)S(1)} collective-permute-done((f32[8,128]{1,0:T(8,128)S(1)}, f32[8,128]{1,0:T(8,128)S(1)}, u32[]{:S(2)}, u32[]{:S(2)}) %collective-permute-start.7) | collective-permute-done | bytes 4128 | tf_op jit(solution)/shard_map/ppermute | solution.py:278
  (22 shorter events, 2.1 us)
Async XLA Ops:
  0.6 13.3 %copy-start.3 = (bf16[80,768]{1,0:T(8,128)(2,1)S(1)}, bf16[80,768]{1,0:T(8,128)(2,1)}, u32[]{:S(2)}) copy-start(bf16[80,768]{1,0:T(8,128)(2,1)} %param.13) | copy-start | bytes 368644
  0.6 13.3 %copy-start.4 = (bf16[80,768]{1,0:T(8,128)(2,1)S(1)}, bf16[80,768]{1,0:T(8,128)(2,1)}, u32[]{:S(2)}) copy-start(bf16[80,768]{1,0:T(8,128)(2,1)} %param.14) | copy-start | bytes 368644
  3.5 44.0 %all-to-all-start = ((bf16[16,16,2688]{2,1,0:T(8,128)(2,1)}), bf16[16,16,2688]{2,1,0:T(8,128)(2,1)S(1)}, u32[]{:S(2)}, u32[]{:S(2)}) async-start(bf16[16,16,2688]{2,1,0:T(8,128)(2,1)} %bitcast.29), calls=%async_computation | async-start | bytes 2752512 | tf_op jit(solution)/shard_map/all_to_all | solution.py:210
  48.9 35.7 %all-to-all-start.1 = ((bf16[8,200,128]{2,1,0:T(8,128)(2,1)}), bf16[8,200,128]{2,1,0:T(8,128)(2,1)S(1)}, u32[]{:S(2)}, u32[]{:S(2)}) async-start(bf16[8,200,128]{2,1,0:T(8,128)(2,1)} %get-tuple-element.8), calls=%async_computation.1 | async-start | bytes 819200 | tf_op jit(solution)/shard_map/all_to_all | solution.py:210
  54.7 10.1 %collective-permute-start = (bf16[80,768]{1,0:T(8,128)(2,1)S(1)}, bf16[80,768]{1,0:T(8,128)(2,1)S(1)}, u32[]{:S(2)}, u32[]{:S(2)}) collective-permute-start(bf16[80,768]{1,0:T(8,128)(2,1)S(1)} %fusion.4), channel_id=1, source_target_pairs={{0,1},{1,0},{2,3},{3,2},{4,5},{5,4},{6,7},{7,6},{8,9},{9,8},{10,11... | collective-permute-start | bytes 368648 | tf_op jit(solution)/shard_map/ppermute | solution.py:242
  64.9 10.7 %collective-permute-start.1 = (bf16[2,80,768]{2,1,0:T(8,128)(2,1)S(1)}, bf16[2,80,768]{2,1,0:T(8,128)(2,1)S(1)}, u32[]{:S(2)}, u32[]{:S(2)}) collective-permute-start(bf16[2,80,768]{2,1,0:T(8,128)(2,1)S(1)} %pad_maximum_fusion.refs_0_), channel_id=1, source_target_pairs={{0,8},{8,16},{16,24},{24,0},{1,9},{9,17},{17,25},{25,1},{2,10},{10... | collective-permute-start | bytes 737288 | tf_op jit(solution)/shard_map/ppermute | solution.py:246
  68.2 12.3 %collective-permute-start.2 = (bf16[2,80,768]{2,1,0:T(8,128)(2,1)S(1)}, bf16[2,80,768]{2,1,0:T(8,128)(2,1)S(1)}, u32[]{:S(2)}, u32[]{:S(2)}) collective-permute-start(bf16[2,80,768]{2,1,0:T(8,128)(2,1)S(1)} %pad_maximum_fusion.refs_0_), channel_id=1, source_target_pairs={{0,16},{8,24},{16,0},{24,8},{1,17},{9,25},{17,1},{25,9},{2,18},{10... | collective-permute-start | bytes 737288 | tf_op jit(solution)/shard_map/ppermute | solution.py:246
  71.3 13.3 %collective-permute-start.3 = (bf16[2,80,768]{2,1,0:T(8,128)(2,1)S(1)}, bf16[2,80,768]{2,1,0:T(8,128)(2,1)S(1)}, u32[]{:S(2)}, u32[]{:S(2)}) collective-permute-start(bf16[2,80,768]{2,1,0:T(8,128)(2,1)S(1)} %pad_maximum_fusion.refs_0_), channel_id=1, source_target_pairs={{0,24},{8,0},{16,8},{24,16},{1,25},{9,1},{17,9},{25,17},{2,26},{10... | collective-permute-start | bytes 737288 | tf_op jit(solution)/shard_map/ppermute | solution.py:246
  75.4 44.8 %copy-start = (s32[128,6]{0,1:T(8,128)S(1)}, s32[128,6]{0,1:T(8,128)}, u32[]{:S(2)}) copy-start(s32[128,6]{0,1:T(8,128)} %param.11) | copy-start | bytes 9220
  75.4 44.8 %copy-start.1 = (s32[128,6]{0,1:T(8,128)S(1)}, s32[128,6]{0,1:T(8,128)}, u32[]{:S(2)}) copy-start(s32[128,6]{0,1:T(8,128)} %param.12) | copy-start | bytes 9220
  75.4 44.8 %copy-start.2 = (s32[128,3]{0,1:T(4,128)S(1)}, s32[128,3]{0,1:T(4,128)}, u32[]{:S(2)}) copy-start(s32[128,3]{0,1:T(4,128)} %param.10) | copy-start | bytes 4612
  87.4 33.8 %all-to-all-start.2 = ((bf16[32,64,128]{2,1,0:T(8,128)(2,1)}), bf16[32,64,128]{2,1,0:T(8,128)(2,1)S(1)}, u32[]{:S(2)}, u32[]{:S(2)}) async-start(bf16[32,64,128]{2,1,0:T(8,128)(2,1)} %shard_map.113), calls=%async_computation.2 | async-start | bytes 1048576 | tf_op jit(solution)/shard_map/all_to_all | solution.py:210
  95.8 3.1 %collective-permute-start.4 = (f32[1,128]{1,0:T(1,128)S(1)}, f32[1,128]{1,0:T(1,128)S(1)}, u32[]{:S(2)}, u32[]{:S(2)}) collective-permute-start(f32[1,128]{1,0:T(1,128)S(1)} %get-tuple-element.9), channel_id=1, source_target_pairs={{0,32},{32,0},{64,96},{96,64},{128,160},{160,128},{192,224},{224,1... | collective-permute-start | bytes 1544 | tf_op jit(solution)/shard_map/ppermute | solution.py:278
  98.9 5.5 %collective-permute-start.5 = (f32[2,128]{1,0:T(2,128)S(1)}, f32[2,128]{1,0:T(2,128)S(1)}, u32[]{:S(2)}, u32[]{:S(2)}) collective-permute-start(f32[2,128]{1,0:T(2,128)S(1)} %pad_maximum_fusion.3), channel_id=1, source_target_pairs={{0,64},{32,96},{64,0},{96,32},{128,192},{160,224},{192,128},{224,1... | collective-permute-start | bytes 3080 | tf_op jit(solution)/shard_map/ppermute | solution.py:278
  104.4 6.4 %collective-permute-start.6 = (f32[4,128]{1,0:T(4,128)S(1)}, f32[4,128]{1,0:T(4,128)S(1)}, u32[]{:S(2)}, u32[]{:S(2)}) collective-permute-start(f32[4,128]{1,0:T(4,128)S(1)} %pad_maximum_fusion.2), channel_id=1, source_target_pairs={{0,128},{32,160},{64,192},{96,224},{128,0},{160,32},{192,64},{224,... | collective-permute-start | bytes 6152 | tf_op jit(solution)/shard_map/ppermute | solution.py:278
  110.8 9.4 %collective-permute-start.7 = (f32[8,128]{1,0:T(8,128)S(1)}, f32[8,128]{1,0:T(8,128)S(1)}, u32[]{:S(2)}, u32[]{:S(2)}) collective-permute-start(f32[8,128]{1,0:T(8,128)S(1)} %pad_maximum_fusion.1), channel_id=1, source_target_pairs={{0,256},{32,288},{64,320},{96,352},{128,384},{160,416},{192,448},{... | collective-permute-start | bytes 12296 | tf_op jit(solution)/shard_map/ppermute | solution.py:278

commit v3 on v2

--- a/solution.py
+++ b/solution.py
@@ -108,24 +108,32 @@
     grad_p_ref[...] = jnp.sum(jnp.where(row == column, grad_p, 0.0), axis=0, keepdims=True)
 
 
-def partial_kernel(me_ref, parts_ref, *refs):
-    *hidden_refs, out_ref = refs
+def collect_kernel(me_ref, *refs):
+    *hidden_refs, out_ref, rows_ref = refs
     n_0 = len(hidden_refs)
     capacity = hidden_refs[0].shape[1]
-    total = None
     for k, hidden_ref in enumerate(hidden_refs):
         for j in range(2):
             block = lax.rem(me_ref[0] - k + n_0, n_0) * 2 + (me_ref[1] ^ j)
-            packed = parts_ref[block, 2 * capacity :].astype(F32)
-            halves = jnp.concatenate([packed, pltpu.roll(packed, HALF, 1)]).astype(BF16)
-            scaled = jnp.concatenate(
+            start = pl.multiple_of(block * capacity, capacity)
+            rows_ref[pl.ds(start, capacity)] = hidden_ref[j].astype(F32)
+    out_ref[...] = rows_ref[...].T.astype(BF16)
+
+
+def partial_kernel(hidden_ref, parts_ref, out_ref):
+    team, rows, _ = parts_ref.shape
+    capacity = rows * 2 // 5
+    blocks = []
+    for block in range(team):
+        packed = parts_ref[block, 2 * capacity :].astype(F32)
+        halves = jnp.concatenate([packed, pltpu.roll(packed, HALF, 1)]).astype(BF16)
+        blocks.append(
+            jnp.concatenate(
                 [parts_ref[block, :capacity], parts_ref[block, capacity : 2 * capacity], halves],
                 axis=1,
             )
-            term = lax.dot_general(
-                hidden_ref[j], scaled, (((0,), (0,)), ((), ())), preferred_element_type=F32
-            )
-            total = term if total is None else total + term
+        )
+    total = jnp.dot(hidden_ref[...], jnp.concatenate(blocks), preferred_element_type=F32)
     n = out_ref.shape[0]
     share = total.shape[0] // n
     total = total.reshape(n, share, 3 * LANES)
@@ -167,16 +175,30 @@
         put(2 * third, tile, jnp.where(low, last_0, pltpu.roll(last_1, HALF, 1)))
 
 
-def return_kernel(me_ref, grad_p_ref, presel_ref, expert_ref, slot_ref, out_ref):
+def grads_kernel(scaled_ref, gate_ref, up_ref, weight_ref, grad_gate_ref, grad_up_ref):
+    d_hidden = lax.dot_general(
+        scaled_ref[...], weight_ref[...], (((1,), (1,)), ((), ())), preferred_element_type=F32
+    )
+    gate, up = gate_ref[...].astype(F32), up_ref[...].astype(F32)
+    sigmoid = jax.nn.sigmoid(gate)
+    slope = sigmoid * (1.0 + gate * (1.0 - sigmoid))
+    grad_gate_ref[...] = (d_hidden * up * slope).astype(BF16)
+    grad_up_ref[...] = (d_hidden * (gate * sigmoid)).astype(BF16)
+
+
+def return_kernel(steps, me_ref, grad_p_ref, presel_ref, expert_ref, slot_ref, out_ref):
     n_node = grad_p_ref.shape[0]
     tokens = presel_ref.shape[1]
     expert, slot, presel = expert_ref[...], slot_ref[...], presel_ref[...]
     slots = columns_of_routes(expert, slot, slot + 1)
-    node_ids = lax.broadcasted_iota(jnp.int32, (n_node, tokens), 0)
+    row = lax.broadcasted_iota(jnp.int32, (n_node, tokens), 0)
+    away = jnp.zeros((n_node, tokens), jnp.int32)
+    for bit, step in enumerate(steps):
+        away = jnp.where((row >> bit) & 1 == 1, away | step, away)
     slot_ids = lax.broadcasted_iota(jnp.int32, (LANES, tokens), 0)
     result = jnp.zeros(out_ref.shape, F32)
     for c in range(PRESEL):
-        here = (presel[c : c + 1] ^ me_ref[0]) == node_ids
+        here = (presel[c : c + 1] ^ me_ref[0]) == away
         by_slot = lax.dot_general(
             grad_p_ref[...],
             jnp.where(here, 1.0, 0.0),
@@ -244,6 +266,12 @@
     hiddens = [hidden_pair]
     for k in range(1, n_0):
         hiddens.append(lax.ppermute(hidden_pair, "dp_0", [(i, (i + k) % n_0) for i in range(n_0)]))
+    team_hidden = call(
+        collect_kernel,
+        shape((units, team * capacity), BF16),
+        [SMEM] + [VMEM] * n_0,
+        [pltpu.VMEM((team * capacity, units), F32)],
+    )(jnp.stack([lax.axis_index(a) for a in TEAM]), *hiddens)
     slot_out = jnp.dot(hidden, weight, preferred_element_type=F32)
 
     scaled, parts, grad_p = call(
@@ -257,29 +285,26 @@
     )(recv, slot_out)
     parts = exchange(parts, TEAM)
 
-    d_hidden = lax.dot_general(scaled, weight, (((1,), (1,)), ((), ())), preferred_element_type=F32)
-    grad_gate = (
-        d_hidden * up_rows * sigmoid_gate * (1.0 + gate_rows * (1.0 - sigmoid_gate))
-    ).astype(BF16)
-    grad_up = (d_hidden * activated).astype(BF16)
+    grad_gate, grad_up = call(
+        grads_kernel, [shape((capacity, units), BF16)] * 2, [VMEM] * 4
+    )(scaled, gate_pre, up_pre, weight)
 
     partial = call(
-        partial_kernel,
-        shape((group, 2 * share + 2 * share // 3, LANES), BF16),
-        [SMEM] + [VMEM] * (1 + n_0),
-    )(jnp.stack([lax.axis_index(a) for a in TEAM]), parts, *hiddens)
+        partial_kernel, shape((group, 2 * share + 2 * share // 3, LANES), BF16), [VMEM] * 2
+    )(team_hidden, parts)
     terms = exchange(partial, DP)
     grad_down = call(
         functools.partial(sum_kernel, n_0, n_1), shape((share, features), BF16), [VMEM]
     )(terms)[None]
 
-    step = 1
-    while step < n_node:
+    steps = [n_node >> (i + 1) for i in range(n_node.bit_length() - 1)]
+    for step in steps:
         other = lax.ppermute(grad_p, "node", [(i, i ^ step) for i in range(n_node)])
         grad_p = jnp.concatenate([grad_p, other])
-        step *= 2
     grad_prob = call(
-        return_kernel, shape(route_expert.shape[::-1], F32), [SMEM] + [VMEM] * 4
+        functools.partial(return_kernel, steps),
+        shape(route_expert.shape[::-1], F32),
+        [SMEM] + [VMEM] * 4,
     )(lax.axis_index("node")[None], grad_p, presel, expert, slot).T
     return (grad_gate, grad_up, grad_down, grad_prob)
 

time: 123 us -> 127 us (1.033)
  the two profiles are of different devices: /device:TPU:2 before, /device:TPU:1 now
where the time goes in v3:
time: 127 us; the launch traced here: 126 us
  waiting for transfers between devices  56.4 us (44%)
  starting transfers between devices  52.9 us (42%)
  Pallas kernels  10.6 us (8%)
  matrix products  2.92 us (2%)
  local copies, waits for them, and re-layouts  2.16 us (2%)
    all_to_all x3, waiting for transfers between devices, exchange(): return lax.all_to_all(value, axes, split_axis=0, concat_axis=0, tiled=True)  31.6 us
    all_to_all x3, starting transfers between devices, exchange(): return lax.all_to_all(value, axes, split_axis=0, concat_axis=0, tiled=True)  26 us
    ppermute x4, starting transfers between devices, step_of(): other = lax.ppermute(grad_p, 'node', [(i, i ^ step) for i in range(n_node)])  13 us
    ppermute x4, waiting for transfers between devices, step_of(): other = lax.ppermute(grad_p, 'node', [(i, i ^ step) for i in range(n_node)])  11.5 us
    ppermute x3, starting transfers between devices, step_of(): lax.ppermute(hidden_pair, 'dp_0', [(i, (i + k) % n_0) for i in range(n_0)])  10.5 us
    ppermute x3, waiting for transfers between devices, step_of(): lax.ppermute(hidden_pair, 'dp_0', [(i, (i + k) % n_0) for i in range(n_0)])  7.11 us
    ppermute x1, waiting for transfers between devices, step_of(): near = lax.ppermute(hidden, 'dp_2', [(0, 1), (1, 0)])  6.22 us
    ppermute x1, starting transfers between devices, step_of(): near = lax.ppermute(hidden, 'dp_2', [(0, 1), (1, 0)])  3.36 us
  transfers between devices with their start and end apart: 11, of which 7 were waited for; matrix products, arithmetic and copies ran while one was open for 3% of the time, Pallas kernels for 3%

profile of v3, /device:TPU:1, one launch (start us, length us, event | category | flops | bytes accessed | tf_op | source)
XLA Modules:
  0.0 125.9 jit_solution(9475908386183988136)
XLA Ops:
  0.7 2.8 %shard_map.111 = bf16[256,2688]{1,0:T(8,128)(2,1)} custom-call(bf16[128,2560]{1,0:T(8,128)(2,1)} %refs_0_.1, bf16[6,128]{1,0:T(8,128)(2,1)} %bitcast.30, s32[3,128]{1,0:T(4,128)} %bitcast.23, s32[6,128]{1,0:T(8,128)} %bitcast.19, s32[6,128]{1,0:T(8,128)} %bitcast.21), custom_call_target="tpu_custom_call" | custom-call | tf_op jit(solution)/shard_map/pallas_call | solution.py:248
  3.5 11.8 %all-to-all-start = ((bf16[16,16,2688]{2,1,0:T(8,128)(2,1)}), bf16[16,16,2688]{2,1,0:T(8,128)(2,1)S(1)}, u32[]{:S(2)}, u32[]{:S(2)}) async-start(bf16[16,16,2688]{2,1,0:T(8,128)(2,1)} %bitcast.25), calls=%async_computation | async-start | bytes 2752512 | tf_op jit(solution)/shard_map/all_to_all | solution.py:232
  15.4 2.9 %fusion.5.out_ref = f32[80,2560]{1,0:T(8,128)S(1)} fusion(bf16[80,768]{1,0:T(8,128)(2,1)S(1)} %fusion.4, bf16[1,768,2560]{2,1,0:T(8,128)(2,1)} %param.15), kind=kOutput, calls=%fused_computation.12 | convolution fusion | flops 314572800 | bytes 4874240 | tf_op jit(solution)/shard_map/dot_general | solution.py:275
  18.3 31.6 %all-to-all-done = bf16[16,16,2688]{2,1,0:T(8,128)(2,1)S(1)} async-done(((bf16[16,16,2688]{2,1,0:T(8,128)(2,1)}), bf16[16,16,2688]{2,1,0:T(8,128)(2,1)S(1)}, u32[]{:S(2)}, u32[]{:S(2)}) %all-to-all-start) | async-done | bytes 1376288 | tf_op jit(solution)/shard_map/all_to_all | solution.py:232
  49.9 1.4 %shard_map.112 = (bf16[80,2560]{1,0:T(8,128)(2,1)S(1)}, bf16[8,200,128]{2,1,0:T(8,128)(2,1)}, f32[1,128]{1,0:T(1,128)S(1)}) custom-call(bf16[256,2688]{1,0:T(8,128)(2,1)S(1)} %bitcast.18, f32[80,2560]{1,0:T(8,128)S(1)} %fusion.5.out_ref), custom_call_target="tpu_custom_call" | custom-call | tf_op jit(solution)/shard_map/pallas_call | solution.py:277
  51.3 5.0 %all-to-all-start.1 = ((bf16[8,200,128]{2,1,0:T(8,128)(2,1)}), bf16[8,200,128]{2,1,0:T(8,128)(2,1)S(1)}, u32[]{:S(2)}, u32[]{:S(2)}) async-start(bf16[8,200,128]{2,1,0:T(8,128)(2,1)} %get-tuple-element.12), calls=%async_computation.1 | async-start | bytes 819200 | tf_op jit(solution)/shard_map/all_to_all | solution.py:232
  56.3 3.4 %collective-permute-start = (bf16[80,768]{1,0:T(8,128)(2,1)S(1)}, bf16[80,768]{1,0:T(8,128)(2,1)S(1)}, u32[]{:S(2)}, u32[]{:S(2)}) collective-permute-start(bf16[80,768]{1,0:T(8,128)(2,1)S(1)} %fusion.4), channel_id=1, source_target_pairs={{0,1},{1,0},{2,3},{3,2},{4,5},{5,4},{6,7},{7,6},{8,9},{9,8},{10,11... | collective-permute-start | bytes 368648 | tf_op jit(solution)/shard_map/ppermute | solution.py:264
  59.7 6.2 %collective-permute-done = bf16[80,768]{1,0:T(8,128)(2,1)S(1)} collective-permute-done((bf16[80,768]{1,0:T(8,128)(2,1)S(1)}, bf16[80,768]{1,0:T(8,128)(2,1)S(1)}, u32[]{:S(2)}, u32[]{:S(2)}) %collective-permute-start) | collective-permute-done | bytes 122912 | tf_op jit(solution)/shard_map/ppermute | solution.py:264
  65.9 3.1 %collective-permute-start.1 = (bf16[2,80,768]{2,1,0:T(8,128)(2,1)S(1)}, bf16[2,80,768]{2,1,0:T(8,128)(2,1)S(1)}, u32[]{:S(2)}, u32[]{:S(2)}) collective-permute-start(bf16[2,80,768]{2,1,0:T(8,128)(2,1)S(1)} %pad_maximum_fusion.refs_0_), channel_id=1, source_target_pairs={{0,8},{8,16},{16,24},{24,0},{1,9},{9,17},{17,25},{25,1},{2,10},{10... | collective-permute-start | bytes 737288 | tf_op jit(solution)/shard_map/ppermute | solution.py:268
  69.1 4.3 %collective-permute-start.2 = (bf16[2,80,768]{2,1,0:T(8,128)(2,1)S(1)}, bf16[2,80,768]{2,1,0:T(8,128)(2,1)S(1)}, u32[]{:S(2)}, u32[]{:S(2)}) collective-permute-start(bf16[2,80,768]{2,1,0:T(8,128)(2,1)S(1)} %pad_maximum_fusion.refs_0_), channel_id=1, source_target_pairs={{0,16},{8,24},{16,0},{24,8},{1,17},{9,25},{17,1},{25,9},{2,18},{10... | collective-permute-start | bytes 737288 | tf_op jit(solution)/shard_map/ppermute | solution.py:268
  73.4 3.0 %collective-permute-start.3 = (bf16[2,80,768]{2,1,0:T(8,128)(2,1)S(1)}, bf16[2,80,768]{2,1,0:T(8,128)(2,1)S(1)}, u32[]{:S(2)}, u32[]{:S(2)}) collective-permute-start(bf16[2,80,768]{2,1,0:T(8,128)(2,1)S(1)} %pad_maximum_fusion.refs_0_), channel_id=1, source_target_pairs={{0,24},{8,0},{16,8},{24,16},{1,25},{9,1},{17,9},{25,17},{2,26},{10... | collective-permute-start | bytes 737288 | tf_op jit(solution)/shard_map/ppermute | solution.py:268
  76.5 5.8 %collective-permute-done.2.refs_2_ = bf16[2,80,768]{2,1,0:T(8,128)(2,1)S(1)} collective-permute-done((bf16[2,80,768]{2,1,0:T(8,128)(2,1)S(1)}, bf16[2,80,768]{2,1,0:T(8,128)(2,1)S(1)}, u32[]{:S(2)}, u32[]{:S(2)}) %collective-permute-start.2) | collective-permute-done | bytes 245792 | tf_op jit(solution)/shard_map/ppermute | solution.py:268
  82.4 1.3 %collective-permute-done.3.refs_3_ = bf16[2,80,768]{2,1,0:T(8,128)(2,1)S(1)} collective-permute-done((bf16[2,80,768]{2,1,0:T(8,128)(2,1)S(1)}, bf16[2,80,768]{2,1,0:T(8,128)(2,1)S(1)}, u32[]{:S(2)}, u32[]{:S(2)}) %collective-permute-start.3) | collective-permute-done | bytes 245792 | tf_op jit(solution)/shard_map/ppermute | solution.py:268
  84.7 1.6 %shard_map.115 = bf16[32,64,128]{2,1,0:T(8,128)(2,1)} custom-call(bf16[768,640]{1,0:T(8,128)(2,1)S(1)} %shard_map.114.hidden_ref, bf16[8,200,128]{2,1,0:T(8,128)(2,1)S(1)} %all-to-all-done.1.parts_ref), custom_call_target="tpu_custom_call" | custom-call | tf_op jit(solution)/shard_map/pallas_call | solution.py:292
  86.3 9.1 %all-to-all-start.2 = ((bf16[32,64,128]{2,1,0:T(8,128)(2,1)}), bf16[32,64,128]{2,1,0:T(8,128)(2,1)S(1)}, u32[]{:S(2)}, u32[]{:S(2)}) async-start(bf16[32,64,128]{2,1,0:T(8,128)(2,1)} %shard_map.115), calls=%async_computation.2 | async-start | bytes 1048576 | tf_op jit(solution)/shard_map/all_to_all | solution.py:232
  95.5 2.7 %collective-permute-start.4 = (f32[1,128]{1,0:T(1,128)S(1)}, f32[1,128]{1,0:T(1,128)S(1)}, u32[]{:S(2)}, u32[]{:S(2)}) collective-permute-start(f32[1,128]{1,0:T(1,128)S(1)} %get-tuple-element.13), channel_id=1, source_target_pairs={{0,256},{32,288},{64,320},{96,352},{128,384},{160,416},{192,448},{... | collective-permute-start | bytes 1544 | tf_op jit(solution)/shard_map/ppermute | solution.py:302
  98.2 5.5 %collective-permute-done.4 = f32[1,128]{1,0:T(1,128)S(1)} collective-permute-done((f32[1,128]{1,0:T(1,128)S(1)}, f32[1,128]{1,0:T(1,128)S(1)}, u32[]{:S(2)}, u32[]{:S(2)}) %collective-permute-start.4) | collective-permute-done | bytes 544 | tf_op jit(solution)/shard_map/ppermute | solution.py:302
  103.7 1.9 %collective-permute-start.5 = (f32[2,128]{1,0:T(2,128)S(1)}, f32[2,128]{1,0:T(2,128)S(1)}, u32[]{:S(2)}, u32[]{:S(2)}) collective-permute-start(f32[2,128]{1,0:T(2,128)S(1)} %pad_maximum_fusion.3), channel_id=1, source_target_pairs={{0,128},{32,160},{64,192},{96,224},{128,0},{160,32},{192,64},{224,... | collective-permute-start | bytes 3080 | tf_op jit(solution)/shard_map/ppermute | solution.py:302
  105.6 3.6 %collective-permute-done.5 = f32[2,128]{1,0:T(2,128)S(1)} collective-permute-done((f32[2,128]{1,0:T(2,128)S(1)}, f32[2,128]{1,0:T(2,128)S(1)}, u32[]{:S(2)}, u32[]{:S(2)}) %collective-permute-start.5) | collective-permute-done | bytes 1056 | tf_op jit(solution)/shard_map/ppermute | solution.py:302
  109.2 1.9 %collective-permute-start.6 = (f32[4,128]{1,0:T(4,128)S(1)}, f32[4,128]{1,0:T(4,128)S(1)}, u32[]{:S(2)}, u32[]{:S(2)}) collective-permute-start(f32[4,128]{1,0:T(4,128)S(1)} %pad_maximum_fusion.2), channel_id=1, source_target_pairs={{0,64},{32,96},{64,0},{96,32},{128,192},{160,224},{192,128},{224,1... | collective-permute-start | bytes 6152 | tf_op jit(solution)/shard_map/ppermute | solution.py:302
  111.1 2.4 %collective-permute-done.6 = f32[4,128]{1,0:T(4,128)S(1)} collective-permute-done((f32[4,128]{1,0:T(4,128)S(1)}, f32[4,128]{1,0:T(4,128)S(1)}, u32[]{:S(2)}, u32[]{:S(2)}) %collective-permute-start.6) | collective-permute-done | bytes 2080 | tf_op jit(solution)/shard_map/ppermute | solution.py:302
  113.5 6.5 %collective-permute-start.7 = (f32[8,128]{1,0:T(8,128)S(1)}, f32[8,128]{1,0:T(8,128)S(1)}, u32[]{:S(2)}, u32[]{:S(2)}) collective-permute-start(f32[8,128]{1,0:T(8,128)S(1)} %pad_maximum_fusion.1), channel_id=1, source_target_pairs={{0,32},{32,0},{64,96},{96,64},{128,160},{160,128},{192,224},{224,1... | collective-permute-start | bytes 12296 | tf_op jit(solution)/shard_map/ppermute | solution.py:302
  120.1 2.1 %copy-done = bf16[1,768,2560]{2,1,0:T(8,128)(2,1)S(1)} copy-done((bf16[1,768,2560]{2,1,0:T(8,128)(2,1)S(1)}, bf16[1,768,2560]{2,1,0:T(8,128)(2,1)}, u32[]{:S(2)}) %copy-start) | copy-done | bytes 3932184
  122.2 2.0 %shard_map.113 = (bf16[80,768]{1,0:T(8,128)(2,1)}, bf16[80,768]{1,0:T(8,128)(2,1)}) custom-call(bf16[80,2560]{1,0:T(8,128)(2,1)S(1)} %get-tuple-element.9.scaled_ref, bf16[80,768]{1,0:T(8,128)(2,1)S(1)} %copy-done.2, bf16[80,768]{1,0:T(8,128)(2,1)S(1)} %copy-done.1, bf16[768,2560]{1,0:T(8,128)(2,1)S(1)} %bitcast.17), custom_call_target="tpu_custom_call" | custom-call | tf_op jit(solution)/shard_map/pallas_call | solution.py:288
  (25 shorter events, 3.0 us)
Async XLA Ops:
  0.6 14.7 %copy-start.2 = (bf16[80,768]{1,0:T(8,128)(2,1)S(1)}, bf16[80,768]{1,0:T(8,128)(2,1)}, u32[]{:S(2)}) copy-start(bf16[80,768]{1,0:T(8,128)(2,1)} %gate_ref.1) | copy-start | bytes 368644
  0.6 14.7 %copy-start.1 = (bf16[80,768]{1,0:T(8,128)(2,1)S(1)}, bf16[80,768]{1,0:T(8,128)(2,1)}, u32[]{:S(2)}) copy-start(bf16[80,768]{1,0:T(8,128)(2,1)} %up_ref.1) | copy-start | bytes 368644
  3.5 46.4 %all-to-all-start = ((bf16[16,16,2688]{2,1,0:T(8,128)(2,1)}), bf16[16,16,2688]{2,1,0:T(8,128)(2,1)S(1)}, u32[]{:S(2)}, u32[]{:S(2)}) async-start(bf16[16,16,2688]{2,1,0:T(8,128)(2,1)} %bitcast.25), calls=%async_computation | async-start | bytes 2752512 | tf_op jit(solution)/shard_map/all_to_all | solution.py:232
  51.3 33.4 %all-to-all-start.1 = ((bf16[8,200,128]{2,1,0:T(8,128)(2,1)}), bf16[8,200,128]{2,1,0:T(8,128)(2,1)S(1)}, u32[]{:S(2)}, u32[]{:S(2)}) async-start(bf16[8,200,128]{2,1,0:T(8,128)(2,1)} %get-tuple-element.12), calls=%async_computation.1 | async-start | bytes 819200 | tf_op jit(solution)/shard_map/all_to_all | solution.py:232
  56.3 9.6 %collective-permute-start = (bf16[80,768]{1,0:T(8,128)(2,1)S(1)}, bf16[80,768]{1,0:T(8,128)(2,1)S(1)}, u32[]{:S(2)}, u32[]{:S(2)}) collective-permute-start(bf16[80,768]{1,0:T(8,128)(2,1)S(1)} %fusion.4), channel_id=1, source_target_pairs={{0,1},{1,0},{2,3},{3,2},{4,5},{5,4},{6,7},{7,6},{8,9},{9,8},{10,11... | collective-permute-start | bytes 368648 | tf_op jit(solution)/shard_map/ppermute | solution.py:264
  65.9 10.6 %collective-permute-start.1 = (bf16[2,80,768]{2,1,0:T(8,128)(2,1)S(1)}, bf16[2,80,768]{2,1,0:T(8,128)(2,1)S(1)}, u32[]{:S(2)}, u32[]{:S(2)}) collective-permute-start(bf16[2,80,768]{2,1,0:T(8,128)(2,1)S(1)} %pad_maximum_fusion.refs_0_), channel_id=1, source_target_pairs={{0,8},{8,16},{16,24},{24,0},{1,9},{9,17},{17,25},{25,1},{2,10},{10... | collective-permute-start | bytes 737288 | tf_op jit(solution)/shard_map/ppermute | solution.py:268
  69.1 13.3 %collective-permute-start.2 = (bf16[2,80,768]{2,1,0:T(8,128)(2,1)S(1)}, bf16[2,80,768]{2,1,0:T(8,128)(2,1)S(1)}, u32[]{:S(2)}, u32[]{:S(2)}) collective-permute-start(bf16[2,80,768]{2,1,0:T(8,128)(2,1)S(1)} %pad_maximum_fusion.refs_0_), channel_id=1, source_target_pairs={{0,16},{8,24},{16,0},{24,8},{1,17},{9,25},{17,1},{25,9},{2,18},{10... | collective-permute-start | bytes 737288 | tf_op jit(solution)/shard_map/ppermute | solution.py:268
  73.4 10.2 %collective-permute-start.3 = (bf16[2,80,768]{2,1,0:T(8,128)(2,1)S(1)}, bf16[2,80,768]{2,1,0:T(8,128)(2,1)S(1)}, u32[]{:S(2)}, u32[]{:S(2)}) collective-permute-start(bf16[2,80,768]{2,1,0:T(8,128)(2,1)S(1)} %pad_maximum_fusion.refs_0_), channel_id=1, source_target_pairs={{0,24},{8,0},{16,8},{24,16},{1,25},{9,1},{17,9},{25,17},{2,26},{10... | collective-permute-start | bytes 737288 | tf_op jit(solution)/shard_map/ppermute | solution.py:268
  84.7 39.5 %copy-start.3 = (s32[128,6]{0,1:T(8,128)S(1)}, s32[128,6]{0,1:T(8,128)}, u32[]{:S(2)}) copy-start(s32[128,6]{0,1:T(8,128)} %param.11) | copy-start | bytes 9220
  84.7 39.5 %copy-start.4 = (s32[128,6]{0,1:T(8,128)S(1)}, s32[128,6]{0,1:T(8,128)}, u32[]{:S(2)}) copy-start(s32[128,6]{0,1:T(8,128)} %param.12) | copy-start | bytes 9220
  84.7 39.5 %copy-start.5 = (s32[128,3]{0,1:T(4,128)S(1)}, s32[128,3]{0,1:T(4,128)}, u32[]{:S(2)}) copy-start(s32[128,3]{0,1:T(4,128)} %param.10) | copy-start | bytes 4612
  86.3 38.9 %all-to-all-start.2 = ((bf16[32,64,128]{2,1,0:T(8,128)(2,1)}), bf16[32,64,128]{2,1,0:T(8,128)(2,1)S(1)}, u32[]{:S(2)}, u32[]{:S(2)}) async-start(bf16[32,64,128]{2,1,0:T(8,128)(2,1)} %shard_map.115), calls=%async_computation.2 | async-start | bytes 1048576 | tf_op jit(solution)/shard_map/all_to_all | solution.py:232
  95.5 8.2 %collective-permute-start.4 = (f32[1,128]{1,0:T(1,128)S(1)}, f32[1,128]{1,0:T(1,128)S(1)}, u32[]{:S(2)}, u32[]{:S(2)}) collective-permute-start(f32[1,128]{1,0:T(1,128)S(1)} %get-tuple-element.13), channel_id=1, source_target_pairs={{0,256},{32,288},{64,320},{96,352},{128,384},{160,416},{192,448},{... | collective-permute-start | bytes 1544 | tf_op jit(solution)/shard_map/ppermute | solution.py:302
  103.7 5.5 %collective-permute-start.5 = (f32[2,128]{1,0:T(2,128)S(1)}, f32[2,128]{1,0:T(2,128)S(1)}, u32[]{:S(2)}, u32[]{:S(2)}) collective-permute-start(f32[2,128]{1,0:T(2,128)S(1)} %pad_maximum_fusion.3), channel_id=1, source_target_pairs={{0,128},{32,160},{64,192},{96,224},{128,0},{160,32},{192,64},{224,... | collective-permute-start | bytes 3080 | tf_op jit(solution)/shard_map/ppermute | solution.py:302
  109.2 4.3 %collective-permute-start.6 = (f32[4,128]{1,0:T(4,128)S(1)}, f32[4,128]{1,0:T(4,128)S(1)}, u32[]{:S(2)}, u32[]{:S(2)}) collective-permute-start(f32[4,128]{1,0:T(4,128)S(1)} %pad_maximum_fusion.2), channel_id=1, source_target_pairs={{0,64},{32,96},{64,0},{96,32},{128,192},{160,224},{192,128},{224,1... | collective-permute-start | bytes 6152 | tf_op jit(solution)/shard_map/ppermute | solution.py:302
  113.5 10.6 %collective-permute-start.7 = (f32[8,128]{1,0:T(8,128)S(1)}, f32[8,128]{1,0:T(8,128)S(1)}, u32[]{:S(2)}, u32[]{:S(2)}) collective-permute-start(f32[8,128]{1,0:T(8,128)S(1)} %pad_maximum_fusion.1), channel_id=1, source_target_pairs={{0,32},{32,0},{64,96},{96,64},{128,160},{160,128},{192,224},{224,1... | collective-permute-start | bytes 12296 | tf_op jit(solution)/shard_map/ppermute | solution.py:302
  120.0 2.1 %copy-start = (bf16[1,768,2560]{2,1,0:T(8,128)(2,1)S(1)}, bf16[1,768,2560]{2,1,0:T(8,128)(2,1)}, u32[]{:S(2)}) copy-start(bf16[1,768,2560]{2,1,0:T(8,128)(2,1)} %param.15) | copy-start | bytes 11796484

commit v4 on v3

--- a/solution.py
+++ b/solution.py
@@ -16,6 +16,8 @@
 NODE_DP = ("node", *DP)
 TEAM = ("dp_0", "dp_2")
 HALF = LANES // 2
+PIECES = 3
+OUT_PIECES = 4
 F32 = jnp.float32
 BF16 = jnp.bfloat16
 
@@ -29,7 +31,7 @@
 
 
 def route_kernel(*refs):
-    sources, send_ref, held, arrived = refs[:5], refs[5], refs[6:11], refs[11]
+    sources, out_ref, held, (send_ref, arrived, left) = refs[:5], refs[5], refs[6:11], refs[11:14]
     copies = [
         pltpu.make_async_copy(source, place, arrived.at[i])
         for i, (source, place) in enumerate(zip(sources, held))
@@ -71,7 +73,17 @@
     send_ref[:, features:] = info.reshape(rows, LANES).astype(BF16)
     pick = jnp.where(picked, 1.0, 0.0).reshape(rows, tokens).astype(BF16)
     copies[0].wait()
-    send_ref[:, :features] = jnp.dot(pick, og_ref[...], preferred_element_type=F32).astype(BF16)
+    leaving = []
+    piece = rows // OUT_PIECES
+    for i in range(OUT_PIECES):
+        some = slice(i * piece, (i + 1) * piece)
+        send_ref[some, :features] = jnp.dot(
+            pick[some], og_ref[...], preferred_element_type=F32
+        ).astype(BF16)
+        leaving.append(pltpu.make_async_copy(send_ref.at[some], out_ref.at[some], left.at[i]))
+        leaving[-1].start()
+    for copy in leaving:
+        copy.wait()
 
 
 def land_kernel(recv_ref, out_ref, scaled_ref, parts_ref, grad_p_ref):
@@ -175,15 +187,38 @@
         put(2 * third, tile, jnp.where(low, last_0, pltpu.roll(last_1, HALF, 1)))
 
 
-def grads_kernel(scaled_ref, gate_ref, up_ref, weight_ref, grad_gate_ref, grad_up_ref):
-    d_hidden = lax.dot_general(
-        scaled_ref[...], weight_ref[...], (((1,), (1,)), ((), ())), preferred_element_type=F32
-    )
-    gate, up = gate_ref[...].astype(F32), up_ref[...].astype(F32)
-    sigmoid = jax.nn.sigmoid(gate)
-    slope = sigmoid * (1.0 + gate * (1.0 - sigmoid))
-    grad_gate_ref[...] = (d_hidden * up * slope).astype(BF16)
-    grad_up_ref[...] = (d_hidden * (gate * sigmoid)).astype(BF16)
+def grads_kernel(*refs):
+    sources, grad_gate_ref, grad_up_ref = refs[:4], refs[4], refs[5]
+    (scaled_ref, gate_ref, up_ref, weight_ref), arrived = refs[6:10], refs[10]
+    copies = [
+        pltpu.make_async_copy(source, place, arrived.at[i])
+        for i, (source, place) in enumerate(zip(sources[:3], refs[6:9]))
+    ]
+    units = weight_ref.shape[0]
+    piece = units // PIECES
+    for i in range(PIECES):
+        rows = pl.ds(i * piece, piece)
+        copies.append(
+            pltpu.make_async_copy(sources[3].at[rows], weight_ref.at[rows], arrived.at[3 + i])
+        )
+    for copy in copies:
+        copy.start()
+    for copy in copies[:3]:
+        copy.wait()
+    for i in range(PIECES):
+        copies[3 + i].wait()
+        rows = slice(i * piece, (i + 1) * piece)
+        d_hidden = lax.dot_general(
+            scaled_ref[...],
+            weight_ref[rows],
+            (((1,), (1,)), ((), ())),
+            preferred_element_type=F32,
+        )
+        gate, up = gate_ref[:, rows].astype(F32), up_ref[:, rows].astype(F32)
+        sigmoid = jax.nn.sigmoid(gate)
+        slope = sigmoid * (1.0 + gate * (1.0 - sigmoid))
+        grad_gate_ref[:, rows] = (d_hidden * up * slope).astype(BF16)
+        grad_up_ref[:, rows] = (d_hidden * (gate * sigmoid)).astype(BF16)
 
 
 def return_kernel(steps, me_ref, grad_p_ref, presel_ref, expert_ref, slot_ref, out_ref):
@@ -216,13 +251,13 @@
 SMEM = pl.BlockSpec(memory_space=pltpu.SMEM)
 
 
-def call(kernel, out_shape, in_specs, scratch=(), vmem_mib=12):
+def call(kernel, out_shape, in_specs, scratch=(), vmem_mib=12, out_space=VMEM):
     many = isinstance(out_shape, (tuple, list))
     return pl.pallas_call(
         kernel,
         out_shape=out_shape,
         in_specs=in_specs,
-        out_specs=[VMEM] * len(out_shape) if many else VMEM,
+        out_specs=[out_space] * len(out_shape) if many else out_space,
         scratch_shapes=scratch,
         compiler_params=pltpu.CompilerParams(vmem_limit_bytes=vmem_mib << 20),
     )
@@ -249,7 +284,10 @@
         route_kernel,
         shape((n_node * SRC_CAP, features + LANES), BF16),
         [HBM] * 5,
-        [pltpu.VMEM(a.shape, a.dtype) for a in routed] + [pltpu.SemaphoreType.DMA((5,))],
+        [pltpu.VMEM(a.shape, a.dtype) for a in routed]
+        + [pltpu.VMEM((n_node * SRC_CAP, features + LANES), BF16)]
+        + [pltpu.SemaphoreType.DMA((5,)), pltpu.SemaphoreType.DMA((OUT_PIECES,))],
+        out_space=HBM,
         vmem_mib=60,
     )(*routed)
     recv = exchange(send.reshape(n_node, SRC_CAP, features + LANES), "node")
@@ -277,17 +315,23 @@
     scaled, parts, grad_p = call(
         land_kernel,
         [
-            shape((capacity, features), BF16),
-            shape((team, features * capacity // (team * LANES), LANES), BF16),
+            pltpu.HBM((capacity, features), BF16),
+            pltpu.HBM((team, features * capacity // (team * LANES), LANES), BF16),
             shape((1, LANES), F32),
         ],
         [VMEM] * 2,
     )(recv, slot_out)
     parts = exchange(parts, TEAM)
 
+    sources = (scaled, gate_pre, up_pre, weight)
     grad_gate, grad_up = call(
-        grads_kernel, [shape((capacity, units), BF16)] * 2, [VMEM] * 4
-    )(scaled, gate_pre, up_pre, weight)
+        grads_kernel,
+        [shape((capacity, units), BF16)] * 2,
+        [HBM] * 4,
+        [pltpu.VMEM(a.shape, a.dtype) for a in sources]
+        + [pltpu.SemaphoreType.DMA((3 + PIECES,))],
+        vmem_mib=60,
+    )(*sources)
 
     partial = call(
         partial_kernel, shape((group, 2 * share + 2 * share // 3, LANES), BF16), [VMEM] * 2

time: 127 us -> 127 us (level)
  Pallas kernels: 10.6 us -> 12.8 us
  local copies, waits for them, and re-layouts: 2.16 us -> 0.06 us
    pallas_call x2, Pallas kernels: 3.42 us -> 5.93 us  [the longest x1 4.46 us: step_of(): call(grads_kernel, [shape((capacity, units), BF16)] * 2, [HBM] * 4, [pltp...]
    unnamed x12 -> x10, local copies, waits for them, and re-layouts: 2.14 us -> 0.03 us
  transfers between devices with their start and end apart: 11 -> 11, of which waited for: 7 -> 7; matrix products, arithmetic and copies ran while one was open for 3% -> 2% of each run, Pallas kernels for 3% -> 5%
where the time goes in v4:
time: 127 us; the launch traced here: 126 us
  waiting for transfers between devices  56.4 us (44%)
  starting transfers between devices  52.9 us (42%)
  Pallas kernels  12.8 us (10%)
  matrix products  2.92 us (2%)
    all_to_all x3, waiting for transfers between devices, exchange(): return lax.all_to_all(value, axes, split_axis=0, concat_axis=0, tiled=True)  31.6 us
    all_to_all x3, starting transfers between devices, exchange(): return lax.all_to_all(value, axes, split_axis=0, concat_axis=0, tiled=True)  26 us
    ppermute x4, starting transfers between devices, step_of(): other = lax.ppermute(grad_p, 'node', [(i, i ^ step) for i in range(n_node)])  13 us
    ppermute x4, waiting for transfers between devices, step_of(): other = lax.ppermute(grad_p, 'node', [(i, i ^ step) for i in range(n_node)])  11.5 us
    ppermute x3, starting transfers between devices, step_of(): lax.ppermute(hidden_pair, 'dp_0', [(i, (i + k) % n_0) for i in range(n_0)])  10.5 us
    ppermute x3, waiting for transfers between devices, step_of(): lax.ppermute(hidden_pair, 'dp_0', [(i, (i + k) % n_0) for i in range(n_0)])  7.11 us
    ppermute x1, waiting for transfers between devices, step_of(): near = lax.ppermute(hidden, 'dp_2', [(0, 1), (1, 0)])  6.21 us
    pallas_call x1, Pallas kernels, step_of(): call(grads_kernel, [shape((capacity, units), BF16)] * 2, [HBM] * 4, [pltp...  4.46 us
  transfers between devices with their start and end apart: 11, of which 7 were waited for; matrix products, arithmetic and copies ran while one was open for 2% of the time, Pallas kernels for 5%

profile of v4, /device:TPU:1, one launch (start us, length us, event | category | flops | bytes accessed | tf_op | source)
XLA Modules:
  0.0 126.1 jit_solution(5461585758743260701)
XLA Ops:
  0.7 2.6 %shard_map.111 = bf16[256,2688]{1,0:T(8,128)(2,1)} custom-call(bf16[128,2560]{1,0:T(8,128)(2,1)} %refs_0_.1, bf16[6,128]{1,0:T(8,128)(2,1)} %bitcast.30, s32[3,128]{1,0:T(4,128)} %bitcast.22, s32[6,128]{1,0:T(8,128)} %bitcast.18, s32[6,128]{1,0:T(8,128)} %bitcast.20), custom_call_target="tpu_custom_call" | custom-call | tf_op jit(solution)/shard_map/pallas_call | solution.py:283
  3.3 11.8 %all-to-all-start = ((bf16[16,16,2688]{2,1,0:T(8,128)(2,1)}), bf16[16,16,2688]{2,1,0:T(8,128)(2,1)S(1)}, u32[]{:S(2)}, u32[]{:S(2)}) async-start(bf16[16,16,2688]{2,1,0:T(8,128)(2,1)} %bitcast.25), calls=%async_computation | async-start | bytes 2752512 | tf_op jit(solution)/shard_map/all_to_all | solution.py:267
  15.2 2.9 %fusion.5.out_ref = f32[80,2560]{1,0:T(8,128)S(1)} fusion(bf16[80,768]{1,0:T(8,128)(2,1)S(1)} %fusion.4, bf16[1,768,2560]{2,1,0:T(8,128)(2,1)} %param.15), kind=kOutput, calls=%fused_computation.12 | convolution fusion | flops 314572800 | bytes 4874240 | tf_op jit(solution)/shard_map/dot_general | solution.py:313
  18.1 31.6 %all-to-all-done = bf16[16,16,2688]{2,1,0:T(8,128)(2,1)S(1)} async-done(((bf16[16,16,2688]{2,1,0:T(8,128)(2,1)}), bf16[16,16,2688]{2,1,0:T(8,128)(2,1)S(1)}, u32[]{:S(2)}, u32[]{:S(2)}) %all-to-all-start) | async-done | bytes 1376288 | tf_op jit(solution)/shard_map/all_to_all | solution.py:267
  49.7 1.5 %shard_map.112 = (bf16[80,2560]{1,0:T(8,128)(2,1)}, bf16[8,200,128]{2,1,0:T(8,128)(2,1)}, f32[1,128]{1,0:T(1,128)S(1)}) custom-call(bf16[256,2688]{1,0:T(8,128)(2,1)S(1)} %bitcast.17, f32[80,2560]{1,0:T(8,128)S(1)} %fusion.5.out_ref), custom_call_target="tpu_custom_call" | custom-call | tf_op jit(solution)/shard_map/pallas_call | solution.py:315
  51.1 5.0 %all-to-all-start.1 = ((bf16[8,200,128]{2,1,0:T(8,128)(2,1)}), bf16[8,200,128]{2,1,0:T(8,128)(2,1)S(1)}, u32[]{:S(2)}, u32[]{:S(2)}) async-start(bf16[8,200,128]{2,1,0:T(8,128)(2,1)} %get-tuple-element.12), calls=%async_computation.1 | async-start | bytes 819200 | tf_op jit(solution)/shard_map/all_to_all | solution.py:267
  56.2 3.4 %collective-permute-start = (bf16[80,768]{1,0:T(8,128)(2,1)S(1)}, bf16[80,768]{1,0:T(8,128)(2,1)S(1)}, u32[]{:S(2)}, u32[]{:S(2)}) collective-permute-start(bf16[80,768]{1,0:T(8,128)(2,1)S(1)} %fusion.4), channel_id=1, source_target_pairs={{0,1},{1,0},{2,3},{3,2},{4,5},{5,4},{6,7},{7,6},{8,9},{9,8},{10,11... | collective-permute-start | bytes 368648 | tf_op jit(solution)/shard_map/ppermute | solution.py:302
  59.5 6.2 %collective-permute-done = bf16[80,768]{1,0:T(8,128)(2,1)S(1)} collective-permute-done((bf16[80,768]{1,0:T(8,128)(2,1)S(1)}, bf16[80,768]{1,0:T(8,128)(2,1)S(1)}, u32[]{:S(2)}, u32[]{:S(2)}) %collective-permute-start) | collective-permute-done | bytes 122912 | tf_op jit(solution)/shard_map/ppermute | solution.py:302
  65.8 3.1 %collective-permute-start.1 = (bf16[2,80,768]{2,1,0:T(8,128)(2,1)S(1)}, bf16[2,80,768]{2,1,0:T(8,128)(2,1)S(1)}, u32[]{:S(2)}, u32[]{:S(2)}) collective-permute-start(bf16[2,80,768]{2,1,0:T(8,128)(2,1)S(1)} %pad_maximum_fusion.refs_0_), channel_id=1, source_target_pairs={{0,8},{8,16},{16,24},{24,0},{1,9},{9,17},{17,25},{25,1},{2,10},{10... | collective-permute-start | bytes 737288 | tf_op jit(solution)/shard_map/ppermute | solution.py:306
  68.9 4.3 %collective-permute-start.2 = (bf16[2,80,768]{2,1,0:T(8,128)(2,1)S(1)}, bf16[2,80,768]{2,1,0:T(8,128)(2,1)S(1)}, u32[]{:S(2)}, u32[]{:S(2)}) collective-permute-start(bf16[2,80,768]{2,1,0:T(8,128)(2,1)S(1)} %pad_maximum_fusion.refs_0_), channel_id=1, source_target_pairs={{0,16},{8,24},{16,0},{24,8},{1,17},{9,25},{17,1},{25,9},{2,18},{10... | collective-permute-start | bytes 737288 | tf_op jit(solution)/shard_map/ppermute | solution.py:306
  73.2 3.0 %collective-permute-start.3 = (bf16[2,80,768]{2,1,0:T(8,128)(2,1)S(1)}, bf16[2,80,768]{2,1,0:T(8,128)(2,1)S(1)}, u32[]{:S(2)}, u32[]{:S(2)}) collective-permute-start(bf16[2,80,768]{2,1,0:T(8,128)(2,1)S(1)} %pad_maximum_fusion.refs_0_), channel_id=1, source_target_pairs={{0,24},{8,0},{16,8},{24,16},{1,25},{9,1},{17,9},{25,17},{2,26},{10... | collective-permute-start | bytes 737288 | tf_op jit(solution)/shard_map/ppermute | solution.py:306
  76.4 5.8 %collective-permute-done.2.refs_2_ = bf16[2,80,768]{2,1,0:T(8,128)(2,1)S(1)} collective-permute-done((bf16[2,80,768]{2,1,0:T(8,128)(2,1)S(1)}, bf16[2,80,768]{2,1,0:T(8,128)(2,1)S(1)}, u32[]{:S(2)}, u32[]{:S(2)}) %collective-permute-start.2) | collective-permute-done | bytes 245792 | tf_op jit(solution)/shard_map/ppermute | solution.py:306
  82.2 1.3 %collective-permute-done.3.refs_3_ = bf16[2,80,768]{2,1,0:T(8,128)(2,1)S(1)} collective-permute-done((bf16[2,80,768]{2,1,0:T(8,128)(2,1)S(1)}, bf16[2,80,768]{2,1,0:T(8,128)(2,1)S(1)}, u32[]{:S(2)}, u32[]{:S(2)}) %collective-permute-start.3) | collective-permute-done | bytes 245792 | tf_op jit(solution)/shard_map/ppermute | solution.py:306
  83.5 1.0 shard_map.114.hidden_ref
  84.5 1.6 %shard_map.115 = bf16[32,64,128]{2,1,0:T(8,128)(2,1)} custom-call(bf16[768,640]{1,0:T(8,128)(2,1)S(1)} %shard_map.114.hidden_ref, bf16[8,200,128]{2,1,0:T(8,128)(2,1)S(1)} %all-to-all-done.1.parts_ref), custom_call_target="tpu_custom_call" | custom-call | tf_op jit(solution)/shard_map/pallas_call | solution.py:336
  86.1 9.1 %all-to-all-start.2 = ((bf16[32,64,128]{2,1,0:T(8,128)(2,1)}), bf16[32,64,128]{2,1,0:T(8,128)(2,1)S(1)}, u32[]{:S(2)}, u32[]{:S(2)}) async-start(bf16[32,64,128]{2,1,0:T(8,128)(2,1)} %shard_map.115), calls=%async_computation.2 | async-start | bytes 1048576 | tf_op jit(solution)/shard_map/all_to_all | solution.py:267
  95.3 2.7 %collective-permute-start.4 = (f32[1,128]{1,0:T(1,128)S(1)}, f32[1,128]{1,0:T(1,128)S(1)}, u32[]{:S(2)}, u32[]{:S(2)}) collective-permute-start(f32[1,128]{1,0:T(1,128)S(1)} %get-tuple-element.13), channel_id=1, source_target_pairs={{0,256},{32,288},{64,320},{96,352},{128,384},{160,416},{192,448},{... | collective-permute-start | bytes 1544 | tf_op jit(solution)/shard_map/ppermute | solution.py:346
  98.0 5.5 %collective-permute-done.4 = f32[1,128]{1,0:T(1,128)S(1)} collective-permute-done((f32[1,128]{1,0:T(1,128)S(1)}, f32[1,128]{1,0:T(1,128)S(1)}, u32[]{:S(2)}, u32[]{:S(2)}) %collective-permute-start.4) | collective-permute-done | bytes 544 | tf_op jit(solution)/shard_map/ppermute | solution.py:346
  103.5 1.9 %collective-permute-start.5 = (f32[2,128]{1,0:T(2,128)S(1)}, f32[2,128]{1,0:T(2,128)S(1)}, u32[]{:S(2)}, u32[]{:S(2)}) collective-permute-start(f32[2,128]{1,0:T(2,128)S(1)} %pad_maximum_fusion.3), channel_id=1, source_target_pairs={{0,128},{32,160},{64,192},{96,224},{128,0},{160,32},{192,64},{224,... | collective-permute-start | bytes 3080 | tf_op jit(solution)/shard_map/ppermute | solution.py:346
  105.4 3.6 %collective-permute-done.5 = f32[2,128]{1,0:T(2,128)S(1)} collective-permute-done((f32[2,128]{1,0:T(2,128)S(1)}, f32[2,128]{1,0:T(2,128)S(1)}, u32[]{:S(2)}, u32[]{:S(2)}) %collective-permute-start.5) | collective-permute-done | bytes 1056 | tf_op jit(solution)/shard_map/ppermute | solution.py:346
  109.0 1.9 %collective-permute-start.6 = (f32[4,128]{1,0:T(4,128)S(1)}, f32[4,128]{1,0:T(4,128)S(1)}, u32[]{:S(2)}, u32[]{:S(2)}) collective-permute-start(f32[4,128]{1,0:T(4,128)S(1)} %pad_maximum_fusion.2), channel_id=1, source_target_pairs={{0,64},{32,96},{64,0},{96,32},{128,192},{160,224},{192,128},{224,1... | collective-permute-start | bytes 6152 | tf_op jit(solution)/shard_map/ppermute | solution.py:346
  111.0 2.4 %collective-permute-done.6 = f32[4,128]{1,0:T(4,128)S(1)} collective-permute-done((f32[4,128]{1,0:T(4,128)S(1)}, f32[4,128]{1,0:T(4,128)S(1)}, u32[]{:S(2)}, u32[]{:S(2)}) %collective-permute-start.6) | collective-permute-done | bytes 2080 | tf_op jit(solution)/shard_map/ppermute | solution.py:346
  113.4 6.5 %collective-permute-start.7 = (f32[8,128]{1,0:T(8,128)S(1)}, f32[8,128]{1,0:T(8,128)S(1)}, u32[]{:S(2)}, u32[]{:S(2)}) collective-permute-start(f32[8,128]{1,0:T(8,128)S(1)} %pad_maximum_fusion.1), channel_id=1, source_target_pairs={{0,32},{32,0},{64,96},{96,64},{128,160},{160,128},{192,224},{224,1... | collective-permute-start | bytes 12296 | tf_op jit(solution)/shard_map/ppermute | solution.py:346
  119.9 4.5 %shard_map.113 = (bf16[80,768]{1,0:T(8,128)(2,1)}, bf16[80,768]{1,0:T(8,128)(2,1)}) custom-call(bf16[80,2560]{1,0:T(8,128)(2,1)} %get-tuple-element.9.refs_0_, bf16[80,768]{1,0:T(8,128)(2,1)} %refs_1_.1, bf16[80,768]{1,0:T(8,128)(2,1)} %refs_2_.1, bf16[768,2560]{1,0:T(8,128)(2,1)} %bitcast.24), custom_call_target="tpu_custom_call" | custom-call | tf_op jit(solution)/shard_map/pallas_call | solution.py:327
  (23 shorter events, 2.0 us)
Async XLA Ops:
  0.6 14.5 %copy-start.4 = (bf16[80,768]{1,0:T(8,128)(2,1)S(1)}, bf16[80,768]{1,0:T(8,128)(2,1)}, u32[]{:S(2)}) copy-start(bf16[80,768]{1,0:T(8,128)(2,1)} %refs_1_.1) | copy-start | bytes 368644
  0.6 14.5 %copy-start.3 = (bf16[80,768]{1,0:T(8,128)(2,1)S(1)}, bf16[80,768]{1,0:T(8,128)(2,1)}, u32[]{:S(2)}) copy-start(bf16[80,768]{1,0:T(8,128)(2,1)} %refs_2_.1) | copy-start | bytes 368644
  3.3 46.4 %all-to-all-start = ((bf16[16,16,2688]{2,1,0:T(8,128)(2,1)}), bf16[16,16,2688]{2,1,0:T(8,128)(2,1)S(1)}, u32[]{:S(2)}, u32[]{:S(2)}) async-start(bf16[16,16,2688]{2,1,0:T(8,128)(2,1)} %bitcast.25), calls=%async_computation | async-start | bytes 2752512 | tf_op jit(solution)/shard_map/all_to_all | solution.py:267
  51.1 33.4 %all-to-all-start.1 = ((bf16[8,200,128]{2,1,0:T(8,128)(2,1)}), bf16[8,200,128]{2,1,0:T(8,128)(2,1)S(1)}, u32[]{:S(2)}, u32[]{:S(2)}) async-start(bf16[8,200,128]{2,1,0:T(8,128)(2,1)} %get-tuple-element.12), calls=%async_computation.1 | async-start | bytes 819200 | tf_op jit(solution)/shard_map/all_to_all | solution.py:267
  56.2 9.6 %collective-permute-start = (bf16[80,768]{1,0:T(8,128)(2,1)S(1)}, bf16[80,768]{1,0:T(8,128)(2,1)S(1)}, u32[]{:S(2)}, u32[]{:S(2)}) collective-permute-start(bf16[80,768]{1,0:T(8,128)(2,1)S(1)} %fusion.4), channel_id=1, source_target_pairs={{0,1},{1,0},{2,3},{3,2},{4,5},{5,4},{6,7},{7,6},{8,9},{9,8},{10,11... | collective-permute-start | bytes 368648 | tf_op jit(solution)/shard_map/ppermute | solution.py:302
  65.8 10.6 %collective-permute-start.1 = (bf16[2,80,768]{2,1,0:T(8,128)(2,1)S(1)}, bf16[2,80,768]{2,1,0:T(8,128)(2,1)S(1)}, u32[]{:S(2)}, u32[]{:S(2)}) collective-permute-start(bf16[2,80,768]{2,1,0:T(8,128)(2,1)S(1)} %pad_maximum_fusion.refs_0_), channel_id=1, source_target_pairs={{0,8},{8,16},{16,24},{24,0},{1,9},{9,17},{17,25},{25,1},{2,10},{10... | collective-permute-start | bytes 737288 | tf_op jit(solution)/shard_map/ppermute | solution.py:306
  68.9 13.3 %collective-permute-start.2 = (bf16[2,80,768]{2,1,0:T(8,128)(2,1)S(1)}, bf16[2,80,768]{2,1,0:T(8,128)(2,1)S(1)}, u32[]{:S(2)}, u32[]{:S(2)}) collective-permute-start(bf16[2,80,768]{2,1,0:T(8,128)(2,1)S(1)} %pad_maximum_fusion.refs_0_), channel_id=1, source_target_pairs={{0,16},{8,24},{16,0},{24,8},{1,17},{9,25},{17,1},{25,9},{2,18},{10... | collective-permute-start | bytes 737288 | tf_op jit(solution)/shard_map/ppermute | solution.py:306
  73.2 10.2 %collective-permute-start.3 = (bf16[2,80,768]{2,1,0:T(8,128)(2,1)S(1)}, bf16[2,80,768]{2,1,0:T(8,128)(2,1)S(1)}, u32[]{:S(2)}, u32[]{:S(2)}) collective-permute-start(bf16[2,80,768]{2,1,0:T(8,128)(2,1)S(1)} %pad_maximum_fusion.refs_0_), channel_id=1, source_target_pairs={{0,24},{8,0},{16,8},{24,16},{1,25},{9,1},{17,9},{25,17},{2,26},{10... | collective-permute-start | bytes 737288 | tf_op jit(solution)/shard_map/ppermute | solution.py:306
  84.5 39.9 %copy-start = (s32[128,6]{0,1:T(8,128)S(1)}, s32[128,6]{0,1:T(8,128)}, u32[]{:S(2)}) copy-start(s32[128,6]{0,1:T(8,128)} %param.11) | copy-start | bytes 9220
  84.5 39.9 %copy-start.1 = (s32[128,6]{0,1:T(8,128)S(1)}, s32[128,6]{0,1:T(8,128)}, u32[]{:S(2)}) copy-start(s32[128,6]{0,1:T(8,128)} %param.12) | copy-start | bytes 9220
  84.5 39.9 %copy-start.2 = (s32[128,3]{0,1:T(4,128)S(1)}, s32[128,3]{0,1:T(4,128)}, u32[]{:S(2)}) copy-start(s32[128,3]{0,1:T(4,128)} %param.10) | copy-start | bytes 4612
  86.1 39.2 %all-to-all-start.2 = ((bf16[32,64,128]{2,1,0:T(8,128)(2,1)}), bf16[32,64,128]{2,1,0:T(8,128)(2,1)S(1)}, u32[]{:S(2)}, u32[]{:S(2)}) async-start(bf16[32,64,128]{2,1,0:T(8,128)(2,1)} %shard_map.115), calls=%async_computation.2 | async-start | bytes 1048576 | tf_op jit(solution)/shard_map/all_to_all | solution.py:267
  95.3 8.2 %collective-permute-start.4 = (f32[1,128]{1,0:T(1,128)S(1)}, f32[1,128]{1,0:T(1,128)S(1)}, u32[]{:S(2)}, u32[]{:S(2)}) collective-permute-start(f32[1,128]{1,0:T(1,128)S(1)} %get-tuple-element.13), channel_id=1, source_target_pairs={{0,256},{32,288},{64,320},{96,352},{128,384},{160,416},{192,448},{... | collective-permute-start | bytes 1544 | tf_op jit(solution)/shard_map/ppermute | solution.py:346
  103.5 5.5 %collective-permute-start.5 = (f32[2,128]{1,0:T(2,128)S(1)}, f32[2,128]{1,0:T(2,128)S(1)}, u32[]{:S(2)}, u32[]{:S(2)}) collective-permute-start(f32[2,128]{1,0:T(2,128)S(1)} %pad_maximum_fusion.3), channel_id=1, source_target_pairs={{0,128},{32,160},{64,192},{96,224},{128,0},{160,32},{192,64},{224,... | collective-permute-start | bytes 3080 | tf_op jit(solution)/shard_map/ppermute | solution.py:346
  109.0 4.3 %collective-permute-start.6 = (f32[4,128]{1,0:T(4,128)S(1)}, f32[4,128]{1,0:T(4,128)S(1)}, u32[]{:S(2)}, u32[]{:S(2)}) collective-permute-start(f32[4,128]{1,0:T(4,128)S(1)} %pad_maximum_fusion.2), channel_id=1, source_target_pairs={{0,64},{32,96},{64,0},{96,32},{128,192},{160,224},{192,128},{224,1... | collective-permute-start | bytes 6152 | tf_op jit(solution)/shard_map/ppermute | solution.py:346
  113.4 11.0 %collective-permute-start.7 = (f32[8,128]{1,0:T(8,128)S(1)}, f32[8,128]{1,0:T(8,128)S(1)}, u32[]{:S(2)}, u32[]{:S(2)}) collective-permute-start(f32[8,128]{1,0:T(8,128)S(1)} %pad_maximum_fusion.1), channel_id=1, source_target_pairs={{0,32},{32,0},{64,96},{96,64},{128,160},{160,128},{192,224},{224,1... | collective-permute-start | bytes 12296 | tf_op jit(solution)/shard_map/ppermute | solution.py:346

commit v5 on v4

--- a/solution.py
+++ b/solution.py
@@ -86,7 +86,9 @@
         copy.wait()
 
 
-def land_kernel(recv_ref, out_ref, scaled_ref, parts_ref, grad_p_ref):
+def land_kernel(
+    recv_ref, slot_out_ref, scaled_out_ref, out_ref, grad_p_ref, scaled_ref, parts_ref, left
+):
     capacity, features = scaled_ref.shape
     recv = recv_ref[...]
     slot = recv_ref[:, features : features + 1].astype(F32)
@@ -97,27 +99,33 @@
     )[:capacity]
     dy = landed[:, :features]
     p = landed[:, features + 1 : features + 2]
-    scaled = (p * dy).astype(BF16)
-    scaled_ref[...] = scaled
     n = parts_ref.shape[0]
     rows = capacity // 2
     low = lax.broadcasted_iota(jnp.int32, (rows, LANES), 1) < HALF
+    copies = []
     for k in range(n):
         for j in range(2):
-            tile = 2 * k + j
-            parts_ref[k, j * capacity : (j + 1) * capacity] = scaled[
-                :, tile * LANES : (tile + 1) * LANES
-            ]
-    for k in range(n):
-        tile = 2 * n + k // 2
-        own = (p * dy[:, tile * LANES : (tile + 1) * LANES])
+            tile = slice((2 * k + j) * LANES, (2 * k + j + 1) * LANES)
+            value = (p * dy[:, tile]).astype(BF16)
+            scaled_ref[:, tile] = value
+            parts_ref[k, j * capacity : (j + 1) * capacity] = value
+        tile = slice((2 * n + k // 2) * LANES, (2 * n + k // 2 + 1) * LANES)
+        own = p * dy[:, tile]
+        if k % 2 == 0:
+            scaled_ref[:, tile] = own.astype(BF16)
         swapped = pltpu.roll(own, HALF, 1)
         top, bottom = (own, swapped) if k % 2 == 0 else (swapped, own)
         parts_ref[k, 2 * capacity :] = jnp.where(low, top[:rows], bottom[rows:]).astype(BF16)
-    grad_p = jnp.sum(dy * out_ref[...], axis=1, keepdims=True)
+        copies.append(pltpu.make_async_copy(parts_ref.at[k], out_ref.at[k], left.at[k]))
+        copies[-1].start()
+    copies.append(pltpu.make_async_copy(scaled_ref, scaled_out_ref, left.at[n]))
+    copies[-1].start()
+    grad_p = jnp.sum(dy * slot_out_ref[...], axis=1, keepdims=True)
     row = lax.broadcasted_iota(jnp.int32, (capacity, LANES), 0)
     column = lax.broadcasted_iota(jnp.int32, (capacity, LANES), 1)
     grad_p_ref[...] = jnp.sum(jnp.where(row == column, grad_p, 0.0), axis=0, keepdims=True)
+    for copy in copies:
+        copy.wait()
 
 
 def collect_kernel(me_ref, *refs):
@@ -132,7 +140,7 @@
     out_ref[...] = rows_ref[...].T.astype(BF16)
 
 
-def partial_kernel(hidden_ref, parts_ref, out_ref):
+def partial_kernel(hidden_ref, parts_ref, out_ref, send_ref, left):
     team, rows, _ = parts_ref.shape
     capacity = rows * 2 // 5
     blocks = []
@@ -145,19 +153,31 @@
                 axis=1,
             )
         )
-    total = jnp.dot(hidden_ref[...], jnp.concatenate(blocks), preferred_element_type=F32)
-    n = out_ref.shape[0]
-    share = total.shape[0] // n
-    total = total.reshape(n, share, 3 * LANES)
-    out_ref[:, :share] = total[:, :, :LANES].astype(BF16)
-    out_ref[:, share : 2 * share] = total[:, :, LANES : 2 * LANES].astype(BF16)
+    scaled = jnp.concatenate(blocks)
+    n = send_ref.shape[0]
+    share = hidden_ref.shape[0] // n
     third = share // 3
-    last = total[:, :, 2 * LANES :]
-    low = lax.broadcasted_iota(jnp.int32, (n, third, LANES), 2) < HALF
-    swapped = pltpu.roll(last[:, third : 2 * third], HALF, 2)
-    mixed = jnp.where(low, last[:, :third], swapped)
-    out_ref[:, 2 * share : 2 * share + third] = mixed.astype(BF16)
-    out_ref[:, 2 * share + third :] = last[:, 2 * third :].astype(BF16)
+    some = n // OUT_PIECES
+    low = lax.broadcasted_iota(jnp.int32, (some, third, LANES), 2) < HALF
+    copies = []
+    for i in range(OUT_PIECES):
+        here = slice(i * some, (i + 1) * some)
+        total = jnp.dot(
+            hidden_ref[i * some * share : (i + 1) * some * share],
+            scaled,
+            preferred_element_type=F32,
+        ).reshape(some, share, 3 * LANES)
+        send_ref[here, :share] = total[:, :, :LANES].astype(BF16)
+        send_ref[here, share : 2 * share] = total[:, :, LANES : 2 * LANES].astype(BF16)
+        last = total[:, :, 2 * LANES :]
+        swapped = pltpu.roll(last[:, third : 2 * third], HALF, 2)
+        mixed = jnp.where(low, last[:, :third], swapped)
+        send_ref[here, 2 * share : 2 * share + third] = mixed.astype(BF16)
+        send_ref[here, 2 * share + third :] = last[:, 2 * third :].astype(BF16)
+        copies.append(pltpu.make_async_copy(send_ref.at[here], out_ref.at[here], left.at[i]))
+        copies[-1].start()
+    for copy in copies:
+        copy.wait()
 
 
 def sum_kernel(n_0, n_1, terms_ref, out_ref):
@@ -257,7 +277,7 @@
         kernel,
         out_shape=out_shape,
         in_specs=in_specs,
-        out_specs=[out_space] * len(out_shape) if many else out_space,
+        out_specs=[out_space] * len(out_shape) if many and out_space is VMEM else out_space,
         scratch_shapes=scratch,
         compiler_params=pltpu.CompilerParams(vmem_limit_bytes=vmem_mib << 20),
     )
@@ -295,10 +315,7 @@
 
     weight = down_weight[0]
     gate_rows = gate_pre.astype(F32)
-    up_rows = up_pre.astype(F32)
-    sigmoid_gate = jax.nn.sigmoid(gate_rows)
-    activated = gate_rows * sigmoid_gate
-    hidden = (activated * up_rows).astype(BF16)
+    hidden = (gate_rows * jax.nn.sigmoid(gate_rows) * up_pre.astype(F32)).astype(BF16)
     near = lax.ppermute(hidden, "dp_2", [(0, 1), (1, 0)])
     hidden_pair = jnp.stack([hidden, near])
     hiddens = [hidden_pair]
@@ -312,14 +329,21 @@
     )(jnp.stack([lax.axis_index(a) for a in TEAM]), *hiddens)
     slot_out = jnp.dot(hidden, weight, preferred_element_type=F32)
 
+    part = (team, features * capacity // (team * LANES), LANES)
     scaled, parts, grad_p = call(
         land_kernel,
         [
             pltpu.HBM((capacity, features), BF16),
-            pltpu.HBM((team, features * capacity // (team * LANES), LANES), BF16),
-            shape((1, LANES), F32),
+            pltpu.HBM(part, BF16),
+            pltpu.VMEM((1, LANES), F32),
         ],
         [VMEM] * 2,
+        [
+            pltpu.VMEM((capacity, features), BF16),
+            pltpu.VMEM(part, BF16),
+            pltpu.SemaphoreType.DMA((1 + team,)),
+        ],
+        out_space=[HBM, HBM, VMEM],
     )(recv, slot_out)
     parts = exchange(parts, TEAM)
 
@@ -333,8 +357,13 @@
         vmem_mib=60,
     )(*sources)
 
+    terms = (group, 2 * share + 2 * share // 3, LANES)
     partial = call(
-        partial_kernel, shape((group, 2 * share + 2 * share // 3, LANES), BF16), [VMEM] * 2
+        partial_kernel,
+        pltpu.HBM(terms, BF16),
+        [VMEM] * 2,
+        [pltpu.VMEM(terms, BF16), pltpu.SemaphoreType.DMA((OUT_PIECES,))],
+        out_space=HBM,
     )(team_hidden, parts)
     terms = exchange(partial, DP)
     grad_down = call(

time: 127 us -> 127 us (level)
  no operation moved by 1% of the time
where the time goes in v5:
time: 127 us; the launch traced here: 126 us
  waiting for transfers between devices  56.4 us (44%)
  starting transfers between devices  52.9 us (42%)
  Pallas kernels  12.9 us (10%)
  matrix products  2.92 us (2%)
    all_to_all x3, waiting for transfers between devices, exchange(): return lax.all_to_all(value, axes, split_axis=0, concat_axis=0, tiled=True)  31.6 us
    all_to_all x3, starting transfers between devices, exchange(): return lax.all_to_all(value, axes, split_axis=0, concat_axis=0, tiled=True)  26 us
    ppermute x4, starting transfers between devices, step_of(): other = lax.ppermute(grad_p, 'node', [(i, i ^ step) for i in range(n_node)])  13 us
    ppermute x4, waiting for transfers between devices, step_of(): other = lax.ppermute(grad_p, 'node', [(i, i ^ step) for i in range(n_node)])  11.5 us
    ppermute x3, starting transfers between devices, step_of(): lax.ppermute(hidden_pair, 'dp_0', [(i, (i + k) % n_0) for i in range(n_0)])  10.5 us
    ppermute x3, waiting for transfers between devices, step_of(): lax.ppermute(hidden_pair, 'dp_0', [(i, (i + k) % n_0) for i in range(n_0)])  7.11 us
    ppermute x1, waiting for transfers between devices, step_of(): near = lax.ppermute(hidden, 'dp_2', [(0, 1), (1, 0)])  6.22 us
    pallas_call x1, Pallas kernels, step_of(): call(grads_kernel, [shape((capacity, units), BF16)] * 2, [HBM] * 4, [pltp...  4.45 us
  transfers between devices with their start and end apart: 11, of which 7 were waited for; matrix products, arithmetic and copies ran while one was open for 2% of the time, Pallas kernels for 5%

profile of v5, /device:TPU:1, one launch (start us, length us, event | category | flops | bytes accessed | tf_op | source)
XLA Modules:
  0.0 126.2 jit_solution(8955128494710200120)
XLA Ops:
  0.7 2.6 %shard_map.111 = bf16[256,2688]{1,0:T(8,128)(2,1)} custom-call(bf16[128,2560]{1,0:T(8,128)(2,1)} %refs_0_.1, bf16[6,128]{1,0:T(8,128)(2,1)} %bitcast.30, s32[3,128]{1,0:T(4,128)} %bitcast.22, s32[6,128]{1,0:T(8,128)} %bitcast.18, s32[6,128]{1,0:T(8,128)} %bitcast.20), custom_call_target="tpu_custom_call" | custom-call | tf_op jit(solution)/shard_map/pallas_call | solution.py:303
  3.3 11.8 %all-to-all-start = ((bf16[16,16,2688]{2,1,0:T(8,128)(2,1)}), bf16[16,16,2688]{2,1,0:T(8,128)(2,1)S(1)}, u32[]{:S(2)}, u32[]{:S(2)}) async-start(bf16[16,16,2688]{2,1,0:T(8,128)(2,1)} %bitcast.25), calls=%async_computation | async-start | bytes 2752512 | tf_op jit(solution)/shard_map/all_to_all | solution.py:287
  15.2 2.9 %fusion.5.slot_out_ref = f32[80,2560]{1,0:T(8,128)S(1)} fusion(bf16[80,768]{1,0:T(8,128)(2,1)S(1)} %fusion.4, bf16[1,768,2560]{2,1,0:T(8,128)(2,1)} %param.15), kind=kOutput, calls=%fused_computation.12 | convolution fusion | flops 314572800 | bytes 4874240 | tf_op jit(solution)/shard_map/dot_general | solution.py:330
  18.1 31.6 %all-to-all-done = bf16[16,16,2688]{2,1,0:T(8,128)(2,1)S(1)} async-done(((bf16[16,16,2688]{2,1,0:T(8,128)(2,1)}), bf16[16,16,2688]{2,1,0:T(8,128)(2,1)S(1)}, u32[]{:S(2)}, u32[]{:S(2)}) %all-to-all-start) | async-done | bytes 1376288 | tf_op jit(solution)/shard_map/all_to_all | solution.py:287
  49.7 1.6 %shard_map.112 = (bf16[80,2560]{1,0:T(8,128)(2,1)}, bf16[8,200,128]{2,1,0:T(8,128)(2,1)}, f32[1,128]{1,0:T(1,128)S(1)}) custom-call(bf16[256,2688]{1,0:T(8,128)(2,1)S(1)} %bitcast.17, f32[80,2560]{1,0:T(8,128)S(1)} %fusion.5.slot_out_ref), custom_call_target="tpu_custom_call" | custom-call | tf_op jit(solution)/shard_map/pallas_call | solution.py:333
  51.3 5.0 %all-to-all-start.1 = ((bf16[8,200,128]{2,1,0:T(8,128)(2,1)}), bf16[8,200,128]{2,1,0:T(8,128)(2,1)S(1)}, u32[]{:S(2)}, u32[]{:S(2)}) async-start(bf16[8,200,128]{2,1,0:T(8,128)(2,1)} %get-tuple-element.12), calls=%async_computation.1 | async-start | bytes 819200 | tf_op jit(solution)/shard_map/all_to_all | solution.py:287
  56.4 3.4 %collective-permute-start = (bf16[80,768]{1,0:T(8,128)(2,1)S(1)}, bf16[80,768]{1,0:T(8,128)(2,1)S(1)}, u32[]{:S(2)}, u32[]{:S(2)}) collective-permute-start(bf16[80,768]{1,0:T(8,128)(2,1)S(1)} %fusion.4), channel_id=1, source_target_pairs={{0,1},{1,0},{2,3},{3,2},{4,5},{5,4},{6,7},{7,6},{8,9},{9,8},{10,11... | collective-permute-start | bytes 368648 | tf_op jit(solution)/shard_map/ppermute | solution.py:319
  59.7 6.2 %collective-permute-done = bf16[80,768]{1,0:T(8,128)(2,1)S(1)} collective-permute-done((bf16[80,768]{1,0:T(8,128)(2,1)S(1)}, bf16[80,768]{1,0:T(8,128)(2,1)S(1)}, u32[]{:S(2)}, u32[]{:S(2)}) %collective-permute-start) | collective-permute-done | bytes 122912 | tf_op jit(solution)/shard_map/ppermute | solution.py:319
  66.0 3.1 %collective-permute-start.1 = (bf16[2,80,768]{2,1,0:T(8,128)(2,1)S(1)}, bf16[2,80,768]{2,1,0:T(8,128)(2,1)S(1)}, u32[]{:S(2)}, u32[]{:S(2)}) collective-permute-start(bf16[2,80,768]{2,1,0:T(8,128)(2,1)S(1)} %pad_maximum_fusion.refs_0_), channel_id=1, source_target_pairs={{0,8},{8,16},{16,24},{24,0},{1,9},{9,17},{17,25},{25,1},{2,10},{10... | collective-permute-start | bytes 737288 | tf_op jit(solution)/shard_map/ppermute | solution.py:323
  69.1 4.3 %collective-permute-start.2 = (bf16[2,80,768]{2,1,0:T(8,128)(2,1)S(1)}, bf16[2,80,768]{2,1,0:T(8,128)(2,1)S(1)}, u32[]{:S(2)}, u32[]{:S(2)}) collective-permute-start(bf16[2,80,768]{2,1,0:T(8,128)(2,1)S(1)} %pad_maximum_fusion.refs_0_), channel_id=1, source_target_pairs={{0,16},{8,24},{16,0},{24,8},{1,17},{9,25},{17,1},{25,9},{2,18},{10... | collective-permute-start | bytes 737288 | tf_op jit(solution)/shard_map/ppermute | solution.py:323
  73.4 3.0 %collective-permute-start.3 = (bf16[2,80,768]{2,1,0:T(8,128)(2,1)S(1)}, bf16[2,80,768]{2,1,0:T(8,128)(2,1)S(1)}, u32[]{:S(2)}, u32[]{:S(2)}) collective-permute-start(bf16[2,80,768]{2,1,0:T(8,128)(2,1)S(1)} %pad_maximum_fusion.refs_0_), channel_id=1, source_target_pairs={{0,24},{8,0},{16,8},{24,16},{1,25},{9,1},{17,9},{25,17},{2,26},{10... | collective-permute-start | bytes 737288 | tf_op jit(solution)/shard_map/ppermute | solution.py:323
  76.6 5.8 %collective-permute-done.2.refs_2_ = bf16[2,80,768]{2,1,0:T(8,128)(2,1)S(1)} collective-permute-done((bf16[2,80,768]{2,1,0:T(8,128)(2,1)S(1)}, bf16[2,80,768]{2,1,0:T(8,128)(2,1)S(1)}, u32[]{:S(2)}, u32[]{:S(2)}) %collective-permute-start.2) | collective-permute-done | bytes 245792 | tf_op jit(solution)/shard_map/ppermute | solution.py:323
  82.4 1.3 %collective-permute-done.3.refs_3_ = bf16[2,80,768]{2,1,0:T(8,128)(2,1)S(1)} collective-permute-done((bf16[2,80,768]{2,1,0:T(8,128)(2,1)S(1)}, bf16[2,80,768]{2,1,0:T(8,128)(2,1)S(1)}, u32[]{:S(2)}, u32[]{:S(2)}) %collective-permute-start.3) | collective-permute-done | bytes 245792 | tf_op jit(solution)/shard_map/ppermute | solution.py:323
  83.7 1.0 shard_map.114.hidden_ref
  84.7 1.5 %shard_map.115 = bf16[32,64,128]{2,1,0:T(8,128)(2,1)} custom-call(bf16[768,640]{1,0:T(8,128)(2,1)S(1)} %shard_map.114.hidden_ref, bf16[8,200,128]{2,1,0:T(8,128)(2,1)S(1)} %all-to-all-done.1.parts_ref), custom_call_target="tpu_custom_call" | custom-call | tf_op jit(solution)/shard_map/pallas_call | solution.py:361
  86.3 9.1 %all-to-all-start.2 = ((bf16[32,64,128]{2,1,0:T(8,128)(2,1)}), bf16[32,64,128]{2,1,0:T(8,128)(2,1)S(1)}, u32[]{:S(2)}, u32[]{:S(2)}) async-start(bf16[32,64,128]{2,1,0:T(8,128)(2,1)} %shard_map.115), calls=%async_computation.2 | async-start | bytes 1048576 | tf_op jit(solution)/shard_map/all_to_all | solution.py:287
  95.4 2.7 %collective-permute-start.4 = (f32[1,128]{1,0:T(1,128)S(1)}, f32[1,128]{1,0:T(1,128)S(1)}, u32[]{:S(2)}, u32[]{:S(2)}) collective-permute-start(f32[1,128]{1,0:T(1,128)S(1)} %get-tuple-element.13), channel_id=1, source_target_pairs={{0,256},{32,288},{64,320},{96,352},{128,384},{160,416},{192,448},{... | collective-permute-start | bytes 1544 | tf_op jit(solution)/shard_map/ppermute | solution.py:375
  98.1 5.5 %collective-permute-done.4 = f32[1,128]{1,0:T(1,128)S(1)} collective-permute-done((f32[1,128]{1,0:T(1,128)S(1)}, f32[1,128]{1,0:T(1,128)S(1)}, u32[]{:S(2)}, u32[]{:S(2)}) %collective-permute-start.4) | collective-permute-done | bytes 544 | tf_op jit(solution)/shard_map/ppermute | solution.py:375
  103.7 1.9 %collective-permute-start.5 = (f32[2,128]{1,0:T(2,128)S(1)}, f32[2,128]{1,0:T(2,128)S(1)}, u32[]{:S(2)}, u32[]{:S(2)}) collective-permute-start(f32[2,128]{1,0:T(2,128)S(1)} %pad_maximum_fusion.3), channel_id=1, source_target_pairs={{0,128},{32,160},{64,192},{96,224},{128,0},{160,32},{192,64},{224,... | collective-permute-start | bytes 3080 | tf_op jit(solution)/shard_map/ppermute | solution.py:375
  105.6 3.6 %collective-permute-done.5 = f32[2,128]{1,0:T(2,128)S(1)} collective-permute-done((f32[2,128]{1,0:T(2,128)S(1)}, f32[2,128]{1,0:T(2,128)S(1)}, u32[]{:S(2)}, u32[]{:S(2)}) %collective-permute-start.5) | collective-permute-done | bytes 1056 | tf_op jit(solution)/shard_map/ppermute | solution.py:375
  109.2 1.9 %collective-permute-start.6 = (f32[4,128]{1,0:T(4,128)S(1)}, f32[4,128]{1,0:T(4,128)S(1)}, u32[]{:S(2)}, u32[]{:S(2)}) collective-permute-start(f32[4,128]{1,0:T(4,128)S(1)} %pad_maximum_fusion.2), channel_id=1, source_target_pairs={{0,64},{32,96},{64,0},{96,32},{128,192},{160,224},{192,128},{224,1... | collective-permute-start | bytes 6152 | tf_op jit(solution)/shard_map/ppermute | solution.py:375
  111.1 2.4 %collective-permute-done.6 = f32[4,128]{1,0:T(4,128)S(1)} collective-permute-done((f32[4,128]{1,0:T(4,128)S(1)}, f32[4,128]{1,0:T(4,128)S(1)}, u32[]{:S(2)}, u32[]{:S(2)}) %collective-permute-start.6) | collective-permute-done | bytes 2080 | tf_op jit(solution)/shard_map/ppermute | solution.py:375
  113.5 6.5 %collective-permute-start.7 = (f32[8,128]{1,0:T(8,128)S(1)}, f32[8,128]{1,0:T(8,128)S(1)}, u32[]{:S(2)}, u32[]{:S(2)}) collective-permute-start(f32[8,128]{1,0:T(8,128)S(1)} %pad_maximum_fusion.1), channel_id=1, source_target_pairs={{0,32},{32,0},{64,96},{96,64},{128,160},{160,128},{192,224},{224,1... | collective-permute-start | bytes 12296 | tf_op jit(solution)/shard_map/ppermute | solution.py:375
  120.0 4.5 %shard_map.113 = (bf16[80,768]{1,0:T(8,128)(2,1)}, bf16[80,768]{1,0:T(8,128)(2,1)}) custom-call(bf16[80,2560]{1,0:T(8,128)(2,1)} %get-tuple-element.9.refs_0_, bf16[80,768]{1,0:T(8,128)(2,1)} %refs_1_.1, bf16[80,768]{1,0:T(8,128)(2,1)} %refs_2_.1, bf16[768,2560]{1,0:T(8,128)(2,1)} %bitcast.24), custom_call_target="tpu_custom_call" | custom-call | tf_op jit(solution)/shard_map/pallas_call | solution.py:351
  (23 shorter events, 2.0 us)
Async XLA Ops:
  0.6 14.5 %copy-start.4 = (bf16[80,768]{1,0:T(8,128)(2,1)S(1)}, bf16[80,768]{1,0:T(8,128)(2,1)}, u32[]{:S(2)}) copy-start(bf16[80,768]{1,0:T(8,128)(2,1)} %refs_1_.1) | copy-start | bytes 368644
  0.6 14.5 %copy-start.3 = (bf16[80,768]{1,0:T(8,128)(2,1)S(1)}, bf16[80,768]{1,0:T(8,128)(2,1)}, u32[]{:S(2)}) copy-start(bf16[80,768]{1,0:T(8,128)(2,1)} %refs_2_.1) | copy-start | bytes 368644
  3.3 46.4 %all-to-all-start = ((bf16[16,16,2688]{2,1,0:T(8,128)(2,1)}), bf16[16,16,2688]{2,1,0:T(8,128)(2,1)S(1)}, u32[]{:S(2)}, u32[]{:S(2)}) async-start(bf16[16,16,2688]{2,1,0:T(8,128)(2,1)} %bitcast.25), calls=%async_computation | async-start | bytes 2752512 | tf_op jit(solution)/shard_map/all_to_all | solution.py:287
  51.3 33.4 %all-to-all-start.1 = ((bf16[8,200,128]{2,1,0:T(8,128)(2,1)}), bf16[8,200,128]{2,1,0:T(8,128)(2,1)S(1)}, u32[]{:S(2)}, u32[]{:S(2)}) async-start(bf16[8,200,128]{2,1,0:T(8,128)(2,1)} %get-tuple-element.12), calls=%async_computation.1 | async-start | bytes 819200 | tf_op jit(solution)/shard_map/all_to_all | solution.py:287
  56.4 9.6 %collective-permute-start = (bf16[80,768]{1,0:T(8,128)(2,1)S(1)}, bf16[80,768]{1,0:T(8,128)(2,1)S(1)}, u32[]{:S(2)}, u32[]{:S(2)}) collective-permute-start(bf16[80,768]{1,0:T(8,128)(2,1)S(1)} %fusion.4), channel_id=1, source_target_pairs={{0,1},{1,0},{2,3},{3,2},{4,5},{5,4},{6,7},{7,6},{8,9},{9,8},{10,11... | collective-permute-start | bytes 368648 | tf_op jit(solution)/shard_map/ppermute | solution.py:319
  66.0 10.6 %collective-permute-start.1 = (bf16[2,80,768]{2,1,0:T(8,128)(2,1)S(1)}, bf16[2,80,768]{2,1,0:T(8,128)(2,1)S(1)}, u32[]{:S(2)}, u32[]{:S(2)}) collective-permute-start(bf16[2,80,768]{2,1,0:T(8,128)(2,1)S(1)} %pad_maximum_fusion.refs_0_), channel_id=1, source_target_pairs={{0,8},{8,16},{16,24},{24,0},{1,9},{9,17},{17,25},{25,1},{2,10},{10... | collective-permute-start | bytes 737288 | tf_op jit(solution)/shard_map/ppermute | solution.py:323
  69.1 13.3 %collective-permute-start.2 = (bf16[2,80,768]{2,1,0:T(8,128)(2,1)S(1)}, bf16[2,80,768]{2,1,0:T(8,128)(2,1)S(1)}, u32[]{:S(2)}, u32[]{:S(2)}) collective-permute-start(bf16[2,80,768]{2,1,0:T(8,128)(2,1)S(1)} %pad_maximum_fusion.refs_0_), channel_id=1, source_target_pairs={{0,16},{8,24},{16,0},{24,8},{1,17},{9,25},{17,1},{25,9},{2,18},{10... | collective-permute-start | bytes 737288 | tf_op jit(solution)/shard_map/ppermute | solution.py:323
  73.4 10.2 %collective-permute-start.3 = (bf16[2,80,768]{2,1,0:T(8,128)(2,1)S(1)}, bf16[2,80,768]{2,1,0:T(8,128)(2,1)S(1)}, u32[]{:S(2)}, u32[]{:S(2)}) collective-permute-start(bf16[2,80,768]{2,1,0:T(8,128)(2,1)S(1)} %pad_maximum_fusion.refs_0_), channel_id=1, source_target_pairs={{0,24},{8,0},{16,8},{24,16},{1,25},{9,1},{17,9},{25,17},{2,26},{10... | collective-permute-start | bytes 737288 | tf_op jit(solution)/shard_map/ppermute | solution.py:323
  84.7 39.8 %copy-start = (s32[128,6]{0,1:T(8,128)S(1)}, s32[128,6]{0,1:T(8,128)}, u32[]{:S(2)}) copy-start(s32[128,6]{0,1:T(8,128)} %param.11) | copy-start | bytes 9220
  84.7 39.8 %copy-start.1 = (s32[128,6]{0,1:T(8,128)S(1)}, s32[128,6]{0,1:T(8,128)}, u32[]{:S(2)}) copy-start(s32[128,6]{0,1:T(8,128)} %param.12) | copy-start | bytes 9220
  84.7 39.8 %copy-start.2 = (s32[128,3]{0,1:T(4,128)S(1)}, s32[128,3]{0,1:T(4,128)}, u32[]{:S(2)}) copy-start(s32[128,3]{0,1:T(4,128)} %param.10) | copy-start | bytes 4612
  86.3 39.2 %all-to-all-start.2 = ((bf16[32,64,128]{2,1,0:T(8,128)(2,1)}), bf16[32,64,128]{2,1,0:T(8,128)(2,1)S(1)}, u32[]{:S(2)}, u32[]{:S(2)}) async-start(bf16[32,64,128]{2,1,0:T(8,128)(2,1)} %shard_map.115), calls=%async_computation.2 | async-start | bytes 1048576 | tf_op jit(solution)/shard_map/all_to_all | solution.py:287
  95.4 8.2 %collective-permute-start.4 = (f32[1,128]{1,0:T(1,128)S(1)}, f32[1,128]{1,0:T(1,128)S(1)}, u32[]{:S(2)}, u32[]{:S(2)}) collective-permute-start(f32[1,128]{1,0:T(1,128)S(1)} %get-tuple-element.13), channel_id=1, source_target_pairs={{0,256},{32,288},{64,320},{96,352},{128,384},{160,416},{192,448},{... | collective-permute-start | bytes 1544 | tf_op jit(solution)/shard_map/ppermute | solution.py:375
  103.7 5.5 %collective-permute-start.5 = (f32[2,128]{1,0:T(2,128)S(1)}, f32[2,128]{1,0:T(2,128)S(1)}, u32[]{:S(2)}, u32[]{:S(2)}) collective-permute-start(f32[2,128]{1,0:T(2,128)S(1)} %pad_maximum_fusion.3), channel_id=1, source_target_pairs={{0,128},{32,160},{64,192},{96,224},{128,0},{160,32},{192,64},{224,... | collective-permute-start | bytes 3080 | tf_op jit(solution)/shard_map/ppermute | solution.py:375
  109.2 4.3 %collective-permute-start.6 = (f32[4,128]{1,0:T(4,128)S(1)}, f32[4,128]{1,0:T(4,128)S(1)}, u32[]{:S(2)}, u32[]{:S(2)}) collective-permute-start(f32[4,128]{1,0:T(4,128)S(1)} %pad_maximum_fusion.2), channel_id=1, source_target_pairs={{0,64},{32,96},{64,0},{96,32},{128,192},{160,224},{192,128},{224,1... | collective-permute-start | bytes 6152 | tf_op jit(solution)/shard_map/ppermute | solution.py:375
  113.5 11.0 %collective-permute-start.7 = (f32[8,128]{1,0:T(8,128)S(1)}, f32[8,128]{1,0:T(8,128)S(1)}, u32[]{:S(2)}, u32[]{:S(2)}) collective-permute-start(f32[8,128]{1,0:T(8,128)S(1)} %pad_maximum_fusion.1), channel_id=1, source_target_pairs={{0,32},{32,0},{64,96},{96,64},{128,160},{160,128},{192,224},{224,1... | collective-permute-start | bytes 12296 | tf_op jit(solution)/shard_map/ppermute | solution.py:375

commit v6 on v5

--- a/solution.py
+++ b/solution.py
@@ -16,7 +16,6 @@
 NODE_DP = ("node", *DP)
 TEAM = ("dp_0", "dp_2")
 HALF = LANES // 2
-PIECES = 3
 OUT_PIECES = 4
 F32 = jnp.float32
 BF16 = jnp.bfloat16
@@ -42,7 +41,7 @@
         copy.wait()
     og_ref, prob_ref, presel_ref, expert_ref, slot_ref = held
     tokens, features = og_ref.shape
-    n_node = send_ref.shape[0] // SRC_CAP
+    n_node = send_ref.shape[0]
     expert, slot, presel = expert_ref[...], slot_ref[...], presel_ref[...]
     slots = columns_of_routes(expert, slot, slot + 1)
     probs = columns_of_routes(expert, slot, prob_ref[...].astype(F32))
@@ -68,19 +67,31 @@
     rows = n_node * SRC_CAP
     slot_rows = jnp.sum(jnp.where(picked, slot_to[:, None, :], 0.0), axis=2, keepdims=True)
     prob_rows = jnp.sum(jnp.where(picked, prob_to[:, None, :], 0.0), axis=2, keepdims=True)
-    lane = lax.broadcasted_iota(jnp.int32, (n_node, SRC_CAP, LANES), 2)
-    info = jnp.where(lane == 0, slot_rows, jnp.where(lane == 1, prob_rows, 0.0))
-    send_ref[:, features:] = info.reshape(rows, LANES).astype(BF16)
+    half = SRC_CAP // 2
+    lane = lax.broadcasted_iota(jnp.int32, (n_node, half, LANES), 2)
+    info = jnp.zeros((n_node, half, LANES), F32)
+    for i, column in enumerate(
+        (slot_rows[:, :half], prob_rows[:, :half], slot_rows[:, half:], prob_rows[:, half:])
+    ):
+        info = jnp.where(lane == i, column, info)
+    tiles = features // LANES
+    send_ref[:, tiles * SRC_CAP :] = info.astype(BF16)
     pick = jnp.where(picked, 1.0, 0.0).reshape(rows, tokens).astype(BF16)
     copies[0].wait()
     leaving = []
-    piece = rows // OUT_PIECES
+    some = n_node // OUT_PIECES
     for i in range(OUT_PIECES):
-        some = slice(i * piece, (i + 1) * piece)
-        send_ref[some, :features] = jnp.dot(
-            pick[some], og_ref[...], preferred_element_type=F32
-        ).astype(BF16)
-        leaving.append(pltpu.make_async_copy(send_ref.at[some], out_ref.at[some], left.at[i]))
+        here = slice(i * some, (i + 1) * some)
+        taken = jnp.dot(
+            pick[i * some * SRC_CAP : (i + 1) * some * SRC_CAP],
+            og_ref[...],
+            preferred_element_type=F32,
+        )
+        for k in range(tiles):
+            send_ref[here, k * SRC_CAP : (k + 1) * SRC_CAP] = (
+                taken[:, k * LANES : (k + 1) * LANES].reshape(some, SRC_CAP, LANES).astype(BF16)
+            )
+        leaving.append(pltpu.make_async_copy(send_ref.at[here], out_ref.at[here], left.at[i]))
         leaving[-1].start()
     for copy in leaving:
         copy.wait()
@@ -90,37 +101,65 @@
     recv_ref, slot_out_ref, scaled_out_ref, out_ref, grad_p_ref, scaled_ref, parts_ref, left
 ):
     capacity, features = scaled_ref.shape
-    recv = recv_ref[...]
-    slot = recv_ref[:, features : features + 1].astype(F32)
-    lane = lax.broadcasted_iota(jnp.int32, (recv.shape[0], LANES), 1).astype(F32)
-    landing = jnp.where(slot == lane + 1.0, 1.0, 0.0).astype(BF16)
-    landed = lax.dot_general(
-        landing, recv, (((0,), (0,)), ((), ())), preferred_element_type=F32
-    )[:capacity]
-    dy = landed[:, :features]
-    p = landed[:, features + 1 : features + 2]
+    n_node = recv_ref.shape[0]
+    rows = n_node * SRC_CAP
+    info = recv_ref[:, features // LANES * SRC_CAP :].astype(F32)
+    slot, prob = (
+        jnp.concatenate([info[:, :, i : i + 1], info[:, :, i + 2 : i + 3]], axis=1).reshape(rows, 1)
+        for i in range(2)
+    )
+    lane = lax.broadcasted_iota(jnp.int32, (rows, LANES), 1).astype(F32)
+    landing = jnp.where(slot == lane + 1.0, 1.0, 0.0).T[:capacity].astype(BF16)
+
+    def landed(value):
+        return jnp.dot(landing, value, preferred_element_type=F32)
+
+    def pair(tile):
+        return landed(
+            jnp.concatenate(
+                [
+                    recv_ref[:, i * SRC_CAP : (i + 1) * SRC_CAP].reshape(rows, LANES)
+                    for i in (tile, tile + 1)
+                ],
+                axis=1,
+            )
+        )
+
+    p = landed(jnp.where(lane < LANES, prob, 0.0).astype(BF16))
     n = parts_ref.shape[0]
-    rows = capacity // 2
-    low = lax.broadcasted_iota(jnp.int32, (rows, LANES), 1) < HALF
+    half = capacity // 2
+    low = lax.broadcasted_iota(jnp.int32, (half, LANES), 1) < HALF
+    sums = jnp.zeros((capacity, LANES), F32)
+
+    def settle(dy, tile):
+        value = p * dy
+        here = slice(tile * LANES, (tile + 1) * LANES)
+        scaled_ref[:, here] = value.astype(BF16)
+        return value, dy * slot_out_ref[:, here]
+
+    for tile in range(2 * n, features // LANES, 2):
+        both = pair(tile)
+        for i in range(2):
+            own, term = settle(both[:, i * LANES : (i + 1) * LANES], tile + i)
+            sums += term
+            k = 2 * (tile + i - 2 * n)
+            swapped = pltpu.roll(own, HALF, 1)
+            parts_ref[k, 2 * capacity :] = jnp.where(low, own[:half], swapped[half:]).astype(BF16)
+            parts_ref[k + 1, 2 * capacity :] = jnp.where(low, swapped[:half], own[half:]).astype(
+                BF16
+            )
     copies = []
     for k in range(n):
+        both = pair(2 * k)
         for j in range(2):
-            tile = slice((2 * k + j) * LANES, (2 * k + j + 1) * LANES)
-            value = (p * dy[:, tile]).astype(BF16)
-            scaled_ref[:, tile] = value
-            parts_ref[k, j * capacity : (j + 1) * capacity] = value
-        tile = slice((2 * n + k // 2) * LANES, (2 * n + k // 2 + 1) * LANES)
-        own = p * dy[:, tile]
-        if k % 2 == 0:
-            scaled_ref[:, tile] = own.astype(BF16)
-        swapped = pltpu.roll(own, HALF, 1)
-        top, bottom = (own, swapped) if k % 2 == 0 else (swapped, own)
-        parts_ref[k, 2 * capacity :] = jnp.where(low, top[:rows], bottom[rows:]).astype(BF16)
+            own, term = settle(both[:, j * LANES : (j + 1) * LANES], 2 * k + j)
+            sums += term
+            parts_ref[k, j * capacity : (j + 1) * capacity] = own.astype(BF16)
         copies.append(pltpu.make_async_copy(parts_ref.at[k], out_ref.at[k], left.at[k]))
         copies[-1].start()
     copies.append(pltpu.make_async_copy(scaled_ref, scaled_out_ref, left.at[n]))
     copies[-1].start()
-    grad_p = jnp.sum(dy * slot_out_ref[...], axis=1, keepdims=True)
+    grad_p = jnp.sum(sums, axis=1, keepdims=True)
     row = lax.broadcasted_iota(jnp.int32, (capacity, LANES), 0)
     column = lax.broadcasted_iota(jnp.int32, (capacity, LANES), 1)
     grad_p_ref[...] = jnp.sum(jnp.where(row == column, grad_p, 0.0), axis=0, keepdims=True)
@@ -207,38 +246,52 @@
         put(2 * third, tile, jnp.where(low, last_0, pltpu.roll(last_1, HALF, 1)))
 
 
-def grads_kernel(*refs):
-    sources, grad_gate_ref, grad_up_ref = refs[:4], refs[4], refs[5]
-    (scaled_ref, gate_ref, up_ref, weight_ref), arrived = refs[6:10], refs[10]
+def grads_kernel(first, *refs):
+    sources, (gate_out_ref, up_out_ref) = refs[:4], refs[-10:-8]
+    scaled_ref, gate_ref, up_ref, weight_ref, gate_grad_ref, up_grad_ref = refs[-8:-2]
+    arrived, left = [refs[-2].at[i] for i in range(5)], refs[-1]
+    units = weight_ref.shape[0]
+    piece = units // 2
+    columns = pl.ds(first, units)
     copies = [
-        pltpu.make_async_copy(source, place, arrived.at[i])
-        for i, (source, place) in enumerate(zip(sources[:3], refs[6:9]))
+        pltpu.make_async_copy(sources[0], scaled_ref, arrived[0]),
+        pltpu.make_async_copy(sources[1].at[:, columns], gate_ref, arrived[1]),
+        pltpu.make_async_copy(sources[2].at[:, columns], up_ref, arrived[2]),
     ]
-    units = weight_ref.shape[0]
-    piece = units // PIECES
-    for i in range(PIECES):
-        rows = pl.ds(i * piece, piece)
+    for i in range(2):
         copies.append(
-            pltpu.make_async_copy(sources[3].at[rows], weight_ref.at[rows], arrived.at[3 + i])
+            pltpu.make_async_copy(
+                sources[3].at[pl.ds(first + i * piece, piece)],
+                weight_ref.at[pl.ds(i * piece, piece)],
+                arrived[3 + i],
+            )
         )
     for copy in copies:
         copy.start()
     for copy in copies[:3]:
         copy.wait()
-    for i in range(PIECES):
+    for i in range(2):
         copies[3 + i].wait()
-        rows = slice(i * piece, (i + 1) * piece)
+        here = slice(i * piece, (i + 1) * piece)
         d_hidden = lax.dot_general(
             scaled_ref[...],
-            weight_ref[rows],
+            weight_ref[here],
             (((1,), (1,)), ((), ())),
             preferred_element_type=F32,
         )
-        gate, up = gate_ref[:, rows].astype(F32), up_ref[:, rows].astype(F32)
+        gate, up = gate_ref[:, here].astype(F32), up_ref[:, here].astype(F32)
         sigmoid = jax.nn.sigmoid(gate)
         slope = sigmoid * (1.0 + gate * (1.0 - sigmoid))
-        grad_gate_ref[:, rows] = (d_hidden * up * slope).astype(BF16)
-        grad_up_ref[:, rows] = (d_hidden * (gate * sigmoid)).astype(BF16)
+        gate_grad_ref[:, here] = (d_hidden * up * slope).astype(BF16)
+        up_grad_ref[:, here] = (d_hidden * (gate * sigmoid)).astype(BF16)
+    copies = [
+        pltpu.make_async_copy(gate_grad_ref, gate_out_ref.at[:, columns], left.at[0]),
+        pltpu.make_async_copy(up_grad_ref, up_out_ref.at[:, columns], left.at[1]),
+    ]
+    for copy in copies:
+        copy.start()
+    for copy in copies:
+        copy.wait()
 
 
 def return_kernel(steps, me_ref, grad_p_ref, presel_ref, expert_ref, slot_ref, out_ref):
@@ -251,17 +304,24 @@
     for bit, step in enumerate(steps):
         away = jnp.where((row >> bit) & 1 == 1, away | step, away)
     slot_ids = lax.broadcasted_iota(jnp.int32, (LANES, tokens), 0)
+    here = jnp.concatenate(
+        [
+            jnp.where((presel[c : c + 1] ^ me_ref[0]) == away, 1.0, 0.0)
+            for c in range(PRESEL)
+        ],
+        axis=1,
+    )
+    by_slot = lax.dot_general(
+        grad_p_ref[...],
+        here,
+        (((0,), (0,)), ((), ())),
+        preferred_element_type=F32,
+        precision=lax.Precision.HIGHEST,
+    )
     result = jnp.zeros(out_ref.shape, F32)
     for c in range(PRESEL):
-        here = (presel[c : c + 1] ^ me_ref[0]) == away
-        by_slot = lax.dot_general(
-            grad_p_ref[...],
-            jnp.where(here, 1.0, 0.0),
-            (((0,), (0,)), ((), ())),
-            preferred_element_type=F32,
-            precision=lax.Precision.HIGHEST,
-        )
-        value = jnp.sum(jnp.where(slot_ids + 1 == slots[c], by_slot, 0.0), axis=0, keepdims=True)
+        values = by_slot[:, c * tokens : (c + 1) * tokens]
+        value = jnp.sum(jnp.where(slot_ids + 1 == slots[c], values, 0.0), axis=0, keepdims=True)
         result += jnp.where((expert == c * EXP_NODE) & (slot >= 0), value, 0.0)
     out_ref[...] = result
 
@@ -271,14 +331,17 @@
 SMEM = pl.BlockSpec(memory_space=pltpu.SMEM)
 
 
-def call(kernel, out_shape, in_specs, scratch=(), vmem_mib=12, out_space=VMEM):
+def call(kernel, out_shape, in_specs, scratch=(), vmem_mib=12, out_space=VMEM, aliases=None):
     many = isinstance(out_shape, (tuple, list))
     return pl.pallas_call(
         kernel,
         out_shape=out_shape,
         in_specs=in_specs,
-        out_specs=[out_space] * len(out_shape) if many and out_space is VMEM else out_space,
+        out_specs=[out_space] * len(out_shape)
+        if many and not isinstance(out_space, list)
+        else out_space,
         scratch_shapes=scratch,
+        input_output_aliases=aliases or {},
         compiler_params=pltpu.CompilerParams(vmem_limit_bytes=vmem_mib << 20),
     )
 
@@ -300,18 +363,18 @@
     presel, expert, slot = presel_nodes.T, route_expert.T, route_slot.T
     routed = (out_grad, gate_prob.T, presel, expert, slot)
 
+    chunks = (n_node, features // LANES * SRC_CAP + SRC_CAP // 2, LANES)
     send = call(
         route_kernel,
-        shape((n_node * SRC_CAP, features + LANES), BF16),
+        shape(chunks, BF16),
         [HBM] * 5,
         [pltpu.VMEM(a.shape, a.dtype) for a in routed]
-        + [pltpu.VMEM((n_node * SRC_CAP, features + LANES), BF16)]
+        + [pltpu.VMEM(chunks, BF16)]
         + [pltpu.SemaphoreType.DMA((5,)), pltpu.SemaphoreType.DMA((OUT_PIECES,))],
         out_space=HBM,
         vmem_mib=60,
     )(*routed)
-    recv = exchange(send.reshape(n_node, SRC_CAP, features + LANES), "node")
-    recv = recv.reshape(n_node * SRC_CAP, features + LANES)
+    recv = exchange(send, "node")
 
     weight = down_weight[0]
     gate_rows = gate_pre.astype(F32)
@@ -348,14 +411,23 @@
     parts = exchange(parts, TEAM)
 
     sources = (scaled, gate_pre, up_pre, weight)
-    grad_gate, grad_up = call(
-        grads_kernel,
-        [shape((capacity, units), BF16)] * 2,
-        [HBM] * 4,
-        [pltpu.VMEM(a.shape, a.dtype) for a in sources]
-        + [pltpu.SemaphoreType.DMA((3 + PIECES,))],
-        vmem_mib=60,
-    )(*sources)
+    piece = units // 2
+    grads = ()
+    for i in range(2):
+        grads = call(
+            functools.partial(grads_kernel, i * piece),
+            [pltpu.HBM((capacity, units), BF16)] * 2,
+            [HBM] * (4 + len(grads)),
+            [pltpu.VMEM(scaled.shape, BF16)]
+            + [pltpu.VMEM((capacity, piece), BF16)] * 2
+            + [pltpu.VMEM((piece, features), BF16)]
+            + [pltpu.VMEM((capacity, piece), BF16)] * 2
+            + [pltpu.SemaphoreType.DMA((5,)), pltpu.SemaphoreType.DMA((2,))],
+            vmem_mib=60,
+            out_space=HBM,
+            aliases={4 + k: k for k in range(len(grads))},
+        )(*sources, *grads)
+    grad_gate, grad_up = grads
 
     terms = (group, 2 * share + 2 * share // 3, LANES)
     partial = call(

time: 127 us -> 129 us (1.016)
  Pallas kernels: 12.9 us -> 15.4 us
    pallas_call x2 -> x3, Pallas kernels: 7.04 us -> 9.53 us  [the longest x2 6.94 us: step_of(): call(functools.partial(grads_kernel, i * piece), [pltpu.HBM((capacity, un...]
  transfers between devices with their start and end apart: 11 -> 11, of which waited for: 7 -> 7; matrix products, arithmetic and copies ran while one was open for 2% -> 2% of each run, Pallas kernels for 5% -> 7%
where the time goes in v6:
time: 129 us; the launch traced here: 128 us
  waiting for transfers between devices  55.4 us (43%)
  starting transfers between devices  53.1 us (41%)
  Pallas kernels  15.4 us (12%)
  matrix products  2.92 us (2%)
    all_to_all x3, waiting for transfers between devices, exchange(): return lax.all_to_all(value, axes, split_axis=0, concat_axis=0, tiled=True)  30.9 us
    all_to_all x3, starting transfers between devices, exchange(): return lax.all_to_all(value, axes, split_axis=0, concat_axis=0, tiled=True)  26 us
    ppermute x4, starting transfers between devices, step_of(): other = lax.ppermute(grad_p, 'node', [(i, i ^ step) for i in range(n_node)])  13.2 us
    ppermute x4, waiting for transfers between devices, step_of(): other = lax.ppermute(grad_p, 'node', [(i, i ^ step) for i in range(n_node)])  11.3 us
    ppermute x3, starting transfers between devices, step_of(): lax.ppermute(hidden_pair, 'dp_0', [(i, (i + k) % n_0) for i in range(n_0)])  10.5 us
    ppermute x3, waiting for transfers between devices, step_of(): lax.ppermute(hidden_pair, 'dp_0', [(i, (i + k) % n_0) for i in range(n_0)])  7.11 us
    pallas_call x2, Pallas kernels, step_of(): call(functools.partial(grads_kernel, i * piece), [pltpu.HBM((capacity, un...  6.94 us
    ppermute x1, waiting for transfers between devices, step_of(): near = lax.ppermute(hidden, 'dp_2', [(0, 1), (1, 0)])  6.09 us
  transfers between devices with their start and end apart: 11, of which 7 were waited for; matrix products, arithmetic and copies ran while one was open for 2% of the time, Pallas kernels for 7%

profile of v6, /device:TPU:1, one launch (start us, length us, event | category | flops | bytes accessed | tf_op | source)
XLA Modules:
  0.0 128.0 jit_solution(7771501316893927343)
XLA Ops:
  0.7 2.6 %shard_map.111 = bf16[16,328,128]{2,1,0:T(8,128)(2,1)} custom-call(bf16[128,2560]{1,0:T(8,128)(2,1)} %refs_0_.1, bf16[6,128]{1,0:T(8,128)(2,1)} %bitcast.27, s32[3,128]{1,0:T(4,128)} %bitcast.19, s32[6,128]{1,0:T(8,128)} %bitcast.15, s32[6,128]{1,0:T(8,128)} %bitcast.17), custom_call_target="tpu_custom_call" | custom-call | tf_op jit(solution)/shard_map/pallas_call | solution.py:367
  3.3 11.8 %all-to-all-start = ((bf16[16,328,128]{2,1,0:T(8,128)(2,1)}), bf16[16,328,128]{2,1,0:T(8,128)(2,1)S(1)}, u32[]{:S(2)}, u32[]{:S(2)}) async-start(bf16[16,328,128]{2,1,0:T(8,128)(2,1)} %shard_map.111), calls=%async_computation | async-start | bytes 2686976 | tf_op jit(solution)/shard_map/all_to_all | solution.py:350
  15.2 2.9 %fusion.5.slot_out_ref = f32[80,2560]{1,0:T(8,128)S(1)} fusion(bf16[80,768]{1,0:T(8,128)(2,1)S(1)} %fusion.4, bf16[1,768,2560]{2,1,0:T(8,128)(2,1)} %param.15), kind=kOutput, calls=%fused_computation.12 | convolution fusion | flops 314572800 | bytes 4874240 | tf_op jit(solution)/shard_map/dot_general | solution.py:393
  18.1 30.9 %all-to-all-done.recv_ref = bf16[16,328,128]{2,1,0:T(8,128)(2,1)S(1)} async-done(((bf16[16,328,128]{2,1,0:T(8,128)(2,1)}), bf16[16,328,128]{2,1,0:T(8,128)(2,1)S(1)}, u32[]{:S(2)}, u32[]{:S(2)}) %all-to-all-start) | async-done | bytes 1343520 | tf_op jit(solution)/shard_map/all_to_all | solution.py:350
  49.0 1.6 %shard_map.112 = (bf16[80,2560]{1,0:T(8,128)(2,1)}, bf16[8,200,128]{2,1,0:T(8,128)(2,1)}, f32[1,128]{1,0:T(1,128)S(1)}) custom-call(bf16[16,328,128]{2,1,0:T(8,128)(2,1)S(1)} %all-to-all-done.recv_ref, f32[80,2560]{1,0:T(8,128)S(1)} %fusion.5.slot_out_ref), custom_call_target="tpu_custom_call" | custom-call | tf_op jit(solution)/shard_map/pallas_call | solution.py:396
  50.6 5.0 %all-to-all-start.1 = ((bf16[8,200,128]{2,1,0:T(8,128)(2,1)}), bf16[8,200,128]{2,1,0:T(8,128)(2,1)S(1)}, u32[]{:S(2)}, u32[]{:S(2)}) async-start(bf16[8,200,128]{2,1,0:T(8,128)(2,1)} %get-tuple-element.16), calls=%async_computation.1 | async-start | bytes 819200 | tf_op jit(solution)/shard_map/all_to_all | solution.py:350
  55.7 3.4 %collective-permute-start = (bf16[80,768]{1,0:T(8,128)(2,1)S(1)}, bf16[80,768]{1,0:T(8,128)(2,1)S(1)}, u32[]{:S(2)}, u32[]{:S(2)}) collective-permute-start(bf16[80,768]{1,0:T(8,128)(2,1)S(1)} %fusion.4), channel_id=1, source_target_pairs={{0,1},{1,0},{2,3},{3,2},{4,5},{5,4},{6,7},{7,6},{8,9},{9,8},{10,11... | collective-permute-start | bytes 368648 | tf_op jit(solution)/shard_map/ppermute | solution.py:382
  59.0 6.1 %collective-permute-done = bf16[80,768]{1,0:T(8,128)(2,1)S(1)} collective-permute-done((bf16[80,768]{1,0:T(8,128)(2,1)S(1)}, bf16[80,768]{1,0:T(8,128)(2,1)S(1)}, u32[]{:S(2)}, u32[]{:S(2)}) %collective-permute-start) | collective-permute-done | bytes 122912 | tf_op jit(solution)/shard_map/ppermute | solution.py:382
  65.2 3.1 %collective-permute-start.1 = (bf16[2,80,768]{2,1,0:T(8,128)(2,1)S(1)}, bf16[2,80,768]{2,1,0:T(8,128)(2,1)S(1)}, u32[]{:S(2)}, u32[]{:S(2)}) collective-permute-start(bf16[2,80,768]{2,1,0:T(8,128)(2,1)S(1)} %pad_maximum_fusion.refs_0_), channel_id=1, source_target_pairs={{0,8},{8,16},{16,24},{24,0},{1,9},{9,17},{17,25},{25,1},{2,10},{10... | collective-permute-start | bytes 737288 | tf_op jit(solution)/shard_map/ppermute | solution.py:386
  68.3 4.3 %collective-permute-start.2 = (bf16[2,80,768]{2,1,0:T(8,128)(2,1)S(1)}, bf16[2,80,768]{2,1,0:T(8,128)(2,1)S(1)}, u32[]{:S(2)}, u32[]{:S(2)}) collective-permute-start(bf16[2,80,768]{2,1,0:T(8,128)(2,1)S(1)} %pad_maximum_fusion.refs_0_), channel_id=1, source_target_pairs={{0,16},{8,24},{16,0},{24,8},{1,17},{9,25},{17,1},{25,9},{2,18},{10... | collective-permute-start | bytes 737288 | tf_op jit(solution)/shard_map/ppermute | solution.py:386
  72.6 3.0 %collective-permute-start.3 = (bf16[2,80,768]{2,1,0:T(8,128)(2,1)S(1)}, bf16[2,80,768]{2,1,0:T(8,128)(2,1)S(1)}, u32[]{:S(2)}, u32[]{:S(2)}) collective-permute-start(bf16[2,80,768]{2,1,0:T(8,128)(2,1)S(1)} %pad_maximum_fusion.refs_0_), channel_id=1, source_target_pairs={{0,24},{8,0},{16,8},{24,16},{1,25},{9,1},{17,9},{25,17},{2,26},{10... | collective-permute-start | bytes 737288 | tf_op jit(solution)/shard_map/ppermute | solution.py:386
  75.8 5.8 %collective-permute-done.2.refs_2_ = bf16[2,80,768]{2,1,0:T(8,128)(2,1)S(1)} collective-permute-done((bf16[2,80,768]{2,1,0:T(8,128)(2,1)S(1)}, bf16[2,80,768]{2,1,0:T(8,128)(2,1)S(1)}, u32[]{:S(2)}, u32[]{:S(2)}) %collective-permute-start.2) | collective-permute-done | bytes 245792 | tf_op jit(solution)/shard_map/ppermute | solution.py:386
  81.6 1.3 collective-permute-done.3.refs_3_
  83.9 1.5 %shard_map.116 = bf16[32,64,128]{2,1,0:T(8,128)(2,1)} custom-call(bf16[768,640]{1,0:T(8,128)(2,1)S(1)} %shard_map.115.hidden_ref, bf16[8,200,128]{2,1,0:T(8,128)(2,1)S(1)} %all-to-all-done.1.parts_ref), custom_call_target="tpu_custom_call" | custom-call | tf_op jit(solution)/shard_map/pallas_call | solution.py:433
  85.4 9.2 %all-to-all-start.2 = ((bf16[32,64,128]{2,1,0:T(8,128)(2,1)}), bf16[32,64,128]{2,1,0:T(8,128)(2,1)S(1)}, u32[]{:S(2)}, u32[]{:S(2)}) async-start(bf16[32,64,128]{2,1,0:T(8,128)(2,1)} %shard_map.116), calls=%async_computation.2 | async-start | bytes 1048576 | tf_op jit(solution)/shard_map/all_to_all | solution.py:350
  94.6 2.8 %collective-permute-start.4 = (f32[1,128]{1,0:T(1,128)S(1)}, f32[1,128]{1,0:T(1,128)S(1)}, u32[]{:S(2)}, u32[]{:S(2)}) collective-permute-start(f32[1,128]{1,0:T(1,128)S(1)} %get-tuple-element.17), channel_id=1, source_target_pairs={{0,256},{32,288},{64,320},{96,352},{128,384},{160,416},{192,448},{... | collective-permute-start | bytes 1544 | tf_op jit(solution)/shard_map/ppermute | solution.py:447
  97.4 5.4 %collective-permute-done.4 = f32[1,128]{1,0:T(1,128)S(1)} collective-permute-done((f32[1,128]{1,0:T(1,128)S(1)}, f32[1,128]{1,0:T(1,128)S(1)}, u32[]{:S(2)}, u32[]{:S(2)}) %collective-permute-start.4) | collective-permute-done | bytes 544 | tf_op jit(solution)/shard_map/ppermute | solution.py:447
  102.8 2.0 %collective-permute-start.5 = (f32[2,128]{1,0:T(2,128)S(1)}, f32[2,128]{1,0:T(2,128)S(1)}, u32[]{:S(2)}, u32[]{:S(2)}) collective-permute-start(f32[2,128]{1,0:T(2,128)S(1)} %pad_maximum_fusion.3), channel_id=1, source_target_pairs={{0,128},{32,160},{64,192},{96,224},{128,0},{160,32},{192,64},{224,... | collective-permute-start | bytes 3080 | tf_op jit(solution)/shard_map/ppermute | solution.py:447
  104.9 3.5 %collective-permute-done.5 = f32[2,128]{1,0:T(2,128)S(1)} collective-permute-done((f32[2,128]{1,0:T(2,128)S(1)}, f32[2,128]{1,0:T(2,128)S(1)}, u32[]{:S(2)}, u32[]{:S(2)}) %collective-permute-start.5) | collective-permute-done | bytes 1056 | tf_op jit(solution)/shard_map/ppermute | solution.py:447
  108.4 1.9 %collective-permute-start.6 = (f32[4,128]{1,0:T(4,128)S(1)}, f32[4,128]{1,0:T(4,128)S(1)}, u32[]{:S(2)}, u32[]{:S(2)}) collective-permute-start(f32[4,128]{1,0:T(4,128)S(1)} %pad_maximum_fusion.2), channel_id=1, source_target_pairs={{0,64},{32,96},{64,0},{96,32},{128,192},{160,224},{192,128},{224,1... | collective-permute-start | bytes 6152 | tf_op jit(solution)/shard_map/ppermute | solution.py:447
  110.3 2.4 %collective-permute-done.6 = f32[4,128]{1,0:T(4,128)S(1)} collective-permute-done((f32[4,128]{1,0:T(4,128)S(1)}, f32[4,128]{1,0:T(4,128)S(1)}, u32[]{:S(2)}, u32[]{:S(2)}) %collective-permute-start.6) | collective-permute-done | bytes 2080 | tf_op jit(solution)/shard_map/ppermute | solution.py:447
  112.7 6.5 %collective-permute-start.7 = (f32[8,128]{1,0:T(8,128)S(1)}, f32[8,128]{1,0:T(8,128)S(1)}, u32[]{:S(2)}, u32[]{:S(2)}) collective-permute-start(f32[8,128]{1,0:T(8,128)S(1)} %pad_maximum_fusion.1), channel_id=1, source_target_pairs={{0,32},{32,0},{64,96},{96,64},{128,160},{160,128},{192,224},{224,1... | collective-permute-start | bytes 12296 | tf_op jit(solution)/shard_map/ppermute | solution.py:447
  119.2 3.5 %shard_map.113 = (bf16[80,768]{1,0:T(8,128)(2,1)}, bf16[80,768]{1,0:T(8,128)(2,1)}) custom-call(bf16[80,2560]{1,0:T(8,128)(2,1)} %get-tuple-element.11.refs_0_, bf16[80,768]{1,0:T(8,128)(2,1)} %refs_1_.3, bf16[80,768]{1,0:T(8,128)(2,1)} %refs_2_.3, bf16[768,2560]{1,0:T(8,128)(2,1)} %bitcast.21), custom_call_target="tpu_custom_call" | custom-call | tf_op jit(solution)/shard_map/pallas_call | solution.py:417
  122.7 3.5 %shard_map.114 = (bf16[80,768]{1,0:T(8,128)(2,1)}, bf16[80,768]{1,0:T(8,128)(2,1)}) custom-call(bf16[80,2560]{1,0:T(8,128)(2,1)} %get-tuple-element.11.refs_0_, bf16[80,768]{1,0:T(8,128)(2,1)} %refs_1_.3, bf16[80,768]{1,0:T(8,128)(2,1)} %refs_2_.3, bf16[768,2560]{1,0:T(8,128)(2,1)} %bitcast.22, ...), custom_call_target="tpu_custom_call", output_to_operand_aliasing={{0}: (4, {}), {1}: (5, {})} | custom-call | tf_op jit(solution)/shard_map/pallas_call | solution.py:417
  (24 shorter events, 3.0 us)
Async XLA Ops:
  0.6 14.5 %copy-start.4 = (bf16[80,768]{1,0:T(8,128)(2,1)S(1)}, bf16[80,768]{1,0:T(8,128)(2,1)}, u32[]{:S(2)}) copy-start(bf16[80,768]{1,0:T(8,128)(2,1)} %refs_1_.3) | copy-start | bytes 368644
  0.6 14.4 %copy-start.3 = (bf16[80,768]{1,0:T(8,128)(2,1)S(1)}, bf16[80,768]{1,0:T(8,128)(2,1)}, u32[]{:S(2)}) copy-start(bf16[80,768]{1,0:T(8,128)(2,1)} %refs_2_.3) | copy-start | bytes 368644
  3.3 45.7 %all-to-all-start = ((bf16[16,328,128]{2,1,0:T(8,128)(2,1)}), bf16[16,328,128]{2,1,0:T(8,128)(2,1)S(1)}, u32[]{:S(2)}, u32[]{:S(2)}) async-start(bf16[16,328,128]{2,1,0:T(8,128)(2,1)} %shard_map.111), calls=%async_computation | async-start | bytes 2686976 | tf_op jit(solution)/shard_map/all_to_all | solution.py:350
  50.6 33.3 %all-to-all-start.1 = ((bf16[8,200,128]{2,1,0:T(8,128)(2,1)}), bf16[8,200,128]{2,1,0:T(8,128)(2,1)S(1)}, u32[]{:S(2)}, u32[]{:S(2)}) async-start(bf16[8,200,128]{2,1,0:T(8,128)(2,1)} %get-tuple-element.16), calls=%async_computation.1 | async-start | bytes 819200 | tf_op jit(solution)/shard_map/all_to_all | solution.py:350
  55.7 9.5 %collective-permute-start = (bf16[80,768]{1,0:T(8,128)(2,1)S(1)}, bf16[80,768]{1,0:T(8,128)(2,1)S(1)}, u32[]{:S(2)}, u32[]{:S(2)}) collective-permute-start(bf16[80,768]{1,0:T(8,128)(2,1)S(1)} %fusion.4), channel_id=1, source_target_pairs={{0,1},{1,0},{2,3},{3,2},{4,5},{5,4},{6,7},{7,6},{8,9},{9,8},{10,11... | collective-permute-start | bytes 368648 | tf_op jit(solution)/shard_map/ppermute | solution.py:382
  65.2 10.6 %collective-permute-start.1 = (bf16[2,80,768]{2,1,0:T(8,128)(2,1)S(1)}, bf16[2,80,768]{2,1,0:T(8,128)(2,1)S(1)}, u32[]{:S(2)}, u32[]{:S(2)}) collective-permute-start(bf16[2,80,768]{2,1,0:T(8,128)(2,1)S(1)} %pad_maximum_fusion.refs_0_), channel_id=1, source_target_pairs={{0,8},{8,16},{16,24},{24,0},{1,9},{9,17},{17,25},{25,1},{2,10},{10... | collective-permute-start | bytes 737288 | tf_op jit(solution)/shard_map/ppermute | solution.py:386
  68.3 13.3 %collective-permute-start.2 = (bf16[2,80,768]{2,1,0:T(8,128)(2,1)S(1)}, bf16[2,80,768]{2,1,0:T(8,128)(2,1)S(1)}, u32[]{:S(2)}, u32[]{:S(2)}) collective-permute-start(bf16[2,80,768]{2,1,0:T(8,128)(2,1)S(1)} %pad_maximum_fusion.refs_0_), channel_id=1, source_target_pairs={{0,16},{8,24},{16,0},{24,8},{1,17},{9,25},{17,1},{25,9},{2,18},{10... | collective-permute-start | bytes 737288 | tf_op jit(solution)/shard_map/ppermute | solution.py:386
  72.6 10.2 %collective-permute-start.3 = (bf16[2,80,768]{2,1,0:T(8,128)(2,1)S(1)}, bf16[2,80,768]{2,1,0:T(8,128)(2,1)S(1)}, u32[]{:S(2)}, u32[]{:S(2)}) collective-permute-start(bf16[2,80,768]{2,1,0:T(8,128)(2,1)S(1)} %pad_maximum_fusion.refs_0_), channel_id=1, source_target_pairs={{0,24},{8,0},{16,8},{24,16},{1,25},{9,1},{17,9},{25,17},{2,26},{10... | collective-permute-start | bytes 737288 | tf_op jit(solution)/shard_map/ppermute | solution.py:386
  85.4 41.8 %all-to-all-start.2 = ((bf16[32,64,128]{2,1,0:T(8,128)(2,1)}), bf16[32,64,128]{2,1,0:T(8,128)(2,1)S(1)}, u32[]{:S(2)}, u32[]{:S(2)}) async-start(bf16[32,64,128]{2,1,0:T(8,128)(2,1)} %shard_map.116), calls=%async_computation.2 | async-start | bytes 1048576 | tf_op jit(solution)/shard_map/all_to_all | solution.py:350
  94.6 8.2 %collective-permute-start.4 = (f32[1,128]{1,0:T(1,128)S(1)}, f32[1,128]{1,0:T(1,128)S(1)}, u32[]{:S(2)}, u32[]{:S(2)}) collective-permute-start(f32[1,128]{1,0:T(1,128)S(1)} %get-tuple-element.17), channel_id=1, source_target_pairs={{0,256},{32,288},{64,320},{96,352},{128,384},{160,416},{192,448},{... | collective-permute-start | bytes 1544 | tf_op jit(solution)/shard_map/ppermute | solution.py:447
  102.8 5.5 %collective-permute-start.5 = (f32[2,128]{1,0:T(2,128)S(1)}, f32[2,128]{1,0:T(2,128)S(1)}, u32[]{:S(2)}, u32[]{:S(2)}) collective-permute-start(f32[2,128]{1,0:T(2,128)S(1)} %pad_maximum_fusion.3), channel_id=1, source_target_pairs={{0,128},{32,160},{64,192},{96,224},{128,0},{160,32},{192,64},{224,... | collective-permute-start | bytes 3080 | tf_op jit(solution)/shard_map/ppermute | solution.py:447
  108.4 4.3 %collective-permute-start.6 = (f32[4,128]{1,0:T(4,128)S(1)}, f32[4,128]{1,0:T(4,128)S(1)}, u32[]{:S(2)}, u32[]{:S(2)}) collective-permute-start(f32[4,128]{1,0:T(4,128)S(1)} %pad_maximum_fusion.2), channel_id=1, source_target_pairs={{0,64},{32,96},{64,0},{96,32},{128,192},{160,224},{192,128},{224,1... | collective-permute-start | bytes 6152 | tf_op jit(solution)/shard_map/ppermute | solution.py:447
  112.7 13.5 %collective-permute-start.7 = (f32[8,128]{1,0:T(8,128)S(1)}, f32[8,128]{1,0:T(8,128)S(1)}, u32[]{:S(2)}, u32[]{:S(2)}) collective-permute-start(f32[8,128]{1,0:T(8,128)S(1)} %pad_maximum_fusion.1), channel_id=1, source_target_pairs={{0,32},{32,0},{64,96},{96,64},{128,160},{160,128},{192,224},{224,1... | collective-permute-start | bytes 12296 | tf_op jit(solution)/shard_map/ppermute | solution.py:447
  119.2 7.0 %copy-start = (s32[128,6]{0,1:T(8,128)S(1)}, s32[128,6]{0,1:T(8,128)}, u32[]{:S(2)}) copy-start(s32[128,6]{0,1:T(8,128)} %param.11) | copy-start | bytes 9220
  119.2 7.0 %copy-start.1 = (s32[128,6]{0,1:T(8,128)S(1)}, s32[128,6]{0,1:T(8,128)}, u32[]{:S(2)}) copy-start(s32[128,6]{0,1:T(8,128)} %param.12) | copy-start | bytes 9220
  119.2 7.0 %copy-start.2 = (s32[128,3]{0,1:T(4,128)S(1)}, s32[128,3]{0,1:T(4,128)}, u32[]{:S(2)}) copy-start(s32[128,3]{0,1:T(4,128)} %param.10) | copy-start | bytes 4612

commit v7 on v6

--- a/solution.py
+++ b/solution.py
@@ -16,6 +16,7 @@
 NODE_DP = ("node", *DP)
 TEAM = ("dp_0", "dp_2")
 HALF = LANES // 2
+PIECES = 3
 OUT_PIECES = 4
 F32 = jnp.float32
 BF16 = jnp.bfloat16
@@ -246,67 +247,57 @@
         put(2 * third, tile, jnp.where(low, last_0, pltpu.roll(last_1, HALF, 1)))
 
 
-def grads_kernel(first, *refs):
-    sources, (gate_out_ref, up_out_ref) = refs[:4], refs[-10:-8]
-    scaled_ref, gate_ref, up_ref, weight_ref, gate_grad_ref, up_grad_ref = refs[-8:-2]
-    arrived, left = [refs[-2].at[i] for i in range(5)], refs[-1]
+def grads_kernel(*refs):
+    sources, grad_gate_ref, grad_up_ref = refs[:4], refs[4], refs[5]
+    (scaled_ref, gate_ref, up_ref, weight_ref), arrived = refs[6:10], refs[10]
+    copies = [
+        pltpu.make_async_copy(source, place, arrived.at[i])
+        for i, (source, place) in enumerate(zip(sources[:3], refs[6:9]))
+    ]
     units = weight_ref.shape[0]
-    piece = units // 2
-    columns = pl.ds(first, units)
-    copies = [
-        pltpu.make_async_copy(sources[0], scaled_ref, arrived[0]),
-        pltpu.make_async_copy(sources[1].at[:, columns], gate_ref, arrived[1]),
-        pltpu.make_async_copy(sources[2].at[:, columns], up_ref, arrived[2]),
-    ]
-    for i in range(2):
+    piece = units // PIECES
+    for i in range(PIECES):
+        rows = pl.ds(i * piece, piece)
         copies.append(
-            pltpu.make_async_copy(
-                sources[3].at[pl.ds(first + i * piece, piece)],
-                weight_ref.at[pl.ds(i * piece, piece)],
-                arrived[3 + i],
-            )
+            pltpu.make_async_copy(sources[3].at[rows], weight_ref.at[rows], arrived.at[3 + i])
         )
     for copy in copies:
         copy.start()
     for copy in copies[:3]:
         copy.wait()
-    for i in range(2):
+    for i in range(PIECES):
         copies[3 + i].wait()
-        here = slice(i * piece, (i + 1) * piece)
+        rows = slice(i * piece, (i + 1) * piece)
         d_hidden = lax.dot_general(
             scaled_ref[...],
-            weight_ref[here],
+            weight_ref[rows],
             (((1,), (1,)), ((), ())),
             preferred_element_type=F32,
         )
-        gate, up = gate_ref[:, here].astype(F32), up_ref[:, here].astype(F32)
+        gate, up = gate_ref[:, rows].astype(F32), up_ref[:, rows].astype(F32)
         sigmoid = jax.nn.sigmoid(gate)
         slope = sigmoid * (1.0 + gate * (1.0 - sigmoid))
-        gate_grad_ref[:, here] = (d_hidden * up * slope).astype(BF16)
-        up_grad_ref[:, here] = (d_hidden * (gate * sigmoid)).astype(BF16)
-    copies = [
-        pltpu.make_async_copy(gate_grad_ref, gate_out_ref.at[:, columns], left.at[0]),
-        pltpu.make_async_copy(up_grad_ref, up_out_ref.at[:, columns], left.at[1]),
-    ]
-    for copy in copies:
-        copy.start()
-    for copy in copies:
-        copy.wait()
-
-
-def return_kernel(steps, me_ref, grad_p_ref, presel_ref, expert_ref, slot_ref, out_ref):
-    n_node = grad_p_ref.shape[0]
+        grad_gate_ref[:, rows] = (d_hidden * up * slope).astype(BF16)
+        grad_up_ref[:, rows] = (d_hidden * (gate * sigmoid)).astype(BF16)
+
+
+def return_kernel(offsets, chips, me_ref, grad_p_ref, presel_ref, expert_ref, slot_ref, out_ref):
     tokens = presel_ref.shape[1]
+    row = lax.broadcasted_iota(jnp.int32, (grad_p_ref.shape[0], tokens), 0)
+    node = jnp.full(row.shape, -1)
+    offsets = [o % chips for o in offsets]
+    for i, offset in enumerate(offsets):
+        if offset in offsets[:i]:
+            continue
+        for flip in range(2):
+            held = lax.rem(me_ref[0] // 2 + offset, chips) * 2 + (me_ref[0] % 2 ^ flip)
+            node = jnp.where(row == flip * len(offsets) + i, held, node)
     expert, slot, presel = expert_ref[...], slot_ref[...], presel_ref[...]
     slots = columns_of_routes(expert, slot, slot + 1)
-    row = lax.broadcasted_iota(jnp.int32, (n_node, tokens), 0)
-    away = jnp.zeros((n_node, tokens), jnp.int32)
-    for bit, step in enumerate(steps):
-        away = jnp.where((row >> bit) & 1 == 1, away | step, away)
     slot_ids = lax.broadcasted_iota(jnp.int32, (LANES, tokens), 0)
     here = jnp.concatenate(
         [
-            jnp.where((presel[c : c + 1] ^ me_ref[0]) == away, 1.0, 0.0)
+            jnp.where(presel[c : c + 1] == node, 1.0, 0.0)
             for c in range(PRESEL)
         ],
         axis=1,
@@ -411,23 +402,14 @@
     parts = exchange(parts, TEAM)
 
     sources = (scaled, gate_pre, up_pre, weight)
-    piece = units // 2
-    grads = ()
-    for i in range(2):
-        grads = call(
-            functools.partial(grads_kernel, i * piece),
-            [pltpu.HBM((capacity, units), BF16)] * 2,
-            [HBM] * (4 + len(grads)),
-            [pltpu.VMEM(scaled.shape, BF16)]
-            + [pltpu.VMEM((capacity, piece), BF16)] * 2
-            + [pltpu.VMEM((piece, features), BF16)]
-            + [pltpu.VMEM((capacity, piece), BF16)] * 2
-            + [pltpu.SemaphoreType.DMA((5,)), pltpu.SemaphoreType.DMA((2,))],
-            vmem_mib=60,
-            out_space=HBM,
-            aliases={4 + k: k for k in range(len(grads))},
-        )(*sources, *grads)
-    grad_gate, grad_up = grads
+    grad_gate, grad_up = call(
+        grads_kernel,
+        [shape((capacity, units), BF16)] * 2,
+        [HBM] * 4,
+        [pltpu.VMEM(a.shape, a.dtype) for a in sources]
+        + [pltpu.SemaphoreType.DMA((3 + PIECES,))],
+        vmem_mib=60,
+    )(*sources)
 
     terms = (group, 2 * share + 2 * share // 3, LANES)
     partial = call(
@@ -442,12 +424,23 @@
         functools.partial(sum_kernel, n_0, n_1), shape((share, features), BF16), [VMEM]
     )(terms)[None]
 
-    steps = [n_node >> (i + 1) for i in range(n_node.bit_length() - 1)]
-    for step in steps:
-        other = lax.ppermute(grad_p, "node", [(i, i ^ step) for i in range(n_node)])
-        grad_p = jnp.concatenate([grad_p, other])
+    chips = n_node // 2
+    offsets = [0]
+    for step in (3, 1):
+        rows = [grad_p]
+        for sign in (1, -1):
+            pairs = [
+                (2 * ((i + sign * step) % chips) + core, 2 * i + core)
+                for i in range(chips)
+                for core in range(2)
+            ]
+            rows.append(lax.ppermute(grad_p, "node", pairs))
+        grad_p = jnp.concatenate(rows)
+        offsets = offsets + [o + step for o in offsets] + [o - step for o in offsets]
+    other = lax.ppermute(grad_p, "node", [(i, i ^ 1) for i in range(n_node)])
+    grad_p = jnp.concatenate([grad_p, other])
     grad_prob = call(
-        functools.partial(return_kernel, steps),
+        functools.partial(return_kernel, offsets, chips),
         shape(route_expert.shape[::-1], F32),
         [SMEM] + [VMEM] * 4,
     )(lax.axis_index("node")[None], grad_p, presel, expert, slot).T

time: 129 us -> 126 us (0.977)
  waiting for transfers between devices: 55.4 us -> 49.5 us
  starting transfers between devices: 53.1 us -> 58.2 us
  Pallas kernels: 15.4 us -> 12.9 us
    ppermute x4 -> x5, waiting for transfers between devices: 11.3 us -> 5.36 us  [the longest x4 5.35 us: step_of(): rows.append(lax.ppermute(grad_p, 'node', pairs))]
    ppermute x4 -> x5, starting transfers between devices: 13.2 us -> 18.3 us  [the longest x4 12.4 us: step_of(): rows.append(lax.ppermute(grad_p, 'node', pairs))]
    pallas_call x3 -> x2, Pallas kernels: 7.91 us -> 5.42 us  [the longest x1 4.46 us: step_of(): call(grads_kernel, [shape((capacity, units), BF16)] * 2, [HBM] * 4, [pltp...]
  transfers between devices with their start and end apart: 11 -> 12, of which waited for: 7 -> 6; matrix products, arithmetic and copies ran while one was open for 2% -> 3% of each run, Pallas kernels for 7% -> 5%
where the time goes in v7:
time: 126 us; the launch traced here: 125 us
  starting transfers between devices  58.2 us (46%)
  waiting for transfers between devices  49.5 us (39%)
  Pallas kernels  12.9 us (10%)
  matrix products  2.92 us (2%)
    all_to_all x3, waiting for transfers between devices, exchange(): return lax.all_to_all(value, axes, split_axis=0, concat_axis=0, tiled=True)  30.9 us
    all_to_all x3, starting transfers between devices, exchange(): return lax.all_to_all(value, axes, split_axis=0, concat_axis=0, tiled=True)  26 us
    ppermute x4, starting transfers between devices, step_of(): rows.append(lax.ppermute(grad_p, 'node', pairs))  12.4 us
    ppermute x3, starting transfers between devices, step_of(): lax.ppermute(hidden_pair, 'dp_0', [(i, (i + k) % n_0) for i in range(n_0)])  10.5 us
    ppermute x3, waiting for transfers between devices, step_of(): lax.ppermute(hidden_pair, 'dp_0', [(i, (i + k) % n_0) for i in range(n_0)])  7.11 us
    ppermute x1, waiting for transfers between devices, step_of(): near = lax.ppermute(hidden, 'dp_2', [(0, 1), (1, 0)])  6.09 us
    ppermute x1, starting transfers between devices, step_of(): other = lax.ppermute(grad_p, 'node', [(i, i ^ 1) for i in range(n_node)])  5.93 us
    ppermute x4, waiting for transfers between devices, step_of(): rows.append(lax.ppermute(grad_p, 'node', pairs))  5.35 us
  transfers between devices with their start and end apart: 12, of which 6 were waited for; matrix products, arithmetic and copies ran while one was open for 3% of the time, Pallas kernels for 5%

profile of v7, /device:TPU:1, one launch (start us, length us, event | category | flops | bytes accessed | tf_op | source)
XLA Modules:
  0.0 124.9 jit_solution(10153480373355993183)
XLA Ops:
  0.7 2.6 %shard_map.111 = bf16[16,328,128]{2,1,0:T(8,128)(2,1)} custom-call(bf16[128,2560]{1,0:T(8,128)(2,1)} %refs_0_.1, bf16[6,128]{1,0:T(8,128)(2,1)} %bitcast.26, s32[3,128]{1,0:T(4,128)} %bitcast.19, s32[6,128]{1,0:T(8,128)} %bitcast.15, s32[6,128]{1,0:T(8,128)} %bitcast.17), custom_call_target="tpu_custom_call" | custom-call | tf_op jit(solution)/shard_map/pallas_call | solution.py:358
  3.3 11.8 %all-to-all-start = ((bf16[16,328,128]{2,1,0:T(8,128)(2,1)}), bf16[16,328,128]{2,1,0:T(8,128)(2,1)S(1)}, u32[]{:S(2)}, u32[]{:S(2)}) async-start(bf16[16,328,128]{2,1,0:T(8,128)(2,1)} %shard_map.111), calls=%async_computation | async-start | bytes 2686976 | tf_op jit(solution)/shard_map/all_to_all | solution.py:341
  15.2 2.9 %fusion.5.slot_out_ref = f32[80,2560]{1,0:T(8,128)S(1)} fusion(bf16[80,768]{1,0:T(8,128)(2,1)S(1)} %fusion.4, bf16[1,768,2560]{2,1,0:T(8,128)(2,1)} %param.15), kind=kOutput, calls=%fused_computation.10 | convolution fusion | flops 314572800 | bytes 4874240 | tf_op jit(solution)/shard_map/dot_general | solution.py:384
  18.1 30.9 %all-to-all-done.recv_ref = bf16[16,328,128]{2,1,0:T(8,128)(2,1)S(1)} async-done(((bf16[16,328,128]{2,1,0:T(8,128)(2,1)}), bf16[16,328,128]{2,1,0:T(8,128)(2,1)S(1)}, u32[]{:S(2)}, u32[]{:S(2)}) %all-to-all-start) | async-done | bytes 1343520 | tf_op jit(solution)/shard_map/all_to_all | solution.py:341
  49.0 1.6 %shard_map.112 = (bf16[80,2560]{1,0:T(8,128)(2,1)}, bf16[8,200,128]{2,1,0:T(8,128)(2,1)}, f32[1,128]{1,0:T(1,128)S(1)}) custom-call(bf16[16,328,128]{2,1,0:T(8,128)(2,1)S(1)} %all-to-all-done.recv_ref, f32[80,2560]{1,0:T(8,128)S(1)} %fusion.5.slot_out_ref), custom_call_target="tpu_custom_call" | custom-call | tf_op jit(solution)/shard_map/pallas_call | solution.py:387
  50.6 5.0 %all-to-all-start.1 = ((bf16[8,200,128]{2,1,0:T(8,128)(2,1)}), bf16[8,200,128]{2,1,0:T(8,128)(2,1)S(1)}, u32[]{:S(2)}, u32[]{:S(2)}) async-start(bf16[8,200,128]{2,1,0:T(8,128)(2,1)} %get-tuple-element.12), calls=%async_computation.1 | async-start | bytes 819200 | tf_op jit(solution)/shard_map/all_to_all | solution.py:341
  55.7 3.4 %collective-permute-start = (bf16[80,768]{1,0:T(8,128)(2,1)S(1)}, bf16[80,768]{1,0:T(8,128)(2,1)S(1)}, u32[]{:S(2)}, u32[]{:S(2)}) collective-permute-start(bf16[80,768]{1,0:T(8,128)(2,1)S(1)} %fusion.4), channel_id=1, source_target_pairs={{0,1},{1,0},{2,3},{3,2},{4,5},{5,4},{6,7},{7,6},{8,9},{9,8},{10,11... | collective-permute-start | bytes 368648 | tf_op jit(solution)/shard_map/ppermute | solution.py:373
  59.0 6.1 %collective-permute-done = bf16[80,768]{1,0:T(8,128)(2,1)S(1)} collective-permute-done((bf16[80,768]{1,0:T(8,128)(2,1)S(1)}, bf16[80,768]{1,0:T(8,128)(2,1)S(1)}, u32[]{:S(2)}, u32[]{:S(2)}) %collective-permute-start) | collective-permute-done | bytes 122912 | tf_op jit(solution)/shard_map/ppermute | solution.py:373
  65.2 3.1 %collective-permute-start.1 = (bf16[2,80,768]{2,1,0:T(8,128)(2,1)S(1)}, bf16[2,80,768]{2,1,0:T(8,128)(2,1)S(1)}, u32[]{:S(2)}, u32[]{:S(2)}) collective-permute-start(bf16[2,80,768]{2,1,0:T(8,128)(2,1)S(1)} %pad_maximum_fusion.refs_0_), channel_id=1, source_target_pairs={{0,8},{8,16},{16,24},{24,0},{1,9},{9,17},{17,25},{25,1},{2,10},{10... | collective-permute-start | bytes 737288 | tf_op jit(solution)/shard_map/ppermute | solution.py:377
  68.3 4.3 %collective-permute-start.2 = (bf16[2,80,768]{2,1,0:T(8,128)(2,1)S(1)}, bf16[2,80,768]{2,1,0:T(8,128)(2,1)S(1)}, u32[]{:S(2)}, u32[]{:S(2)}) collective-permute-start(bf16[2,80,768]{2,1,0:T(8,128)(2,1)S(1)} %pad_maximum_fusion.refs_0_), channel_id=1, source_target_pairs={{0,16},{8,24},{16,0},{24,8},{1,17},{9,25},{17,1},{25,9},{2,18},{10... | collective-permute-start | bytes 737288 | tf_op jit(solution)/shard_map/ppermute | solution.py:377
  72.6 3.0 %collective-permute-start.3 = (bf16[2,80,768]{2,1,0:T(8,128)(2,1)S(1)}, bf16[2,80,768]{2,1,0:T(8,128)(2,1)S(1)}, u32[]{:S(2)}, u32[]{:S(2)}) collective-permute-start(bf16[2,80,768]{2,1,0:T(8,128)(2,1)S(1)} %pad_maximum_fusion.refs_0_), channel_id=1, source_target_pairs={{0,24},{8,0},{16,8},{24,16},{1,25},{9,1},{17,9},{25,17},{2,26},{10... | collective-permute-start | bytes 737288 | tf_op jit(solution)/shard_map/ppermute | solution.py:377
  75.8 5.8 %collective-permute-done.2.refs_2_ = bf16[2,80,768]{2,1,0:T(8,128)(2,1)S(1)} collective-permute-done((bf16[2,80,768]{2,1,0:T(8,128)(2,1)S(1)}, bf16[2,80,768]{2,1,0:T(8,128)(2,1)S(1)}, u32[]{:S(2)}, u32[]{:S(2)}) %collective-permute-start.2) | collective-permute-done | bytes 245792 | tf_op jit(solution)/shard_map/ppermute | solution.py:377
  81.6 1.3 %collective-permute-done.3.refs_3_ = bf16[2,80,768]{2,1,0:T(8,128)(2,1)S(1)} collective-permute-done((bf16[2,80,768]{2,1,0:T(8,128)(2,1)S(1)}, bf16[2,80,768]{2,1,0:T(8,128)(2,1)S(1)}, u32[]{:S(2)}, u32[]{:S(2)}) %collective-permute-start.3) | collective-permute-done | bytes 245792 | tf_op jit(solution)/shard_map/ppermute | solution.py:377
  82.9 1.0 shard_map.114.hidden_ref
  83.9 1.5 %shard_map.115 = bf16[32,64,128]{2,1,0:T(8,128)(2,1)} custom-call(bf16[768,640]{1,0:T(8,128)(2,1)S(1)} %shard_map.114.hidden_ref, bf16[8,200,128]{2,1,0:T(8,128)(2,1)S(1)} %all-to-all-done.1.parts_ref), custom_call_target="tpu_custom_call" | custom-call | tf_op jit(solution)/shard_map/pallas_call | solution.py:415
  85.5 9.2 %all-to-all-start.2 = ((bf16[32,64,128]{2,1,0:T(8,128)(2,1)}), bf16[32,64,128]{2,1,0:T(8,128)(2,1)S(1)}, u32[]{:S(2)}, u32[]{:S(2)}) async-start(bf16[32,64,128]{2,1,0:T(8,128)(2,1)} %shard_map.115), calls=%async_computation.2 | async-start | bytes 1048576 | tf_op jit(solution)/shard_map/all_to_all | solution.py:341
  94.6 1.9 %collective-permute-start.4 = (f32[1,128]{1,0:T(1,128)S(1)}, f32[1,128]{1,0:T(1,128)S(1)}, u32[]{:S(2)}, u32[]{:S(2)}) collective-permute-start(f32[1,128]{1,0:T(1,128)S(1)} %get-tuple-element.13), channel_id=1, source_target_pairs={{192,0},{224,32},{256,64},{288,96},{320,128},{352,160},{384,192},{... | collective-permute-start | bytes 1544 | tf_op jit(solution)/shard_map/ppermute | solution.py:437
  96.6 5.2 %collective-permute-start.5 = (f32[1,128]{1,0:T(1,128)S(1)}, f32[1,128]{1,0:T(1,128)S(1)}, u32[]{:S(2)}, u32[]{:S(2)}) collective-permute-start(f32[1,128]{1,0:T(1,128)S(1)} %get-tuple-element.13), channel_id=1, source_target_pairs={{320,0},{352,32},{384,64},{416,96},{448,128},{480,160},{0,192},{32... | collective-permute-start | bytes 1544 | tf_op jit(solution)/shard_map/ppermute | solution.py:437
  101.7 2.4 %collective-permute-done.5 = f32[1,128]{1,0:T(1,128)S(1)} collective-permute-done((f32[1,128]{1,0:T(1,128)S(1)}, f32[1,128]{1,0:T(1,128)S(1)}, u32[]{:S(2)}, u32[]{:S(2)}) %collective-permute-start.5) | collective-permute-done | bytes 544 | tf_op jit(solution)/shard_map/ppermute | solution.py:437
  104.2 1.9 %collective-permute-start.6 = (f32[3,128]{1,0:T(4,128)S(1)}, f32[3,128]{1,0:T(4,128)S(1)}, u32[]{:S(2)}, u32[]{:S(2)}) collective-permute-start(f32[3,128]{1,0:T(4,128)S(1)} %pad_maximum_fusion.1), channel_id=1, source_target_pairs={{64,0},{96,32},{128,64},{160,96},{192,128},{224,160},{256,192},{28... | collective-permute-start | bytes 4616 | tf_op jit(solution)/shard_map/ppermute | solution.py:437
  106.1 3.4 %collective-permute-start.7 = (f32[3,128]{1,0:T(4,128)S(1)}, f32[3,128]{1,0:T(4,128)S(1)}, u32[]{:S(2)}, u32[]{:S(2)}) collective-permute-start(f32[3,128]{1,0:T(4,128)S(1)} %pad_maximum_fusion.1), channel_id=1, source_target_pairs={{448,0},{480,32},{0,64},{32,96},{64,128},{96,160},{128,192},{160,2... | collective-permute-start | bytes 4616 | tf_op jit(solution)/shard_map/ppermute | solution.py:437
  109.5 2.9 %collective-permute-done.7 = f32[3,128]{1,0:T(4,128)S(1)} collective-permute-done((f32[3,128]{1,0:T(4,128)S(1)}, f32[3,128]{1,0:T(4,128)S(1)}, u32[]{:S(2)}, u32[]{:S(2)}) %collective-permute-start.7) | collective-permute-done | bytes 1568 | tf_op jit(solution)/shard_map/ppermute | solution.py:437
  112.5 5.9 %collective-permute-start.8 = (f32[9,128]{1,0:T(8,128)S(1)}, f32[9,128]{1,0:T(8,128)S(1)}, u32[]{:S(2)}, u32[]{:S(2)}) collective-permute-start(f32[9,128]{1,0:T(8,128)S(1)} %concatenate.12), channel_id=1, source_target_pairs={{0,32},{32,0},{64,96},{96,64},{128,160},{160,128},{192,224},{224,1... | collective-permute-start | bytes 13832 | tf_op jit(solution)/shard_map/ppermute | solution.py:440
  118.5 4.5 %shard_map.113 = (bf16[80,768]{1,0:T(8,128)(2,1)}, bf16[80,768]{1,0:T(8,128)(2,1)}) custom-call(bf16[80,2560]{1,0:T(8,128)(2,1)} %get-tuple-element.9.refs_0_, bf16[80,768]{1,0:T(8,128)(2,1)} %refs_1_.1, bf16[80,768]{1,0:T(8,128)(2,1)} %refs_2_.1, bf16[768,2560]{1,0:T(8,128)(2,1)} %bitcast.21), custom_call_target="tpu_custom_call" | custom-call | tf_op jit(solution)/shard_map/pallas_call | solution.py:405
  (24 shorter events, 2.3 us)
Async XLA Ops:
  0.6 14.5 %copy-start.4 = (bf16[80,768]{1,0:T(8,128)(2,1)S(1)}, bf16[80,768]{1,0:T(8,128)(2,1)}, u32[]{:S(2)}) copy-start(bf16[80,768]{1,0:T(8,128)(2,1)} %refs_1_.1) | copy-start | bytes 368644
  0.6 14.4 %copy-start.3 = (bf16[80,768]{1,0:T(8,128)(2,1)S(1)}, bf16[80,768]{1,0:T(8,128)(2,1)}, u32[]{:S(2)}) copy-start(bf16[80,768]{1,0:T(8,128)(2,1)} %refs_2_.1) | copy-start | bytes 368644
  3.3 45.7 %all-to-all-start = ((bf16[16,328,128]{2,1,0:T(8,128)(2,1)}), bf16[16,328,128]{2,1,0:T(8,128)(2,1)S(1)}, u32[]{:S(2)}, u32[]{:S(2)}) async-start(bf16[16,328,128]{2,1,0:T(8,128)(2,1)} %shard_map.111), calls=%async_computation | async-start | bytes 2686976 | tf_op jit(solution)/shard_map/all_to_all | solution.py:341
  50.6 33.3 %all-to-all-start.1 = ((bf16[8,200,128]{2,1,0:T(8,128)(2,1)}), bf16[8,200,128]{2,1,0:T(8,128)(2,1)S(1)}, u32[]{:S(2)}, u32[]{:S(2)}) async-start(bf16[8,200,128]{2,1,0:T(8,128)(2,1)} %get-tuple-element.12), calls=%async_computation.1 | async-start | bytes 819200 | tf_op jit(solution)/shard_map/all_to_all | solution.py:341
  55.7 9.5 %collective-permute-start = (bf16[80,768]{1,0:T(8,128)(2,1)S(1)}, bf16[80,768]{1,0:T(8,128)(2,1)S(1)}, u32[]{:S(2)}, u32[]{:S(2)}) collective-permute-start(bf16[80,768]{1,0:T(8,128)(2,1)S(1)} %fusion.4), channel_id=1, source_target_pairs={{0,1},{1,0},{2,3},{3,2},{4,5},{5,4},{6,7},{7,6},{8,9},{9,8},{10,11... | collective-permute-start | bytes 368648 | tf_op jit(solution)/shard_map/ppermute | solution.py:373
  65.2 10.6 %collective-permute-start.1 = (bf16[2,80,768]{2,1,0:T(8,128)(2,1)S(1)}, bf16[2,80,768]{2,1,0:T(8,128)(2,1)S(1)}, u32[]{:S(2)}, u32[]{:S(2)}) collective-permute-start(bf16[2,80,768]{2,1,0:T(8,128)(2,1)S(1)} %pad_maximum_fusion.refs_0_), channel_id=1, source_target_pairs={{0,8},{8,16},{16,24},{24,0},{1,9},{9,17},{17,25},{25,1},{2,10},{10... | collective-permute-start | bytes 737288 | tf_op jit(solution)/shard_map/ppermute | solution.py:377
  68.3 13.3 %collective-permute-start.2 = (bf16[2,80,768]{2,1,0:T(8,128)(2,1)S(1)}, bf16[2,80,768]{2,1,0:T(8,128)(2,1)S(1)}, u32[]{:S(2)}, u32[]{:S(2)}) collective-permute-start(bf16[2,80,768]{2,1,0:T(8,128)(2,1)S(1)} %pad_maximum_fusion.refs_0_), channel_id=1, source_target_pairs={{0,16},{8,24},{16,0},{24,8},{1,17},{9,25},{17,1},{25,9},{2,18},{10... | collective-permute-start | bytes 737288 | tf_op jit(solution)/shard_map/ppermute | solution.py:377
  72.6 10.2 %collective-permute-start.3 = (bf16[2,80,768]{2,1,0:T(8,128)(2,1)S(1)}, bf16[2,80,768]{2,1,0:T(8,128)(2,1)S(1)}, u32[]{:S(2)}, u32[]{:S(2)}) collective-permute-start(bf16[2,80,768]{2,1,0:T(8,128)(2,1)S(1)} %pad_maximum_fusion.refs_0_), channel_id=1, source_target_pairs={{0,24},{8,0},{16,8},{24,16},{1,25},{9,1},{17,9},{25,17},{2,26},{10... | collective-permute-start | bytes 737288 | tf_op jit(solution)/shard_map/ppermute | solution.py:377
  83.9 39.3 %copy-start = (s32[128,6]{0,1:T(8,128)S(1)}, s32[128,6]{0,1:T(8,128)}, u32[]{:S(2)}) copy-start(s32[128,6]{0,1:T(8,128)} %param.11) | copy-start | bytes 9220
  83.9 39.3 %copy-start.1 = (s32[128,6]{0,1:T(8,128)S(1)}, s32[128,6]{0,1:T(8,128)}, u32[]{:S(2)}) copy-start(s32[128,6]{0,1:T(8,128)} %param.12) | copy-start | bytes 9220
  83.9 39.3 %copy-start.2 = (s32[128,3]{0,1:T(4,128)S(1)}, s32[128,3]{0,1:T(4,128)}, u32[]{:S(2)}) copy-start(s32[128,3]{0,1:T(4,128)} %param.10) | copy-start | bytes 4612
  85.5 38.7 %all-to-all-start.2 = ((bf16[32,64,128]{2,1,0:T(8,128)(2,1)}), bf16[32,64,128]{2,1,0:T(8,128)(2,1)S(1)}, u32[]{:S(2)}, u32[]{:S(2)}) async-start(bf16[32,64,128]{2,1,0:T(8,128)(2,1)} %shard_map.115), calls=%async_computation.2 | async-start | bytes 1048576 | tf_op jit(solution)/shard_map/all_to_all | solution.py:341
  94.6 7.1 %collective-permute-start.4 = (f32[1,128]{1,0:T(1,128)S(1)}, f32[1,128]{1,0:T(1,128)S(1)}, u32[]{:S(2)}, u32[]{:S(2)}) collective-permute-start(f32[1,128]{1,0:T(1,128)S(1)} %get-tuple-element.13), channel_id=1, source_target_pairs={{192,0},{224,32},{256,64},{288,96},{320,128},{352,160},{384,192},{... | collective-permute-start | bytes 1544 | tf_op jit(solution)/shard_map/ppermute | solution.py:437
  96.6 7.6 %collective-permute-start.5 = (f32[1,128]{1,0:T(1,128)S(1)}, f32[1,128]{1,0:T(1,128)S(1)}, u32[]{:S(2)}, u32[]{:S(2)}) collective-permute-start(f32[1,128]{1,0:T(1,128)S(1)} %get-tuple-element.13), channel_id=1, source_target_pairs={{320,0},{352,32},{384,64},{416,96},{448,128},{480,160},{0,192},{32... | collective-permute-start | bytes 1544 | tf_op jit(solution)/shard_map/ppermute | solution.py:437
  104.2 5.3 %collective-permute-start.6 = (f32[3,128]{1,0:T(4,128)S(1)}, f32[3,128]{1,0:T(4,128)S(1)}, u32[]{:S(2)}, u32[]{:S(2)}) collective-permute-start(f32[3,128]{1,0:T(4,128)S(1)} %pad_maximum_fusion.1), channel_id=1, source_target_pairs={{64,0},{96,32},{128,64},{160,96},{192,128},{224,160},{256,192},{28... | collective-permute-start | bytes 4616 | tf_op jit(solution)/shard_map/ppermute | solution.py:437
  106.1 6.3 %collective-permute-start.7 = (f32[3,128]{1,0:T(4,128)S(1)}, f32[3,128]{1,0:T(4,128)S(1)}, u32[]{:S(2)}, u32[]{:S(2)}) collective-permute-start(f32[3,128]{1,0:T(4,128)S(1)} %pad_maximum_fusion.1), channel_id=1, source_target_pairs={{448,0},{480,32},{0,64},{32,96},{64,128},{96,160},{128,192},{160,2... | collective-permute-start | bytes 4616 | tf_op jit(solution)/shard_map/ppermute | solution.py:437
  112.5 10.4 %collective-permute-start.8 = (f32[9,128]{1,0:T(8,128)S(1)}, f32[9,128]{1,0:T(8,128)S(1)}, u32[]{:S(2)}, u32[]{:S(2)}) collective-permute-start(f32[9,128]{1,0:T(8,128)S(1)} %concatenate.12), channel_id=1, source_target_pairs={{0,32},{32,0},{64,96},{96,64},{128,160},{160,128},{192,224},{224,1... | collective-permute-start | bytes 13832 | tf_op jit(solution)/shard_map/ppermute | solution.py:440

commit v8 on v7

--- a/solution.py
+++ b/solution.py
@@ -13,7 +13,10 @@
 SRC_CAP = 16
 LANES = 128
 DP = ("dp_0", "dp_1", "dp_2")
-NODE_DP = ("node", *DP)
+NODE = ("chip", "core")
+NODE_DP = (*NODE, *DP)
+TO_NODE = ("core", "chip")
+TO_DP = ("dp_1", "dp_2", "dp_0")
 TEAM = ("dp_0", "dp_2")
 HALF = LANES // 2
 PIECES = 3
@@ -46,7 +49,8 @@
     expert, slot, presel = expert_ref[...], slot_ref[...], presel_ref[...]
     slots = columns_of_routes(expert, slot, slot + 1)
     probs = columns_of_routes(expert, slot, prob_ref[...].astype(F32))
-    node_ids = lax.broadcasted_iota(jnp.int32, (n_node, tokens), 0)
+    row = lax.broadcasted_iota(jnp.int32, (n_node, tokens), 0)
+    node_ids = lax.rem(row, n_node // 2) * 2 + row // (n_node // 2)
     slot_to = jnp.zeros((n_node, tokens), F32)
     prob_to = jnp.zeros((n_node, tokens), F32)
     for c in range(PRESEL):
@@ -194,27 +198,25 @@
             )
         )
     scaled = jnp.concatenate(blocks)
-    n = send_ref.shape[0]
-    share = hidden_ref.shape[0] // n
+    some, n_0 = send_ref.shape[:2]
+    share = hidden_ref.shape[0] // (some * n_0)
     third = share // 3
-    some = n // OUT_PIECES
     low = lax.broadcasted_iota(jnp.int32, (some, third, LANES), 2) < HALF
     copies = []
-    for i in range(OUT_PIECES):
-        here = slice(i * some, (i + 1) * some)
+    for i in range(n_0):
         total = jnp.dot(
             hidden_ref[i * some * share : (i + 1) * some * share],
             scaled,
             preferred_element_type=F32,
         ).reshape(some, share, 3 * LANES)
-        send_ref[here, :share] = total[:, :, :LANES].astype(BF16)
-        send_ref[here, share : 2 * share] = total[:, :, LANES : 2 * LANES].astype(BF16)
+        send_ref[:, i, :share] = total[:, :, :LANES].astype(BF16)
+        send_ref[:, i, share : 2 * share] = total[:, :, LANES : 2 * LANES].astype(BF16)
         last = total[:, :, 2 * LANES :]
         swapped = pltpu.roll(last[:, third : 2 * third], HALF, 2)
         mixed = jnp.where(low, last[:, :third], swapped)
-        send_ref[here, 2 * share : 2 * share + third] = mixed.astype(BF16)
-        send_ref[here, 2 * share + third :] = last[:, 2 * third :].astype(BF16)
-        copies.append(pltpu.make_async_copy(send_ref.at[here], out_ref.at[here], left.at[i]))
+        send_ref[:, i, 2 * share : 2 * share + third] = mixed.astype(BF16)
+        send_ref[:, i, 2 * share + third :] = last[:, 2 * third :].astype(BF16)
+        copies.append(pltpu.make_async_copy(send_ref.at[:, i], out_ref.at[:, i], left.at[i]))
         copies[-1].start()
     for copy in copies:
         copy.wait()
@@ -234,7 +236,7 @@
         for j in range(2):
             total = None
             for i in range(n_1):
-                term = terms_ref[(k * n_1 + i) * 2 + j].astype(F32)
+                term = terms_ref[(i * 2 + j) * n_0 + k].astype(F32)
                 total = term if total is None else total + term
             tile = 2 * (2 * k + j)
             put(0, tile, total[:share])
@@ -346,7 +348,8 @@
 ):
     _, features = out_grad.shape
     capacity, units = gate_pre.shape
-    n_node, n_0, n_1, n_2 = (lax.axis_size(a) for a in NODE_DP)
+    chips, cores, n_0, n_1, n_2 = (lax.axis_size(a) for a in NODE_DP)
+    n_node = chips * cores
     team = n_0 * n_2
     group = team * n_1
     share = units // group
@@ -365,7 +368,7 @@
         out_space=HBM,
         vmem_mib=60,
     )(*routed)
-    recv = exchange(send, "node")
+    recv = exchange(send, TO_NODE)
 
     weight = down_weight[0]
     gate_rows = gate_pre.astype(F32)
@@ -411,20 +414,19 @@
         vmem_mib=60,
     )(*sources)
 
-    terms = (group, 2 * share + 2 * share // 3, LANES)
+    terms = (n_1 * n_2, n_0, 2 * share + 2 * share // 3, LANES)
     partial = call(
         partial_kernel,
         pltpu.HBM(terms, BF16),
         [VMEM] * 2,
-        [pltpu.VMEM(terms, BF16), pltpu.SemaphoreType.DMA((OUT_PIECES,))],
+        [pltpu.VMEM(terms, BF16), pltpu.SemaphoreType.DMA((n_0,))],
         out_space=HBM,
     )(team_hidden, parts)
-    terms = exchange(partial, DP)
+    terms = exchange(partial.reshape(group, *terms[2:]), TO_DP)
     grad_down = call(
         functools.partial(sum_kernel, n_0, n_1), shape((share, features), BF16), [VMEM]
     )(terms)[None]
 
-    chips = n_node // 2
     offsets = [0]
     for step in (3, 1):
         rows = [grad_p]
@@ -434,26 +436,26 @@
                 for i in range(chips)
                 for core in range(2)
             ]
-            rows.append(lax.ppermute(grad_p, "node", pairs))
+            rows.append(lax.ppermute(grad_p, NODE, pairs))
         grad_p = jnp.concatenate(rows)
         offsets = offsets + [o + step for o in offsets] + [o - step for o in offsets]
-    other = lax.ppermute(grad_p, "node", [(i, i ^ 1) for i in range(n_node)])
+    other = lax.ppermute(grad_p, NODE, [(i, i ^ 1) for i in range(n_node)])
     grad_p = jnp.concatenate([grad_p, other])
     grad_prob = call(
         functools.partial(return_kernel, offsets, chips),
         shape(route_expert.shape[::-1], F32),
         [SMEM] + [VMEM] * 4,
-    )(lax.axis_index("node")[None], grad_p, presel, expert, slot).T
+    )(lax.axis_index(NODE)[None], grad_p, presel, expert, slot).T
     return (grad_gate, grad_up, grad_down, grad_prob)
 
 
 def solution(mesh):
-    finer = Mesh(mesh.devices.reshape(mesh.shape["node"], 4, 4, 2), NODE_DP)
-    in_specs = (P(NODE_DP, None),) * 7 + (P("node", None, None),)
+    finer = Mesh(mesh.devices.reshape(mesh.shape["node"] // 2, 2, 4, 4, 2), NODE_DP)
+    in_specs = (P(NODE_DP, None),) * 7 + (P(NODE, None, None),)
     out_specs = (
         P(NODE_DP, None),
         P(NODE_DP, None),
-        P("node", DP, None),
+        P(NODE, DP, None),
         P(NODE_DP, None),
     )
     return jax.shard_map(

time: 126 us -> 125 us (level)
  waiting for transfers between devices: 49.5 us -> 48.2 us
    all_to_all x3, waiting for transfers between devices: 30.9 us -> 29.5 us  [exchange(): return lax.all_to_all(value, axes, split_axis=0, concat_axis=0, tiled=True)]
where the time goes in v8:
time: 125 us; the launch traced here: 124 us
  starting transfers between devices  59 us (47%)
  waiting for transfers between devices  48.2 us (39%)
  Pallas kernels  12.9 us (10%)
  matrix products  2.92 us (2%)
    all_to_all x3, waiting for transfers between devices, exchange(): return lax.all_to_all(value, axes, split_axis=0, concat_axis=0, tiled=True)  29.5 us
    all_to_all x3, starting transfers between devices, exchange(): return lax.all_to_all(value, axes, split_axis=0, concat_axis=0, tiled=True)  26.5 us
    ppermute x4, starting transfers between devices, step_of(): rows.append(lax.ppermute(grad_p, NODE, pairs))  12.4 us
    ppermute x3, starting transfers between devices, step_of(): lax.ppermute(hidden_pair, 'dp_0', [(i, (i + k) % n_0) for i in range(n_0)])  10.5 us
    ppermute x3, waiting for transfers between devices, step_of(): lax.ppermute(hidden_pair, 'dp_0', [(i, (i + k) % n_0) for i in range(n_0)])  6.69 us
    ppermute x1, starting transfers between devices, step_of(): other = lax.ppermute(grad_p, NODE, [(i, i ^ 1) for i in range(n_node)])  6.31 us
    ppermute x4, waiting for transfers between devices, step_of(): rows.append(lax.ppermute(grad_p, NODE, pairs))  6.03 us
    ppermute x1, waiting for transfers between devices, step_of(): near = lax.ppermute(hidden, 'dp_2', [(0, 1), (1, 0)])  5.91 us
  transfers between devices with their start and end apart: 12, of which 6 were waited for; matrix products, arithmetic and copies ran while one was open for 3% of the time, Pallas kernels for 5%

profile of v8, /device:TPU:1, one launch (start us, length us, event | category | flops | bytes accessed | tf_op | source)
XLA Modules:
  0.0 124.5 jit_solution(5906571653703529275)
XLA Ops:
  0.7 2.6 %shard_map.111 = bf16[16,328,128]{2,1,0:T(8,128)(2,1)} custom-call(bf16[128,2560]{1,0:T(8,128)(2,1)} %refs_0_.1, bf16[6,128]{1,0:T(8,128)(2,1)} %bitcast.28, s32[3,128]{1,0:T(4,128)} %bitcast.20, s32[6,128]{1,0:T(8,128)} %bitcast.16, s32[6,128]{1,0:T(8,128)} %bitcast.18), custom_call_target="tpu_custom_call" | custom-call | tf_op jit(solution)/shard_map/pallas_call | solution.py:361
  3.3 11.8 %all-to-all-start = ((bf16[16,328,128]{2,1,0:T(8,128)(2,1)}), bf16[16,328,128]{2,1,0:T(8,128)(2,1)S(1)}, u32[]{:S(2)}, u32[]{:S(2)}) async-start(bf16[16,328,128]{2,1,0:T(8,128)(2,1)} %shard_map.111), calls=%async_computation | async-start | bytes 2686976 | tf_op jit(solution)/shard_map/all_to_all | solution.py:343
  15.2 2.9 %fusion.5.slot_out_ref = f32[80,2560]{1,0:T(8,128)S(1)} fusion(bf16[80,768]{1,0:T(8,128)(2,1)S(1)} %fusion.4, bf16[1,768,2560]{2,1,0:T(8,128)(2,1)} %param.15), kind=kOutput, calls=%fused_computation.10 | convolution fusion | flops 314572800 | bytes 4874240 | tf_op jit(solution)/shard_map/dot_general | solution.py:387
  18.1 29.5 %all-to-all-done.recv_ref = bf16[16,328,128]{2,1,0:T(8,128)(2,1)S(1)} async-done(((bf16[16,328,128]{2,1,0:T(8,128)(2,1)}), bf16[16,328,128]{2,1,0:T(8,128)(2,1)S(1)}, u32[]{:S(2)}, u32[]{:S(2)}) %all-to-all-start) | async-done | bytes 1343520 | tf_op jit(solution)/shard_map/all_to_all | solution.py:343
  47.6 1.6 %shard_map.112 = (bf16[80,2560]{1,0:T(8,128)(2,1)}, bf16[8,200,128]{2,1,0:T(8,128)(2,1)}, f32[1,128]{1,0:T(1,128)S(1)}) custom-call(bf16[16,328,128]{2,1,0:T(8,128)(2,1)S(1)} %all-to-all-done.recv_ref, f32[80,2560]{1,0:T(8,128)S(1)} %fusion.5.slot_out_ref), custom_call_target="tpu_custom_call" | custom-call | tf_op jit(solution)/shard_map/pallas_call | solution.py:390
  49.3 5.0 %all-to-all-start.1 = ((bf16[8,200,128]{2,1,0:T(8,128)(2,1)}), bf16[8,200,128]{2,1,0:T(8,128)(2,1)S(1)}, u32[]{:S(2)}, u32[]{:S(2)}) async-start(bf16[8,200,128]{2,1,0:T(8,128)(2,1)} %get-tuple-element.12), calls=%async_computation.1 | async-start | bytes 819200 | tf_op jit(solution)/shard_map/all_to_all | solution.py:343
  54.3 3.4 %collective-permute-start = (bf16[80,768]{1,0:T(8,128)(2,1)S(1)}, bf16[80,768]{1,0:T(8,128)(2,1)S(1)}, u32[]{:S(2)}, u32[]{:S(2)}) collective-permute-start(bf16[80,768]{1,0:T(8,128)(2,1)S(1)} %fusion.4), channel_id=1, source_target_pairs={{0,1},{1,0},{2,3},{3,2},{4,5},{5,4},{6,7},{7,6},{8,9},{9,8},{10,11... | collective-permute-start | bytes 368648 | tf_op jit(solution)/shard_map/ppermute | solution.py:376
  57.7 5.9 %collective-permute-done = bf16[80,768]{1,0:T(8,128)(2,1)S(1)} collective-permute-done((bf16[80,768]{1,0:T(8,128)(2,1)S(1)}, bf16[80,768]{1,0:T(8,128)(2,1)S(1)}, u32[]{:S(2)}, u32[]{:S(2)}) %collective-permute-start) | collective-permute-done | bytes 122912 | tf_op jit(solution)/shard_map/ppermute | solution.py:376
  63.6 3.1 %collective-permute-start.1 = (bf16[2,80,768]{2,1,0:T(8,128)(2,1)S(1)}, bf16[2,80,768]{2,1,0:T(8,128)(2,1)S(1)}, u32[]{:S(2)}, u32[]{:S(2)}) collective-permute-start(bf16[2,80,768]{2,1,0:T(8,128)(2,1)S(1)} %pad_maximum_fusion.refs_0_), channel_id=1, source_target_pairs={{0,8},{8,16},{16,24},{24,0},{1,9},{9,17},{17,25},{25,1},{2,10},{10... | collective-permute-start | bytes 737288 | tf_op jit(solution)/shard_map/ppermute | solution.py:380
  66.7 4.3 %collective-permute-start.2 = (bf16[2,80,768]{2,1,0:T(8,128)(2,1)S(1)}, bf16[2,80,768]{2,1,0:T(8,128)(2,1)S(1)}, u32[]{:S(2)}, u32[]{:S(2)}) collective-permute-start(bf16[2,80,768]{2,1,0:T(8,128)(2,1)S(1)} %pad_maximum_fusion.refs_0_), channel_id=1, source_target_pairs={{0,16},{8,24},{16,0},{24,8},{1,17},{9,25},{17,1},{25,9},{2,18},{10... | collective-permute-start | bytes 737288 | tf_op jit(solution)/shard_map/ppermute | solution.py:380
  71.0 3.1 %collective-permute-start.3 = (bf16[2,80,768]{2,1,0:T(8,128)(2,1)S(1)}, bf16[2,80,768]{2,1,0:T(8,128)(2,1)S(1)}, u32[]{:S(2)}, u32[]{:S(2)}) collective-permute-start(bf16[2,80,768]{2,1,0:T(8,128)(2,1)S(1)} %pad_maximum_fusion.refs_0_), channel_id=1, source_target_pairs={{0,24},{8,0},{16,8},{24,16},{1,25},{9,1},{17,9},{25,17},{2,26},{10... | collective-permute-start | bytes 737288 | tf_op jit(solution)/shard_map/ppermute | solution.py:380
  74.2 5.1 %collective-permute-done.2.refs_2_ = bf16[2,80,768]{2,1,0:T(8,128)(2,1)S(1)} collective-permute-done((bf16[2,80,768]{2,1,0:T(8,128)(2,1)S(1)}, bf16[2,80,768]{2,1,0:T(8,128)(2,1)S(1)}, u32[]{:S(2)}, u32[]{:S(2)}) %collective-permute-start.2) | collective-permute-done | bytes 245792 | tf_op jit(solution)/shard_map/ppermute | solution.py:380
  79.4 1.5 %collective-permute-done.3.refs_3_ = bf16[2,80,768]{2,1,0:T(8,128)(2,1)S(1)} collective-permute-done((bf16[2,80,768]{2,1,0:T(8,128)(2,1)S(1)}, bf16[2,80,768]{2,1,0:T(8,128)(2,1)S(1)}, u32[]{:S(2)}, u32[]{:S(2)}) %collective-permute-start.3) | collective-permute-done | bytes 245792 | tf_op jit(solution)/shard_map/ppermute | solution.py:380
  80.9 1.0 shard_map.114.hidden_ref
  82.0 1.6 %shard_map.115 = bf16[8,4,64,128]{3,2,1,0:T(8,128)(2,1)} custom-call(bf16[768,640]{1,0:T(8,128)(2,1)S(1)} %shard_map.114.hidden_ref, bf16[8,200,128]{2,1,0:T(8,128)(2,1)S(1)} %all-to-all-done.1.parts_ref), custom_call_target="tpu_custom_call" | custom-call | tf_op jit(solution)/shard_map/pallas_call | solution.py:418
  83.5 9.6 %all-to-all-start.2 = ((bf16[32,64,128]{2,1,0:T(8,128)(2,1)}), bf16[32,64,128]{2,1,0:T(8,128)(2,1)S(1)}, u32[]{:S(2)}, u32[]{:S(2)}) async-start(bf16[32,64,128]{2,1,0:T(8,128)(2,1)} %bitcast.23), calls=%async_computation.2 | async-start | bytes 1048576 | tf_op jit(solution)/shard_map/all_to_all | solution.py:343
  93.1 3.6 %collective-permute-start.4 = (f32[1,128]{1,0:T(1,128)S(1)}, f32[1,128]{1,0:T(1,128)S(1)}, u32[]{:S(2)}, u32[]{:S(2)}) collective-permute-start(f32[1,128]{1,0:T(1,128)S(1)} %get-tuple-element.13), channel_id=1, source_target_pairs={{192,0},{224,32},{256,64},{288,96},{320,128},{352,160},{384,192},{... | collective-permute-start | bytes 1544 | tf_op jit(solution)/shard_map/ppermute | solution.py:439
  96.8 3.4 %collective-permute-start.5 = (f32[1,128]{1,0:T(1,128)S(1)}, f32[1,128]{1,0:T(1,128)S(1)}, u32[]{:S(2)}, u32[]{:S(2)}) collective-permute-start(f32[1,128]{1,0:T(1,128)S(1)} %get-tuple-element.13), channel_id=1, source_target_pairs={{320,0},{352,32},{384,64},{416,96},{448,128},{480,160},{0,192},{32... | collective-permute-start | bytes 1544 | tf_op jit(solution)/shard_map/ppermute | solution.py:439
  100.2 3.9 %collective-permute-done.5 = f32[1,128]{1,0:T(1,128)S(1)} collective-permute-done((f32[1,128]{1,0:T(1,128)S(1)}, f32[1,128]{1,0:T(1,128)S(1)}, u32[]{:S(2)}, u32[]{:S(2)}) %collective-permute-start.5) | collective-permute-done | bytes 544 | tf_op jit(solution)/shard_map/ppermute | solution.py:439
  104.1 1.9 %collective-permute-start.6 = (f32[3,128]{1,0:T(4,128)S(1)}, f32[3,128]{1,0:T(4,128)S(1)}, u32[]{:S(2)}, u32[]{:S(2)}) collective-permute-start(f32[3,128]{1,0:T(4,128)S(1)} %pad_maximum_fusion.1), channel_id=1, source_target_pairs={{64,0},{96,32},{128,64},{160,96},{192,128},{224,160},{256,192},{28... | collective-permute-start | bytes 4616 | tf_op jit(solution)/shard_map/ppermute | solution.py:439
  106.0 3.4 %collective-permute-start.7 = (f32[3,128]{1,0:T(4,128)S(1)}, f32[3,128]{1,0:T(4,128)S(1)}, u32[]{:S(2)}, u32[]{:S(2)}) collective-permute-start(f32[3,128]{1,0:T(4,128)S(1)} %pad_maximum_fusion.1), channel_id=1, source_target_pairs={{448,0},{480,32},{0,64},{32,96},{64,128},{96,160},{128,192},{160,2... | collective-permute-start | bytes 4616 | tf_op jit(solution)/shard_map/ppermute | solution.py:439
  109.4 2.2 %collective-permute-done.7 = f32[3,128]{1,0:T(4,128)S(1)} collective-permute-done((f32[3,128]{1,0:T(4,128)S(1)}, f32[3,128]{1,0:T(4,128)S(1)}, u32[]{:S(2)}, u32[]{:S(2)}) %collective-permute-start.7) | collective-permute-done | bytes 1568 | tf_op jit(solution)/shard_map/ppermute | solution.py:439
  111.7 6.3 %collective-permute-start.8 = (f32[9,128]{1,0:T(8,128)S(1)}, f32[9,128]{1,0:T(8,128)S(1)}, u32[]{:S(2)}, u32[]{:S(2)}) collective-permute-start(f32[9,128]{1,0:T(8,128)S(1)} %concatenate.12), channel_id=1, source_target_pairs={{0,32},{32,0},{64,96},{96,64},{128,160},{160,128},{192,224},{224,1... | collective-permute-start | bytes 13832 | tf_op jit(solution)/shard_map/ppermute | solution.py:442
  118.0 4.5 %shard_map.113 = (bf16[80,768]{1,0:T(8,128)(2,1)}, bf16[80,768]{1,0:T(8,128)(2,1)}) custom-call(bf16[80,2560]{1,0:T(8,128)(2,1)} %get-tuple-element.9.refs_0_, bf16[80,768]{1,0:T(8,128)(2,1)} %refs_1_.1, bf16[80,768]{1,0:T(8,128)(2,1)} %refs_2_.1, bf16[768,2560]{1,0:T(8,128)(2,1)} %bitcast.22), custom_call_target="tpu_custom_call" | custom-call | tf_op jit(solution)/shard_map/pallas_call | solution.py:408
  (24 shorter events, 2.3 us)
Async XLA Ops:
  0.6 14.5 %copy-start.4 = (bf16[80,768]{1,0:T(8,128)(2,1)S(1)}, bf16[80,768]{1,0:T(8,128)(2,1)}, u32[]{:S(2)}) copy-start(bf16[80,768]{1,0:T(8,128)(2,1)} %refs_1_.1) | copy-start | bytes 368644
  0.6 14.4 %copy-start.3 = (bf16[80,768]{1,0:T(8,128)(2,1)S(1)}, bf16[80,768]{1,0:T(8,128)(2,1)}, u32[]{:S(2)}) copy-start(bf16[80,768]{1,0:T(8,128)(2,1)} %refs_2_.1) | copy-start | bytes 368644
  3.3 44.4 %all-to-all-start = ((bf16[16,328,128]{2,1,0:T(8,128)(2,1)}), bf16[16,328,128]{2,1,0:T(8,128)(2,1)S(1)}, u32[]{:S(2)}, u32[]{:S(2)}) async-start(bf16[16,328,128]{2,1,0:T(8,128)(2,1)} %shard_map.111), calls=%async_computation | async-start | bytes 2686976 | tf_op jit(solution)/shard_map/all_to_all | solution.py:343
  49.3 32.7 %all-to-all-start.1 = ((bf16[8,200,128]{2,1,0:T(8,128)(2,1)}), bf16[8,200,128]{2,1,0:T(8,128)(2,1)S(1)}, u32[]{:S(2)}, u32[]{:S(2)}) async-start(bf16[8,200,128]{2,1,0:T(8,128)(2,1)} %get-tuple-element.12), calls=%async_computation.1 | async-start | bytes 819200 | tf_op jit(solution)/shard_map/all_to_all | solution.py:343
  54.3 9.3 %collective-permute-start = (bf16[80,768]{1,0:T(8,128)(2,1)S(1)}, bf16[80,768]{1,0:T(8,128)(2,1)S(1)}, u32[]{:S(2)}, u32[]{:S(2)}) collective-permute-start(bf16[80,768]{1,0:T(8,128)(2,1)S(1)} %fusion.4), channel_id=1, source_target_pairs={{0,1},{1,0},{2,3},{3,2},{4,5},{5,4},{6,7},{7,6},{8,9},{9,8},{10,11... | collective-permute-start | bytes 368648 | tf_op jit(solution)/shard_map/ppermute | solution.py:376
  63.6 10.6 %collective-permute-start.1 = (bf16[2,80,768]{2,1,0:T(8,128)(2,1)S(1)}, bf16[2,80,768]{2,1,0:T(8,128)(2,1)S(1)}, u32[]{:S(2)}, u32[]{:S(2)}) collective-permute-start(bf16[2,80,768]{2,1,0:T(8,128)(2,1)S(1)} %pad_maximum_fusion.refs_0_), channel_id=1, source_target_pairs={{0,8},{8,16},{16,24},{24,0},{1,9},{9,17},{17,25},{25,1},{2,10},{10... | collective-permute-start | bytes 737288 | tf_op jit(solution)/shard_map/ppermute | solution.py:380
  66.7 12.6 %collective-permute-start.2 = (bf16[2,80,768]{2,1,0:T(8,128)(2,1)S(1)}, bf16[2,80,768]{2,1,0:T(8,128)(2,1)S(1)}, u32[]{:S(2)}, u32[]{:S(2)}) collective-permute-start(bf16[2,80,768]{2,1,0:T(8,128)(2,1)S(1)} %pad_maximum_fusion.refs_0_), channel_id=1, source_target_pairs={{0,16},{8,24},{16,0},{24,8},{1,17},{9,25},{17,1},{25,9},{2,18},{10... | collective-permute-start | bytes 737288 | tf_op jit(solution)/shard_map/ppermute | solution.py:380
  71.0 9.9 %collective-permute-start.3 = (bf16[2,80,768]{2,1,0:T(8,128)(2,1)S(1)}, bf16[2,80,768]{2,1,0:T(8,128)(2,1)S(1)}, u32[]{:S(2)}, u32[]{:S(2)}) collective-permute-start(bf16[2,80,768]{2,1,0:T(8,128)(2,1)S(1)} %pad_maximum_fusion.refs_0_), channel_id=1, source_target_pairs={{0,24},{8,0},{16,8},{24,16},{1,25},{9,1},{17,9},{25,17},{2,26},{10... | collective-permute-start | bytes 737288 | tf_op jit(solution)/shard_map/ppermute | solution.py:380
  81.9 40.8 %copy-start = (s32[128,6]{0,1:T(8,128)S(1)}, s32[128,6]{0,1:T(8,128)}, u32[]{:S(2)}) copy-start(s32[128,6]{0,1:T(8,128)} %param.11) | copy-start | bytes 9220
  81.9 40.8 %copy-start.1 = (s32[128,6]{0,1:T(8,128)S(1)}, s32[128,6]{0,1:T(8,128)}, u32[]{:S(2)}) copy-start(s32[128,6]{0,1:T(8,128)} %param.12) | copy-start | bytes 9220
  81.9 40.8 %copy-start.2 = (s32[128,3]{0,1:T(4,128)S(1)}, s32[128,3]{0,1:T(4,128)}, u32[]{:S(2)}) copy-start(s32[128,3]{0,1:T(4,128)} %param.10) | copy-start | bytes 4612
  83.5 40.2 %all-to-all-start.2 = ((bf16[32,64,128]{2,1,0:T(8,128)(2,1)}), bf16[32,64,128]{2,1,0:T(8,128)(2,1)S(1)}, u32[]{:S(2)}, u32[]{:S(2)}) async-start(bf16[32,64,128]{2,1,0:T(8,128)(2,1)} %bitcast.23), calls=%async_computation.2 | async-start | bytes 1048576 | tf_op jit(solution)/shard_map/all_to_all | solution.py:343
  93.1 7.1 %collective-permute-start.4 = (f32[1,128]{1,0:T(1,128)S(1)}, f32[1,128]{1,0:T(1,128)S(1)}, u32[]{:S(2)}, u32[]{:S(2)}) collective-permute-start(f32[1,128]{1,0:T(1,128)S(1)} %get-tuple-element.13), channel_id=1, source_target_pairs={{192,0},{224,32},{256,64},{288,96},{320,128},{352,160},{384,192},{... | collective-permute-start | bytes 1544 | tf_op jit(solution)/shard_map/ppermute | solution.py:439
  96.8 7.3 %collective-permute-start.5 = (f32[1,128]{1,0:T(1,128)S(1)}, f32[1,128]{1,0:T(1,128)S(1)}, u32[]{:S(2)}, u32[]{:S(2)}) collective-permute-start(f32[1,128]{1,0:T(1,128)S(1)} %get-tuple-element.13), channel_id=1, source_target_pairs={{320,0},{352,32},{384,64},{416,96},{448,128},{480,160},{0,192},{32... | collective-permute-start | bytes 1544 | tf_op jit(solution)/shard_map/ppermute | solution.py:439
  104.1 5.3 %collective-permute-start.6 = (f32[3,128]{1,0:T(4,128)S(1)}, f32[3,128]{1,0:T(4,128)S(1)}, u32[]{:S(2)}, u32[]{:S(2)}) collective-permute-start(f32[3,128]{1,0:T(4,128)S(1)} %pad_maximum_fusion.1), channel_id=1, source_target_pairs={{64,0},{96,32},{128,64},{160,96},{192,128},{224,160},{256,192},{28... | collective-permute-start | bytes 4616 | tf_op jit(solution)/shard_map/ppermute | solution.py:439
  106.0 5.5 %collective-permute-start.7 = (f32[3,128]{1,0:T(4,128)S(1)}, f32[3,128]{1,0:T(4,128)S(1)}, u32[]{:S(2)}, u32[]{:S(2)}) collective-permute-start(f32[3,128]{1,0:T(4,128)S(1)} %pad_maximum_fusion.1), channel_id=1, source_target_pairs={{448,0},{480,32},{0,64},{32,96},{64,128},{96,160},{128,192},{160,2... | collective-permute-start | bytes 4616 | tf_op jit(solution)/shard_map/ppermute | solution.py:439
  111.7 10.8 %collective-permute-start.8 = (f32[9,128]{1,0:T(8,128)S(1)}, f32[9,128]{1,0:T(8,128)S(1)}, u32[]{:S(2)}, u32[]{:S(2)}) collective-permute-start(f32[9,128]{1,0:T(8,128)S(1)} %concatenate.12), channel_id=1, source_target_pairs={{0,32},{32,0},{64,96},{96,64},{128,160},{160,128},{192,224},{224,1... | collective-permute-start | bytes 13832 | tf_op jit(solution)/shard_map/ppermute | solution.py:442

commit v9 on v8

--- a/solution.py
+++ b/solution.py
@@ -20,7 +20,7 @@
 TEAM = ("dp_0", "dp_2")
 HALF = LANES // 2
 PIECES = 3
-OUT_PIECES = 4
+OUT_PIECES = 2
 F32 = jnp.float32
 BF16 = jnp.bfloat16
 
@@ -160,7 +160,7 @@
             own, term = settle(both[:, j * LANES : (j + 1) * LANES], 2 * k + j)
             sums += term
             parts_ref[k, j * capacity : (j + 1) * capacity] = own.astype(BF16)
-        copies.append(pltpu.make_async_copy(parts_ref.at[k], out_ref.at[k], left.at[k]))
+        copies.append(pltpu.make_async_copy(parts_ref.at[k], out_ref.at[k % 2 * (n // 2) + k // 2], left.at[k]))
         copies[-1].start()
     copies.append(pltpu.make_async_copy(scaled_ref, scaled_out_ref, left.at[n]))
     copies[-1].start()
@@ -188,7 +188,7 @@
     team, rows, _ = parts_ref.shape
     capacity = rows * 2 // 5
     blocks = []
-    for block in range(team):
+    for block in [k % 2 * (team // 2) + k // 2 for k in range(team)]:
         packed = parts_ref[block, 2 * capacity :].astype(F32)
         halves = jnp.concatenate([packed, pltpu.roll(packed, HALF, 1)]).astype(BF16)
         blocks.append(
@@ -203,21 +203,28 @@
     third = share // 3
     low = lax.broadcasted_iota(jnp.int32, (some, third, LANES), 2) < HALF
     copies = []
-    for i in range(n_0):
+    step = n_0 // 2
+    for i in range(0, n_0, step):
         total = jnp.dot(
-            hidden_ref[i * some * share : (i + 1) * some * share],
+            hidden_ref[i * some * share : (i + step) * some * share],
             scaled,
             preferred_element_type=F32,
-        ).reshape(some, share, 3 * LANES)
-        send_ref[:, i, :share] = total[:, :, :LANES].astype(BF16)
-        send_ref[:, i, share : 2 * share] = total[:, :, LANES : 2 * LANES].astype(BF16)
-        last = total[:, :, 2 * LANES :]
-        swapped = pltpu.roll(last[:, third : 2 * third], HALF, 2)
-        mixed = jnp.where(low, last[:, :third], swapped)
-        send_ref[:, i, 2 * share : 2 * share + third] = mixed.astype(BF16)
-        send_ref[:, i, 2 * share + third :] = last[:, 2 * third :].astype(BF16)
-        copies.append(pltpu.make_async_copy(send_ref.at[:, i], out_ref.at[:, i], left.at[i]))
-        copies[-1].start()
+        ).reshape(step, some, share, 3 * LANES)
+        for k in range(step):
+            each = total[k]
+            send_ref[:, i + k, :share] = each[:, :, :LANES].astype(BF16)
+            send_ref[:, i + k, share : 2 * share] = each[:, :, LANES : 2 * LANES].astype(BF16)
+            last = each[:, :, 2 * LANES :]
+            swapped = pltpu.roll(last[:, third : 2 * third], HALF, 2)
+            mixed = jnp.where(low, last[:, :third], swapped)
+            send_ref[:, i + k, 2 * share : 2 * share + third] = mixed.astype(BF16)
+            send_ref[:, i + k, 2 * share + third :] = last[:, 2 * third :].astype(BF16)
+            copies.append(
+                pltpu.make_async_copy(
+                    send_ref.at[:, i + k], out_ref.at[:, i + k], left.at[i + k]
+                )
+            )
+            copies[-1].start()
     for copy in copies:
         copy.wait()
 
@@ -402,7 +409,7 @@
         ],
         out_space=[HBM, HBM, VMEM],
     )(recv, slot_out)
-    parts = exchange(parts, TEAM)
+    parts = exchange(parts, TEAM[::-1])
 
     sources = (scaled, gate_pre, up_pre, weight)
     grad_gate, grad_up = call(

time: 125 us -> 125 us (level)
  no operation moved by 1% of the time
where the time goes in v9:
time: 125 us; the launch traced here: 124 us
  starting transfers between devices  58.9 us (47%)
  waiting for transfers between devices  48.2 us (39%)
  Pallas kernels  13 us (10%)
  matrix products  2.92 us (2%)
    all_to_all x3, waiting for transfers between devices, exchange(): return lax.all_to_all(value, axes, split_axis=0, concat_axis=0, tiled=True)  29.5 us
    all_to_all x3, starting transfers between devices, exchange(): return lax.all_to_all(value, axes, split_axis=0, concat_axis=0, tiled=True)  26.4 us
    ppermute x4, starting transfers between devices, step_of(): rows.append(lax.ppermute(grad_p, NODE, pairs))  12.4 us
    ppermute x3, starting transfers between devices, step_of(): lax.ppermute(hidden_pair, 'dp_0', [(i, (i + k) % n_0) for i in range(n_0)])  10.5 us
    ppermute x3, waiting for transfers between devices, step_of(): lax.ppermute(hidden_pair, 'dp_0', [(i, (i + k) % n_0) for i in range(n_0)])  6.74 us
    ppermute x1, starting transfers between devices, step_of(): other = lax.ppermute(grad_p, NODE, [(i, i ^ 1) for i in range(n_node)])  6.31 us
    ppermute x4, waiting for transfers between devices, step_of(): rows.append(lax.ppermute(grad_p, NODE, pairs))  6.03 us
    ppermute x1, waiting for transfers between devices, step_of(): near = lax.ppermute(hidden, 'dp_2', [(0, 1), (1, 0)])  5.91 us
  transfers between devices with their start and end apart: 12, of which 6 were waited for; matrix products, arithmetic and copies ran while one was open for 3% of the time, Pallas kernels for 5%

profile of v9, /device:TPU:1, one launch (start us, length us, event | category | flops | bytes accessed | tf_op | source)
XLA Modules:
  0.0 124.5 jit_solution(15446289569555717819)
XLA Ops:
  0.7 2.7 %shard_map.111 = bf16[16,328,128]{2,1,0:T(8,128)(2,1)} custom-call(bf16[128,2560]{1,0:T(8,128)(2,1)} %refs_0_.1, bf16[6,128]{1,0:T(8,128)(2,1)} %bitcast.28, s32[3,128]{1,0:T(4,128)} %bitcast.20, s32[6,128]{1,0:T(8,128)} %bitcast.16, s32[6,128]{1,0:T(8,128)} %bitcast.18), custom_call_target="tpu_custom_call" | custom-call | tf_op jit(solution)/shard_map/pallas_call | solution.py:368
  3.3 11.8 %all-to-all-start = ((bf16[16,328,128]{2,1,0:T(8,128)(2,1)}), bf16[16,328,128]{2,1,0:T(8,128)(2,1)S(1)}, u32[]{:S(2)}, u32[]{:S(2)}) async-start(bf16[16,328,128]{2,1,0:T(8,128)(2,1)} %shard_map.111), calls=%async_computation | async-start | bytes 2686976 | tf_op jit(solution)/shard_map/all_to_all | solution.py:350
  15.3 2.9 %fusion.5.slot_out_ref = f32[80,2560]{1,0:T(8,128)S(1)} fusion(bf16[80,768]{1,0:T(8,128)(2,1)S(1)} %fusion.4, bf16[1,768,2560]{2,1,0:T(8,128)(2,1)} %param.15), kind=kOutput, calls=%fused_computation.10 | convolution fusion | flops 314572800 | bytes 4874240 | tf_op jit(solution)/shard_map/dot_general | solution.py:394
  18.2 29.5 %all-to-all-done.recv_ref = bf16[16,328,128]{2,1,0:T(8,128)(2,1)S(1)} async-done(((bf16[16,328,128]{2,1,0:T(8,128)(2,1)}), bf16[16,328,128]{2,1,0:T(8,128)(2,1)S(1)}, u32[]{:S(2)}, u32[]{:S(2)}) %all-to-all-start) | async-done | bytes 1343520 | tf_op jit(solution)/shard_map/all_to_all | solution.py:350
  47.7 1.6 %shard_map.112 = (bf16[80,2560]{1,0:T(8,128)(2,1)}, bf16[8,200,128]{2,1,0:T(8,128)(2,1)}, f32[1,128]{1,0:T(1,128)S(1)}) custom-call(bf16[16,328,128]{2,1,0:T(8,128)(2,1)S(1)} %all-to-all-done.recv_ref, f32[80,2560]{1,0:T(8,128)S(1)} %fusion.5.slot_out_ref), custom_call_target="tpu_custom_call" | custom-call | tf_op jit(solution)/shard_map/pallas_call | solution.py:397
  49.3 5.0 %all-to-all-start.1 = ((bf16[8,200,128]{2,1,0:T(8,128)(2,1)}), bf16[8,200,128]{2,1,0:T(8,128)(2,1)S(1)}, u32[]{:S(2)}, u32[]{:S(2)}) async-start(bf16[8,200,128]{2,1,0:T(8,128)(2,1)} %get-tuple-element.12), calls=%async_computation.1 | async-start | bytes 819200 | tf_op jit(solution)/shard_map/all_to_all | solution.py:350
  54.4 3.4 %collective-permute-start = (bf16[80,768]{1,0:T(8,128)(2,1)S(1)}, bf16[80,768]{1,0:T(8,128)(2,1)S(1)}, u32[]{:S(2)}, u32[]{:S(2)}) collective-permute-start(bf16[80,768]{1,0:T(8,128)(2,1)S(1)} %fusion.4), channel_id=1, source_target_pairs={{0,1},{1,0},{2,3},{3,2},{4,5},{5,4},{6,7},{7,6},{8,9},{9,8},{10,11... | collective-permute-start | bytes 368648 | tf_op jit(solution)/shard_map/ppermute | solution.py:383
  57.8 5.9 %collective-permute-done = bf16[80,768]{1,0:T(8,128)(2,1)S(1)} collective-permute-done((bf16[80,768]{1,0:T(8,128)(2,1)S(1)}, bf16[80,768]{1,0:T(8,128)(2,1)S(1)}, u32[]{:S(2)}, u32[]{:S(2)}) %collective-permute-start) | collective-permute-done | bytes 122912 | tf_op jit(solution)/shard_map/ppermute | solution.py:383
  63.7 3.1 %collective-permute-start.1 = (bf16[2,80,768]{2,1,0:T(8,128)(2,1)S(1)}, bf16[2,80,768]{2,1,0:T(8,128)(2,1)S(1)}, u32[]{:S(2)}, u32[]{:S(2)}) collective-permute-start(bf16[2,80,768]{2,1,0:T(8,128)(2,1)S(1)} %pad_maximum_fusion.refs_0_), channel_id=1, source_target_pairs={{0,8},{8,16},{16,24},{24,0},{1,9},{9,17},{17,25},{25,1},{2,10},{10... | collective-permute-start | bytes 737288 | tf_op jit(solution)/shard_map/ppermute | solution.py:387
  66.8 4.3 %collective-permute-start.2 = (bf16[2,80,768]{2,1,0:T(8,128)(2,1)S(1)}, bf16[2,80,768]{2,1,0:T(8,128)(2,1)S(1)}, u32[]{:S(2)}, u32[]{:S(2)}) collective-permute-start(bf16[2,80,768]{2,1,0:T(8,128)(2,1)S(1)} %pad_maximum_fusion.refs_0_), channel_id=1, source_target_pairs={{0,16},{8,24},{16,0},{24,8},{1,17},{9,25},{17,1},{25,9},{2,18},{10... | collective-permute-start | bytes 737288 | tf_op jit(solution)/shard_map/ppermute | solution.py:387
  71.2 3.0 %collective-permute-start.3 = (bf16[2,80,768]{2,1,0:T(8,128)(2,1)S(1)}, bf16[2,80,768]{2,1,0:T(8,128)(2,1)S(1)}, u32[]{:S(2)}, u32[]{:S(2)}) collective-permute-start(bf16[2,80,768]{2,1,0:T(8,128)(2,1)S(1)} %pad_maximum_fusion.refs_0_), channel_id=1, source_target_pairs={{0,24},{8,0},{16,8},{24,16},{1,25},{9,1},{17,9},{25,17},{2,26},{10... | collective-permute-start | bytes 737288 | tf_op jit(solution)/shard_map/ppermute | solution.py:387
  74.3 5.2 %collective-permute-done.2.refs_2_ = bf16[2,80,768]{2,1,0:T(8,128)(2,1)S(1)} collective-permute-done((bf16[2,80,768]{2,1,0:T(8,128)(2,1)S(1)}, bf16[2,80,768]{2,1,0:T(8,128)(2,1)S(1)}, u32[]{:S(2)}, u32[]{:S(2)}) %collective-permute-start.2) | collective-permute-done | bytes 245792 | tf_op jit(solution)/shard_map/ppermute | solution.py:387
  79.5 1.5 %collective-permute-done.3.refs_3_ = bf16[2,80,768]{2,1,0:T(8,128)(2,1)S(1)} collective-permute-done((bf16[2,80,768]{2,1,0:T(8,128)(2,1)S(1)}, bf16[2,80,768]{2,1,0:T(8,128)(2,1)S(1)}, u32[]{:S(2)}, u32[]{:S(2)}) %collective-permute-start.3) | collective-permute-done | bytes 245792 | tf_op jit(solution)/shard_map/ppermute | solution.py:387
  81.0 1.0 shard_map.114.hidden_ref
  82.1 1.5 %shard_map.115 = bf16[8,4,64,128]{3,2,1,0:T(8,128)(2,1)} custom-call(bf16[768,640]{1,0:T(8,128)(2,1)S(1)} %shard_map.114.hidden_ref, bf16[8,200,128]{2,1,0:T(8,128)(2,1)S(1)} %all-to-all-done.1.parts_ref), custom_call_target="tpu_custom_call" | custom-call | tf_op jit(solution)/shard_map/pallas_call | solution.py:425
  83.6 9.5 %all-to-all-start.2 = ((bf16[32,64,128]{2,1,0:T(8,128)(2,1)}), bf16[32,64,128]{2,1,0:T(8,128)(2,1)S(1)}, u32[]{:S(2)}, u32[]{:S(2)}) async-start(bf16[32,64,128]{2,1,0:T(8,128)(2,1)} %bitcast.23), calls=%async_computation.2 | async-start | bytes 1048576 | tf_op jit(solution)/shard_map/all_to_all | solution.py:350
  93.2 3.6 %collective-permute-start.4 = (f32[1,128]{1,0:T(1,128)S(1)}, f32[1,128]{1,0:T(1,128)S(1)}, u32[]{:S(2)}, u32[]{:S(2)}) collective-permute-start(f32[1,128]{1,0:T(1,128)S(1)} %get-tuple-element.13), channel_id=1, source_target_pairs={{192,0},{224,32},{256,64},{288,96},{320,128},{352,160},{384,192},{... | collective-permute-start | bytes 1544 | tf_op jit(solution)/shard_map/ppermute | solution.py:446
  96.8 3.4 %collective-permute-start.5 = (f32[1,128]{1,0:T(1,128)S(1)}, f32[1,128]{1,0:T(1,128)S(1)}, u32[]{:S(2)}, u32[]{:S(2)}) collective-permute-start(f32[1,128]{1,0:T(1,128)S(1)} %get-tuple-element.13), channel_id=1, source_target_pairs={{320,0},{352,32},{384,64},{416,96},{448,128},{480,160},{0,192},{32... | collective-permute-start | bytes 1544 | tf_op jit(solution)/shard_map/ppermute | solution.py:446
  100.3 3.9 %collective-permute-done.5 = f32[1,128]{1,0:T(1,128)S(1)} collective-permute-done((f32[1,128]{1,0:T(1,128)S(1)}, f32[1,128]{1,0:T(1,128)S(1)}, u32[]{:S(2)}, u32[]{:S(2)}) %collective-permute-start.5) | collective-permute-done | bytes 544 | tf_op jit(solution)/shard_map/ppermute | solution.py:446
  104.1 1.9 %collective-permute-start.6 = (f32[3,128]{1,0:T(4,128)S(1)}, f32[3,128]{1,0:T(4,128)S(1)}, u32[]{:S(2)}, u32[]{:S(2)}) collective-permute-start(f32[3,128]{1,0:T(4,128)S(1)} %pad_maximum_fusion.1), channel_id=1, source_target_pairs={{64,0},{96,32},{128,64},{160,96},{192,128},{224,160},{256,192},{28... | collective-permute-start | bytes 4616 | tf_op jit(solution)/shard_map/ppermute | solution.py:446
  106.1 3.4 %collective-permute-start.7 = (f32[3,128]{1,0:T(4,128)S(1)}, f32[3,128]{1,0:T(4,128)S(1)}, u32[]{:S(2)}, u32[]{:S(2)}) collective-permute-start(f32[3,128]{1,0:T(4,128)S(1)} %pad_maximum_fusion.1), channel_id=1, source_target_pairs={{448,0},{480,32},{0,64},{32,96},{64,128},{96,160},{128,192},{160,2... | collective-permute-start | bytes 4616 | tf_op jit(solution)/shard_map/ppermute | solution.py:446
  109.4 2.2 %collective-permute-done.7 = f32[3,128]{1,0:T(4,128)S(1)} collective-permute-done((f32[3,128]{1,0:T(4,128)S(1)}, f32[3,128]{1,0:T(4,128)S(1)}, u32[]{:S(2)}, u32[]{:S(2)}) %collective-permute-start.7) | collective-permute-done | bytes 1568 | tf_op jit(solution)/shard_map/ppermute | solution.py:446
  111.7 6.3 %collective-permute-start.8 = (f32[9,128]{1,0:T(8,128)S(1)}, f32[9,128]{1,0:T(8,128)S(1)}, u32[]{:S(2)}, u32[]{:S(2)}) collective-permute-start(f32[9,128]{1,0:T(8,128)S(1)} %concatenate.12), channel_id=1, source_target_pairs={{0,32},{32,0},{64,96},{96,64},{128,160},{160,128},{192,224},{224,1... | collective-permute-start | bytes 13832 | tf_op jit(solution)/shard_map/ppermute | solution.py:449
  118.0 4.5 %shard_map.113 = (bf16[80,768]{1,0:T(8,128)(2,1)}, bf16[80,768]{1,0:T(8,128)(2,1)}) custom-call(bf16[80,2560]{1,0:T(8,128)(2,1)} %get-tuple-element.9.refs_0_, bf16[80,768]{1,0:T(8,128)(2,1)} %refs_1_.1, bf16[80,768]{1,0:T(8,128)(2,1)} %refs_2_.1, bf16[768,2560]{1,0:T(8,128)(2,1)} %bitcast.22), custom_call_target="tpu_custom_call" | custom-call | tf_op jit(solution)/shard_map/pallas_call | solution.py:415
  (24 shorter events, 2.3 us)
Async XLA Ops:
  0.6 14.5 %copy-start.4 = (bf16[80,768]{1,0:T(8,128)(2,1)S(1)}, bf16[80,768]{1,0:T(8,128)(2,1)}, u32[]{:S(2)}) copy-start(bf16[80,768]{1,0:T(8,128)(2,1)} %refs_1_.1) | copy-start | bytes 368644
  0.6 14.5 %copy-start.3 = (bf16[80,768]{1,0:T(8,128)(2,1)S(1)}, bf16[80,768]{1,0:T(8,128)(2,1)}, u32[]{:S(2)}) copy-start(bf16[80,768]{1,0:T(8,128)(2,1)} %refs_2_.1) | copy-start | bytes 368644
  3.3 44.4 %all-to-all-start = ((bf16[16,328,128]{2,1,0:T(8,128)(2,1)}), bf16[16,328,128]{2,1,0:T(8,128)(2,1)S(1)}, u32[]{:S(2)}, u32[]{:S(2)}) async-start(bf16[16,328,128]{2,1,0:T(8,128)(2,1)} %shard_map.111), calls=%async_computation | async-start | bytes 2686976 | tf_op jit(solution)/shard_map/all_to_all | solution.py:350
  49.3 32.7 %all-to-all-start.1 = ((bf16[8,200,128]{2,1,0:T(8,128)(2,1)}), bf16[8,200,128]{2,1,0:T(8,128)(2,1)S(1)}, u32[]{:S(2)}, u32[]{:S(2)}) async-start(bf16[8,200,128]{2,1,0:T(8,128)(2,1)} %get-tuple-element.12), calls=%async_computation.1 | async-start | bytes 819200 | tf_op jit(solution)/shard_map/all_to_all | solution.py:350
  54.4 9.3 %collective-permute-start = (bf16[80,768]{1,0:T(8,128)(2,1)S(1)}, bf16[80,768]{1,0:T(8,128)(2,1)S(1)}, u32[]{:S(2)}, u32[]{:S(2)}) collective-permute-start(bf16[80,768]{1,0:T(8,128)(2,1)S(1)} %fusion.4), channel_id=1, source_target_pairs={{0,1},{1,0},{2,3},{3,2},{4,5},{5,4},{6,7},{7,6},{8,9},{9,8},{10,11... | collective-permute-start | bytes 368648 | tf_op jit(solution)/shard_map/ppermute | solution.py:383
  63.7 10.6 %collective-permute-start.1 = (bf16[2,80,768]{2,1,0:T(8,128)(2,1)S(1)}, bf16[2,80,768]{2,1,0:T(8,128)(2,1)S(1)}, u32[]{:S(2)}, u32[]{:S(2)}) collective-permute-start(bf16[2,80,768]{2,1,0:T(8,128)(2,1)S(1)} %pad_maximum_fusion.refs_0_), channel_id=1, source_target_pairs={{0,8},{8,16},{16,24},{24,0},{1,9},{9,17},{17,25},{25,1},{2,10},{10... | collective-permute-start | bytes 737288 | tf_op jit(solution)/shard_map/ppermute | solution.py:387
  66.8 12.6 %collective-permute-start.2 = (bf16[2,80,768]{2,1,0:T(8,128)(2,1)S(1)}, bf16[2,80,768]{2,1,0:T(8,128)(2,1)S(1)}, u32[]{:S(2)}, u32[]{:S(2)}) collective-permute-start(bf16[2,80,768]{2,1,0:T(8,128)(2,1)S(1)} %pad_maximum_fusion.refs_0_), channel_id=1, source_target_pairs={{0,16},{8,24},{16,0},{24,8},{1,17},{9,25},{17,1},{25,9},{2,18},{10... | collective-permute-start | bytes 737288 | tf_op jit(solution)/shard_map/ppermute | solution.py:387
  71.2 9.9 %collective-permute-start.3 = (bf16[2,80,768]{2,1,0:T(8,128)(2,1)S(1)}, bf16[2,80,768]{2,1,0:T(8,128)(2,1)S(1)}, u32[]{:S(2)}, u32[]{:S(2)}) collective-permute-start(bf16[2,80,768]{2,1,0:T(8,128)(2,1)S(1)} %pad_maximum_fusion.refs_0_), channel_id=1, source_target_pairs={{0,24},{8,0},{16,8},{24,16},{1,25},{9,1},{17,9},{25,17},{2,26},{10... | collective-permute-start | bytes 737288 | tf_op jit(solution)/shard_map/ppermute | solution.py:387
  82.0 40.7 %copy-start = (s32[128,6]{0,1:T(8,128)S(1)}, s32[128,6]{0,1:T(8,128)}, u32[]{:S(2)}) copy-start(s32[128,6]{0,1:T(8,128)} %param.11) | copy-start | bytes 9220
  82.1 40.7 %copy-start.1 = (s32[128,6]{0,1:T(8,128)S(1)}, s32[128,6]{0,1:T(8,128)}, u32[]{:S(2)}) copy-start(s32[128,6]{0,1:T(8,128)} %param.12) | copy-start | bytes 9220
  82.1 40.7 %copy-start.2 = (s32[128,3]{0,1:T(4,128)S(1)}, s32[128,3]{0,1:T(4,128)}, u32[]{:S(2)}) copy-start(s32[128,3]{0,1:T(4,128)} %param.10) | copy-start | bytes 4612
  83.6 40.1 %all-to-all-start.2 = ((bf16[32,64,128]{2,1,0:T(8,128)(2,1)}), bf16[32,64,128]{2,1,0:T(8,128)(2,1)S(1)}, u32[]{:S(2)}, u32[]{:S(2)}) async-start(bf16[32,64,128]{2,1,0:T(8,128)(2,1)} %bitcast.23), calls=%async_computation.2 | async-start | bytes 1048576 | tf_op jit(solution)/shard_map/all_to_all | solution.py:350
  93.2 7.1 %collective-permute-start.4 = (f32[1,128]{1,0:T(1,128)S(1)}, f32[1,128]{1,0:T(1,128)S(1)}, u32[]{:S(2)}, u32[]{:S(2)}) collective-permute-start(f32[1,128]{1,0:T(1,128)S(1)} %get-tuple-element.13), channel_id=1, source_target_pairs={{192,0},{224,32},{256,64},{288,96},{320,128},{352,160},{384,192},{... | collective-permute-start | bytes 1544 | tf_op jit(solution)/shard_map/ppermute | solution.py:446
  96.8 7.3 %collective-permute-start.5 = (f32[1,128]{1,0:T(1,128)S(1)}, f32[1,128]{1,0:T(1,128)S(1)}, u32[]{:S(2)}, u32[]{:S(2)}) collective-permute-start(f32[1,128]{1,0:T(1,128)S(1)} %get-tuple-element.13), channel_id=1, source_target_pairs={{320,0},{352,32},{384,64},{416,96},{448,128},{480,160},{0,192},{32... | collective-permute-start | bytes 1544 | tf_op jit(solution)/shard_map/ppermute | solution.py:446
  104.1 5.3 %collective-permute-start.6 = (f32[3,128]{1,0:T(4,128)S(1)}, f32[3,128]{1,0:T(4,128)S(1)}, u32[]{:S(2)}, u32[]{:S(2)}) collective-permute-start(f32[3,128]{1,0:T(4,128)S(1)} %pad_maximum_fusion.1), channel_id=1, source_target_pairs={{64,0},{96,32},{128,64},{160,96},{192,128},{224,160},{256,192},{28... | collective-permute-start | bytes 4616 | tf_op jit(solution)/shard_map/ppermute | solution.py:446
  106.1 5.5 %collective-permute-start.7 = (f32[3,128]{1,0:T(4,128)S(1)}, f32[3,128]{1,0:T(4,128)S(1)}, u32[]{:S(2)}, u32[]{:S(2)}) collective-permute-start(f32[3,128]{1,0:T(4,128)S(1)} %pad_maximum_fusion.1), channel_id=1, source_target_pairs={{448,0},{480,32},{0,64},{32,96},{64,128},{96,160},{128,192},{160,2... | collective-permute-start | bytes 4616 | tf_op jit(solution)/shard_map/ppermute | solution.py:446
  111.7 10.8 %collective-permute-start.8 = (f32[9,128]{1,0:T(8,128)S(1)}, f32[9,128]{1,0:T(8,128)S(1)}, u32[]{:S(2)}, u32[]{:S(2)}) collective-permute-start(f32[9,128]{1,0:T(8,128)S(1)} %concatenate.12), channel_id=1, source_target_pairs={{0,32},{32,0},{64,96},{96,64},{128,160},{160,128},{192,224},{224,1... | collective-permute-start | bytes 13832 | tf_op jit(solution)/shard_map/ppermute | solution.py:449
